TPU v7x, 8 devices: a whole 2x2x1 slice. The times are simulated.
8 devices in a mesh: dp: 1 (over z), tp: 8 (over y, x, core).
Axes of the slice: x: 2, y: 2, z: 1, core: 2. Of those that a mesh axis runs over, the one named last changes fastest.
Arguments:
- x_in: float32 [16, 128, 3072], P('dp', 'tp')
- d_out: bfloat16 [16, 128, 3072], P('dp', 'tp')
- lengths: int32 [16], P('dp')
- w_qkv: bfloat16 [3, 3072, 3, 32, 96], P(None, None, None, 'tp')
- w_out: bfloat16 [3, 32, 96, 3072], P(None, 'tp')
- w_up: bfloat16 [3, 3072, 12288], P(None, None, 'tp')
- b_up: float32 [3, 12288], P(None, 'tp')
- w_down: bfloat16 [3, 12288, 3072], P(None, 'tp')
- vec_par: float32 [3, 6, 3072], replicated
Outputs:
- output 1: float32 [16, 128, 3072], P('dp', 'tp')
- output 2: float32 [16, 128, 3072], P('dp', 'tp')
- output 3: bfloat16 [3, 3072, 3, 32, 96], P('dp', None, None, 'tp')
- output 4: bfloat16 [3, 32, 96, 3072], P('dp', 'tp')
- output 5: bfloat16 [3, 3072, 12288], P('dp', None, 'tp')
- output 6: float32 [3, 12288], P('dp', 'tp')
- output 7: bfloat16 [3, 12288, 3072], P('dp', 'tp')
- output 8: float32 [3, 6, 3072], P('dp')
All inputs are finite; a program needn't handle non-finite values.
Results may differ from a plain program's by a relative error of at most 0.02.
Values are sent between devices in bfloat16 or wider.
A program may use at most 1 GiB of HBM per device.

v0:
```python
import jax
import jax.numpy as jnp
from jax import lax
from jax.sharding import PartitionSpec as P

TENSOR_AXIS = 'tp'
PARTS_AXIS = 'dp'


def layer_norm(x_val, gain_vec, shift_vec):
    row_mean = jnp.mean(x_val, axis=-1, keepdims=True)
    centered = x_val - row_mean
    row_var = jnp.mean(centered * centered, axis=-1, keepdims=True)
    return centered * lax.rsqrt(row_var + 1e-5) * gain_vec + shift_vec


def gelu_tanh(pre_act):
    return jax.nn.gelu(pre_act, approximate=True)


def visible_mask(lengths, seq_len):
    positions = jnp.arange(seq_len)
    causal = positions[None, :] <= positions[:, None]
    return causal[None, None] & (positions[None, None, None, :] < lengths[:, None, None, None])


def attention_fwd(q_all, k_all, v_all, lengths):
    score_scale = q_all.shape[3] ** -0.5
    scores = jnp.einsum('bhqe,bhke->bhqk', q_all, k_all, preferred_element_type=jnp.float32) * score_scale
    attn_prob = jax.nn.softmax(jnp.where(visible_mask(lengths, q_all.shape[2]), scores, -1e30), axis=-1)
    context = jnp.einsum('bhqk,bhke->bhqe', attn_prob.astype(jnp.bfloat16), v_all, preferred_element_type=jnp.float32)
    return context.astype(jnp.bfloat16), attn_prob


def attention_bwd(d_ctx, q_all, k_all, v_all, attn_prob):
    score_scale = q_all.shape[3] ** -0.5
    d_prob = jnp.einsum('bhqe,bhke->bhqk', d_ctx, v_all, preferred_element_type=jnp.float32).astype(jnp.bfloat16).astype(jnp.float32)
    d_v = jnp.einsum('bhqk,bhqe->bhke', attn_prob.astype(jnp.bfloat16), d_ctx, preferred_element_type=jnp.float32).astype(jnp.bfloat16)
    d_score = attn_prob * (d_prob - jnp.sum(d_prob * attn_prob, axis=-1, keepdims=True))
    d_score = (d_score * score_scale).astype(jnp.bfloat16)
    d_q = jnp.einsum('bhqk,bhke->bhqe', d_score, k_all, preferred_element_type=jnp.float32).astype(jnp.bfloat16)
    d_k = jnp.einsum('bhqk,bhqe->bhke', d_score, q_all, preferred_element_type=jnp.float32).astype(jnp.bfloat16)
    return jnp.stack([d_q, d_k, d_v])


def layer_fwd(x_cur, lengths, weights, vec_layer):
    w_qkv, w_out, w_up, b_up, w_down = weights
    a_shard = layer_norm(x_cur, vec_layer[0], vec_layer[1]).astype(jnp.bfloat16)
    a_full = lax.all_gather(a_shard, TENSOR_AXIS, axis=1, tiled=True)
    qkv_all = jnp.einsum('bsd,dthe->tbhse', a_full, w_qkv, preferred_element_type=jnp.float32).astype(jnp.bfloat16)
    context, attn_prob = attention_fwd(qkv_all[0], qkv_all[1], qkv_all[2], lengths)
    attn_part = jnp.einsum('bhse,hed->bsd', context, w_out, preferred_element_type=jnp.float32).astype(jnp.bfloat16)
    attn_shard = lax.psum_scatter(attn_part, TENSOR_AXIS, scatter_dimension=1, tiled=True)
    hidden = x_cur + attn_shard.astype(jnp.float32) + vec_layer[4]
    m_shard = layer_norm(hidden, vec_layer[2], vec_layer[3]).astype(jnp.bfloat16)
    m_full = lax.all_gather(m_shard, TENSOR_AXIS, axis=1, tiled=True)
    pre_act = jnp.einsum('bsd,df->bsf', m_full, w_up, preferred_element_type=jnp.float32) + b_up
    act_bf = gelu_tanh(pre_act).astype(jnp.bfloat16)
    mlp_part = jnp.einsum('bsf,fd->bsd', act_bf, w_down, preferred_element_type=jnp.float32).astype(jnp.bfloat16)
    mlp_shard = lax.psum_scatter(mlp_part, TENSOR_AXIS, scatter_dimension=1, tiled=True)
    x_next = hidden + mlp_shard.astype(jnp.float32) + vec_layer[5]
    return x_next, (x_cur, a_full, qkv_all, context, attn_prob, hidden, m_full, pre_act, act_bf)


def layer_bwd(d_cur, residues, weights, vec_layer):
    w_qkv, w_out, w_up, w_down = weights[0], weights[1], weights[2], weights[4]
    x_prev, a_full, qkv_all, context, attn_prob, hidden, m_full, pre_act, act_bf = residues
    d_mlp = lax.all_gather(d_cur.astype(jnp.bfloat16), TENSOR_AXIS, axis=1, tiled=True)
    d_act = jnp.einsum('bsd,fd->bsf', d_mlp, w_down, preferred_element_type=jnp.float32).astype(jnp.bfloat16)
    g_down = jnp.einsum('bsf,bsd->fd', act_bf, d_mlp, preferred_element_type=jnp.float32).astype(jnp.bfloat16)
    d_pre = jax.vjp(gelu_tanh, pre_act)[1](d_act.astype(jnp.float32))[0]
    d_pre_bf = d_pre.astype(jnp.bfloat16)
    g_up = jnp.einsum('bsd,bsf->df', m_full, d_pre_bf, preferred_element_type=jnp.float32).astype(jnp.bfloat16)
    g_bup = jnp.sum(d_pre, axis=(0, 1))
    d_mid_part = jnp.einsum('bsf,df->bsd', d_pre_bf, w_up, preferred_element_type=jnp.float32).astype(jnp.bfloat16)
    d_mid = lax.psum_scatter(d_mid_part, TENSOR_AXIS, scatter_dimension=1, tiled=True)
    d_hid_ln, d_gain2, d_shift2 = jax.vjp(layer_norm, hidden, vec_layer[2], vec_layer[3])[1](d_mid.astype(jnp.float32))
    d_hid = d_cur + d_hid_ln
    d_attn = lax.all_gather(d_hid.astype(jnp.bfloat16), TENSOR_AXIS, axis=1, tiled=True)
    d_ctx = jnp.einsum('bsd,hed->bhse', d_attn, w_out, preferred_element_type=jnp.float32).astype(jnp.bfloat16)
    g_out = jnp.einsum('bhse,bsd->hed', context, d_attn, preferred_element_type=jnp.float32).astype(jnp.bfloat16)
    d_qkv = attention_bwd(d_ctx, qkv_all[0], qkv_all[1], qkv_all[2], attn_prob)
    g_qkv = jnp.einsum('bsd,tbhse->dthe', a_full, d_qkv, preferred_element_type=jnp.float32).astype(jnp.bfloat16)
    d_in_part = jnp.einsum('tbhse,dthe->bsd', d_qkv, w_qkv, preferred_element_type=jnp.float32).astype(jnp.bfloat16)
    d_in = lax.psum_scatter(d_in_part, TENSOR_AXIS, scatter_dimension=1, tiled=True)
    d_x_ln, d_gain1, d_shift1 = jax.vjp(layer_norm, x_prev, vec_layer[0], vec_layer[1])[1](d_in.astype(jnp.float32))
    g_vec = jnp.stack([d_gain1, d_shift1, d_gain2, d_shift2, jnp.sum(d_hid, axis=(0, 1)), jnp.sum(d_cur, axis=(0, 1))])
    return d_hid + d_x_ln, (g_qkv, g_out, g_up, g_bup, g_down, g_vec)


def group_body(x_loc, dy_loc, len_loc, wqkv_loc, wout_loc, wup_loc, bup_loc, wdown_loc, vec_loc):
    n_layers = wqkv_loc.shape[0]
    saved_acts = []
    x_cur = x_loc
    for layer_idx in range(n_layers):
        weights = (wqkv_loc[layer_idx], wout_loc[layer_idx], wup_loc[layer_idx], bup_loc[layer_idx], wdown_loc[layer_idx])
        x_cur, residues = layer_fwd(x_cur, len_loc, weights, vec_loc[layer_idx])
        saved_acts.append(residues)
    d_cur = dy_loc.astype(jnp.float32)
    layer_grads = [None] * n_layers
    for layer_idx in reversed(range(n_layers)):
        weights = (wqkv_loc[layer_idx], wout_loc[layer_idx], wup_loc[layer_idx], bup_loc[layer_idx], wdown_loc[layer_idx])
        d_cur, grad_set = layer_bwd(d_cur, saved_acts[layer_idx], weights, vec_loc[layer_idx])
        layer_grads[layer_idx] = grad_set
    stacked = [jnp.stack([grad_set[grad_pos] for grad_set in layer_grads]) for grad_pos in range(6)]
    g_vec = lax.psum(stacked[5], TENSOR_AXIS)
    return x_cur, d_cur, stacked[0], stacked[1], stacked[2], stacked[3], stacked[4], g_vec


def solution(mesh):
    act_spec = P(PARTS_AXIS, TENSOR_AXIS, None)
    in_specs = (act_spec, act_spec, P(PARTS_AXIS), P(None, None, None, TENSOR_AXIS, None), P(None, TENSOR_AXIS, None, None), P(None, None, TENSOR_AXIS), P(None, TENSOR_AXIS), P(None, TENSOR_AXIS, None), P())
    out_specs = (act_spec, act_spec, P(PARTS_AXIS, None, None, TENSOR_AXIS, None), P(PARTS_AXIS, TENSOR_AXIS, None, None), P(PARTS_AXIS, None, TENSOR_AXIS), P(PARTS_AXIS, TENSOR_AXIS), P(PARTS_AXIS, TENSOR_AXIS, None), P(PARTS_AXIS, None, None))
    return jax.shard_map(group_body, mesh=mesh, in_specs=in_specs, out_specs=out_specs, check_vma=False)
```

profile of v0, /device:TPU:0, one launch (start us, length us, event | category | flops | bytes accessed | tf_op | source)
XLA Modules:
  0.0 2565.7 jit_solution(6425748341160567468)
XLA Ops:
  14.8 68.8 %all-gather.13.cloned.1.call-done = bf16[16,128,3072]{2,1,0:T(8,128)(2,1)} async-done(((bf16[16,16,3072]{2,1,0:T(8,128)(2,1)}), bf16[16,128,3072]{2,1,0:T(8,128)(2,1)}) %all-gather.13.cloned.1.call-update) | async-done | bytes 12582928 | tf_op jit(solution)/shard_map/all_gather | solution.py:49
  120.7 82.6 %reduce-scatter.13.cloned.1.call-done = bf16[16,16,3072]{2,1,0:T(8,128)(2,1)} async-done(((bf16[16,128,3072]{2,1,0:T(8,128)(2,1)}), bf16[16,16,3072]{2,1,0:T(8,128)(2,1)}) %reduce-scatter.13.cloned.1.call-update) | async-done | bytes 1572880 | tf_op jit(solution)/shard_map/reduce_scatter | solution.py:53
  210.0 65.5 %all-gather.15.cloned.1.call-done = bf16[16,128,3072]{2,1,0:T(8,128)(2,1)} async-done(((bf16[16,16,3072]{2,1,0:T(8,128)(2,1)}), bf16[16,128,3072]{2,1,0:T(8,128)(2,1)}) %all-gather.15.cloned.1.call-update) | async-done | bytes 12582928 | tf_op jit(solution)/shard_map/all_gather | solution.py:56
  335.7 82.2 %reduce-scatter.15.cloned.1.call-done = bf16[16,16,3072]{2,1,0:T(8,128)(2,1)} async-done(((bf16[16,128,3072]{2,1,0:T(8,128)(2,1)}), bf16[16,16,3072]{2,1,0:T(8,128)(2,1)}) %reduce-scatter.15.cloned.1.call-update) | async-done | bytes 1572880 | tf_op jit(solution)/shard_map/reduce_scatter | solution.py:60
  423.7 66.4 %all-gather.17.cloned.1.call-done = bf16[16,128,3072]{2,1,0:T(8,128)(2,1)} async-done(((bf16[16,16,3072]{2,1,0:T(8,128)(2,1)}), bf16[16,128,3072]{2,1,0:T(8,128)(2,1)}) %all-gather.17.cloned.1.call-update) | async-done | bytes 12582928 | tf_op jit(solution)/shard_map/all_gather | solution.py:49
  527.2 82.6 %reduce-scatter.17.cloned.1.call-done = bf16[16,16,3072]{2,1,0:T(8,128)(2,1)} async-done(((bf16[16,128,3072]{2,1,0:T(8,128)(2,1)}), bf16[16,16,3072]{2,1,0:T(8,128)(2,1)}) %reduce-scatter.17.cloned.1.call-update) | async-done | bytes 1572880 | tf_op jit(solution)/shard_map/reduce_scatter | solution.py:53
  615.8 66.2 %all-gather.19.cloned.1.call-done = bf16[16,128,3072]{2,1,0:T(8,128)(2,1)} async-done(((bf16[16,16,3072]{2,1,0:T(8,128)(2,1)}), bf16[16,128,3072]{2,1,0:T(8,128)(2,1)}) %all-gather.19.cloned.1.call-update) | async-done | bytes 12582928 | tf_op jit(solution)/shard_map/all_gather | solution.py:56
  742.2 82.2 %reduce-scatter.19.cloned.1.call-done = bf16[16,16,3072]{2,1,0:T(8,128)(2,1)} async-done(((bf16[16,128,3072]{2,1,0:T(8,128)(2,1)}), bf16[16,16,3072]{2,1,0:T(8,128)(2,1)}) %reduce-scatter.19.cloned.1.call-update) | async-done | bytes 1572880 | tf_op jit(solution)/shard_map/reduce_scatter | solution.py:60
  830.2 66.4 %all-gather.21.cloned.1.call-done = bf16[16,128,3072]{2,1,0:T(8,128)(2,1)} async-done(((bf16[16,16,3072]{2,1,0:T(8,128)(2,1)}), bf16[16,128,3072]{2,1,0:T(8,128)(2,1)}) %all-gather.21.cloned.1.call-update) | async-done | bytes 12582928 | tf_op jit(solution)/shard_map/all_gather | solution.py:49
  933.8 82.6 %reduce-scatter.21.cloned.1.call-done = bf16[16,16,3072]{2,1,0:T(8,128)(2,1)} async-done(((bf16[16,128,3072]{2,1,0:T(8,128)(2,1)}), bf16[16,16,3072]{2,1,0:T(8,128)(2,1)}) %reduce-scatter.21.cloned.1.call-update) | async-done | bytes 1572880 | tf_op jit(solution)/shard_map/reduce_scatter | solution.py:53
  1023.0 65.6 %all-gather.23.cloned.1.call-done = bf16[16,128,3072]{2,1,0:T(8,128)(2,1)} async-done(((bf16[16,16,3072]{2,1,0:T(8,128)(2,1)}), bf16[16,128,3072]{2,1,0:T(8,128)(2,1)}) %all-gather.23.cloned.1.call-update) | async-done | bytes 12582928 | tf_op jit(solution)/shard_map/all_gather | solution.py:56
  1115.1 41.5 %all-gather.25.cloned.1.call-done = bf16[16,128,3072]{2,1,0:T(8,128)(2,1)} async-done(((bf16[16,16,3072]{2,1,0:T(8,128)(2,1)}), bf16[16,128,3072]{2,1,0:T(8,128)(2,1)}) %all-gather.25.cloned.1.call-update) | async-done | bytes 12582928 | tf_op jit(solution)/shard_map/all_gather | solution.py:68
  1251.2 48.9 %reduce-scatter.25.cloned.1.call-done = bf16[16,16,3072]{2,1,0:T(8,128)(2,1)} async-done(((bf16[16,128,3072]{2,1,0:T(8,128)(2,1)}), bf16[16,16,3072]{2,1,0:T(8,128)(2,1)}) %reduce-scatter.25.cloned.1.call-update) | async-done | bytes 1572880 | tf_op jit(solution)/shard_map/reduce_scatter | solution.py:76
  1305.3 80.6 %reduce-scatter.23.cloned.1.call-done = bf16[16,16,3072]{2,1,0:T(8,128)(2,1)} async-done(((bf16[16,128,3072]{2,1,0:T(8,128)(2,1)}), bf16[16,16,3072]{2,1,0:T(8,128)(2,1)}) %reduce-scatter.23.cloned.1.call-update) | async-done | bytes 1572880 | tf_op jit(solution)/shard_map/reduce_scatter | solution.py:60
  1394.4 66.4 %all-gather.27.cloned.1.call-done = bf16[16,128,3072]{2,1,0:T(8,128)(2,1)} async-done(((bf16[16,16,3072]{2,1,0:T(8,128)(2,1)}), bf16[16,128,3072]{2,1,0:T(8,128)(2,1)}) %all-gather.27.cloned.1.call-update) | async-done | bytes 12582928 | tf_op jit(solution)/shard_map/all_gather | solution.py:79
  1511.3 82.6 %reduce-scatter.27.cloned.1.call-done = bf16[16,16,3072]{2,1,0:T(8,128)(2,1)} async-done(((bf16[16,128,3072]{2,1,0:T(8,128)(2,1)}), bf16[16,16,3072]{2,1,0:T(8,128)(2,1)}) %reduce-scatter.27.cloned.1.call-update) | async-done | bytes 1572880 | tf_op jit(solution)/shard_map/reduce_scatter | solution.py:85
  1604.4 66.4 %all-gather.29.cloned.1.call-done = bf16[16,128,3072]{2,1,0:T(8,128)(2,1)} async-done(((bf16[16,16,3072]{2,1,0:T(8,128)(2,1)}), bf16[16,128,3072]{2,1,0:T(8,128)(2,1)}) %all-gather.29.cloned.1.call-update) | async-done | bytes 12582928 | tf_op jit(solution)/shard_map/all_gather | solution.py:68
  1670.8 35.0 %fusion.351 = (f32[1536]{0:T(1024)}, bf16[16,128,1536]{2,1,0:T(8,128)(2,1)}) fusion(f32[16,128,1536]{2,1,0:T(8,128)} %fusion.77, f32[1536]{0:T(1024)S(1)} %copy-done.122, bf16[16,128,3072]{2,1,0:T(8,128)(2,1)} %all-gather.29.cloned.1.call-done, bf16[3,1536,3072]{2,1,0:T(8,128)(2,1)} %param.16), kind=kOutput, calls=%fused_computation.442 | convolution fusion | flops 19402848256 | bytes 40906752 | tf_op jit(solution)/shard_map/bsd,fd->bsf/dot_general | solution.py:69
  1732.4 82.2 %reduce-scatter.29.cloned.1.call-done = bf16[16,16,3072]{2,1,0:T(8,128)(2,1)} async-done(((bf16[16,128,3072]{2,1,0:T(8,128)(2,1)}), bf16[16,16,3072]{2,1,0:T(8,128)(2,1)}) %reduce-scatter.29.cloned.1.call-update) | async-done | bytes 1572880 | tf_op jit(solution)/shard_map/reduce_scatter | solution.py:76
  1825.1 66.4 %all-gather.31.cloned.1.call-done = bf16[16,128,3072]{2,1,0:T(8,128)(2,1)} async-done(((bf16[16,16,3072]{2,1,0:T(8,128)(2,1)}), bf16[16,128,3072]{2,1,0:T(8,128)(2,1)}) %all-gather.31.cloned.1.call-update) | async-done | bytes 12582928 | tf_op jit(solution)/shard_map/all_gather | solution.py:79
  1941.5 82.6 %reduce-scatter.31.cloned.1.call-done = bf16[16,16,3072]{2,1,0:T(8,128)(2,1)} async-done(((bf16[16,128,3072]{2,1,0:T(8,128)(2,1)}), bf16[16,16,3072]{2,1,0:T(8,128)(2,1)}) %reduce-scatter.31.cloned.1.call-update) | async-done | bytes 1572880 | tf_op jit(solution)/shard_map/reduce_scatter | solution.py:85
  2100.9 35.2 %fusion.352 = (f32[1536]{0:T(1024)}, bf16[16,128,1536]{2,1,0:T(8,128)(2,1)}) fusion(f32[16,128,1536]{2,1,0:T(8,128)} %fusion.85, f32[1536]{0:T(1024)S(1)} %copy-done.119, bf16[16,128,3072]{2,1,0:T(8,128)(2,1)} %all-gather.33.cloned.1.call-done, bf16[3,1536,3072]{2,1,0:T(8,128)(2,1)} %param.16), kind=kOutput, calls=%fused_computation.443 | convolution fusion | flops 19402848256 | bytes 40906752 | tf_op jit(solution)/shard_map/bsd,fd->bsf/dot_general | solution.py:69
  2467.5 41.1 %reduce-scatter.35.cloned.1.call-done = bf16[16,16,3072]{2,1,0:T(8,128)(2,1)} async-done(((bf16[16,128,3072]{2,1,0:T(8,128)(2,1)}), bf16[16,16,3072]{2,1,0:T(8,128)(2,1)}) %reduce-scatter.35.cloned.1.call-update) | async-done | bytes 1572880 | tf_op jit(solution)/shard_map/reduce_scatter | solution.py:85
  2519.4 37.6 %all-reduce.2.cloned.1.call-done = f32[3,6,3072]{2,1,0:T(8,128)} async-done(((f32[3,6,3072]{2,1,0:T(8,128)}), f32[3,6,3072]{2,1,0:T(8,128)}) %all-reduce.2.cloned.1.call-update) | async-done | bytes 221200 | tf_op jit(solution)/shard_map/psum | solution.py:106
  (505 shorter events, 972.5 us)
Async XLA Ops:
  14.3 189.0 %reduce-scatter.13.cloned.1.call-start = ((), (), s32[]{:S(2)}) async-start(), calls=%async_computation.13 | async-start | bytes 14155776 | tf_op jit(solution)/shard_map/reduce_scatter | solution.py:53
  120.6 154.8 %all-gather.15.cloned.1.call-start = ((), (), s32[]{:S(2)}) async-start(), calls=%async_computation.14 | async-start | bytes 14155776 | tf_op jit(solution)/shard_map/all_gather | solution.py:56
  209.0 208.8 %reduce-scatter.15.cloned.1.call-start = ((), (), s32[]{:S(2)}) async-start(), calls=%async_computation.15 | async-start | bytes 14155776 | tf_op jit(solution)/shard_map/reduce_scatter | solution.py:60
  335.2 154.8 %all-gather.17.cloned.1.call-start = ((), (), s32[]{:S(2)}) async-start(), calls=%async_computation.16 | async-start | bytes 14155776 | tf_op jit(solution)/shard_map/all_gather | solution.py:49
  423.6 186.1 %reduce-scatter.17.cloned.1.call-start = ((), (), s32[]{:S(2)}) async-start(), calls=%async_computation.17 | async-start | bytes 14155776 | tf_op jit(solution)/shard_map/reduce_scatter | solution.py:53
  527.1 154.9 %all-gather.19.cloned.1.call-start = ((), (), s32[]{:S(2)}) async-start(), calls=%async_computation.18 | async-start | bytes 14155776 | tf_op jit(solution)/shard_map/all_gather | solution.py:56
  615.6 208.8 %reduce-scatter.19.cloned.1.call-start = ((), (), s32[]{:S(2)}) async-start(), calls=%async_computation.19 | async-start | bytes 14155776 | tf_op jit(solution)/shard_map/reduce_scatter | solution.py:60
  741.8 154.8 %all-gather.21.cloned.1.call-start = ((), (), s32[]{:S(2)}) async-start(), calls=%async_computation.20 | async-start | bytes 14155776 | tf_op jit(solution)/shard_map/all_gather | solution.py:49
  830.2 186.2 %reduce-scatter.21.cloned.1.call-start = ((), (), s32[]{:S(2)}) async-start(), calls=%async_computation.21 | async-start | bytes 14155776 | tf_op jit(solution)/shard_map/reduce_scatter | solution.py:53
  933.7 154.9 %all-gather.23.cloned.1.call-start = ((), (), s32[]{:S(2)}) async-start(), calls=%async_computation.22 | async-start | bytes 14155776 | tf_op jit(solution)/shard_map/all_gather | solution.py:56
  1022.2 134.4 %all-gather.25.cloned.1.call-start = ((), (), s32[]{:S(2)}) async-start(), calls=%async_computation.24 | async-start | bytes 14155776 | tf_op jit(solution)/shard_map/all_gather | solution.py:68
  1022.8 277.4 %reduce-scatter.25.cloned.1.call-start = ((), (), s32[]{:S(2)}) async-start(), calls=%async_computation.25 | async-start | bytes 14155776 | tf_op jit(solution)/shard_map/reduce_scatter | solution.py:76
  1217.5 168.4 %reduce-scatter.23.cloned.1.call-start = ((), (), s32[]{:S(2)}) async-start(), calls=%async_computation.23 | async-start | bytes 14155776 | tf_op jit(solution)/shard_map/reduce_scatter | solution.py:60
  1251.2 209.6 %all-gather.27.cloned.1.call-start = ((), (), s32[]{:S(2)}) async-start(), calls=%async_computation.26 | async-start | bytes 14155776 | tf_op jit(solution)/shard_map/all_gather | solution.py:79
  1394.4 199.5 %reduce-scatter.27.cloned.1.call-start = ((), (), s32[]{:S(2)}) async-start(), calls=%async_computation.27 | async-start | bytes 14155776 | tf_op jit(solution)/shard_map/reduce_scatter | solution.py:85
  1511.2 159.5 %all-gather.29.cloned.1.call-start = ((), (), s32[]{:S(2)}) async-start(), calls=%async_computation.28 | async-start | bytes 14155776 | tf_op jit(solution)/shard_map/all_gather | solution.py:68
  1604.3 210.2 %reduce-scatter.29.cloned.1.call-start = ((), (), s32[]{:S(2)}) async-start(), calls=%async_computation.29 | async-start | bytes 14155776 | tf_op jit(solution)/shard_map/reduce_scatter | solution.py:76
  1731.9 159.5 %all-gather.31.cloned.1.call-start = ((), (), s32[]{:S(2)}) async-start(), calls=%async_computation.30 | async-start | bytes 14155776 | tf_op jit(solution)/shard_map/all_gather | solution.py:79
  1825.0 199.0 %reduce-scatter.31.cloned.1.call-start = ((), (), s32[]{:S(2)}) async-start(), calls=%async_computation.31 | async-start | bytes 14155776 | tf_op jit(solution)/shard_map/reduce_scatter | solution.py:85
  1941.5 159.4 %all-gather.33.cloned.1.call-start = ((), (), s32[]{:S(2)}) async-start(), calls=%async_computation.32 | async-start | bytes 14155776 | tf_op jit(solution)/shard_map/all_gather | solution.py:68
  2034.5 210.4 %reduce-scatter.33.cloned.1.call-start = ((), (), s32[]{:S(2)}) async-start(), calls=%async_computation.33 | async-start | bytes 14155776 | tf_op jit(solution)/shard_map/reduce_scatter | solution.py:76
  2162.1 213.8 %all-gather.35.cloned.1.call-start = ((), (), s32[]{:S(2)}) async-start(), calls=%async_computation.34 | async-start | bytes 14155776 | tf_op jit(solution)/shard_map/all_gather | solution.py:79
  2255.2 253.4 %reduce-scatter.35.cloned.1.call-start = ((), (), s32[]{:S(2)}) async-start(), calls=%async_computation.35 | async-start | bytes 14155776 | tf_op jit(solution)/shard_map/reduce_scatter | solution.py:85
  2425.9 131.1 %all-reduce.2.cloned.1.call-start = ((), (), s32[]{:S(2)}) async-start(), calls=%async_computation.36 | async-start | bytes 589824 | tf_op jit(solution)/shard_map/psum | solution.py:106
  (158 other events, 4642.3 us)
Sparse Core Ops, SparseCore 0:
  14.4 69.1 all-gather.12
  120.8 82.4 reduce-scatter.12
  209.2 66.2 all-gather.14
  335.4 82.4 reduce-scatter.14
  423.8 66.2 all-gather.16
  527.3 82.4 reduce-scatter.16
  615.7 66.2 all-gather.18
  741.9 82.4 reduce-scatter.18
  830.3 66.2 all-gather.20
  933.9 82.4 reduce-scatter.20
  1022.3 66.2 all-gather.22
  1090.3 66.2 all-gather.24
  1217.7 82.4 reduce-scatter.24
  1303.4 82.4 reduce-scatter.22
  1394.5 66.2 all-gather.26
  1511.3 82.4 reduce-scatter.26
  1604.5 66.2 all-gather.28
  1732.0 82.4 reduce-scatter.28
  1825.2 66.2 all-gather.30
  1941.6 82.4 reduce-scatter.30
  2034.6 66.2 all-gather.32
  2162.2 82.4 reduce-scatter.32
  2255.3 66.2 all-gather.34
  2426.0 82.4 reduce-scatter.34
  (1 shorter events, 42.7 us)
where the time goes:
time: 2570 us
  waiting for transfers between devices  1520 us (59%)
  matrix products  848 us (33%)
  other arithmetic  140 us (5%)
  local copies, waits for them, and re-layouts  41.2 us (2%)
    reduce_scatter x3, waiting for transfers between devices, layer_fwd(): lax.psum_scatter(attn_part, TENSOR_AXIS, scatter_dimension=1, tiled=True)  248 us
    reduce_scatter x3, waiting for transfers between devices, layer_fwd(): lax.psum_scatter(mlp_part, TENSOR_AXIS, scatter_dimension=1, tiled=True)  245 us
    reduce_scatter x3, waiting for transfers between devices, layer_bwd(): lax.psum_scatter(d_in_part, TENSOR_AXIS, scatter_dimension=1, tiled=True)  206 us
    all_gather x3, waiting for transfers between devices, layer_fwd(): a_full = lax.all_gather(a_shard, TENSOR_AXIS, axis=1, tiled=True)  202 us
    all_gather x3, waiting for transfers between devices, layer_fwd(): m_full = lax.all_gather(m_shard, TENSOR_AXIS, axis=1, tiled=True)  197 us
    all_gather x3, waiting for transfers between devices, layer_bwd(): lax.all_gather(d_hid.astype(jnp.bfloat16), TENSOR_AXIS, axis=1, tiled=True)  133 us
    reduce_scatter x3, waiting for transfers between devices, layer_bwd(): lax.psum_scatter(d_mid_part, TENSOR_AXIS, scatter_dimension=1, tiled=True)  131 us
    all_gather x3, waiting for transfers between devices, layer_bwd(): lax.all_gather(d_cur.astype(jnp.bfloat16), TENSOR_AXIS, axis=1, tiled=True)  118 us
  transfers between devices with their start and end apart: 25, of which 23 were waited for; matrix products, arithmetic and copies ran while one was open for 14% of the time, Pallas kernels for 0%

commit v1 on v0

v1 whole, which is shorter than its diff:
```python
from types import SimpleNamespace

import jax
import jax.numpy as jnp
from jax import lax
from jax.experimental import pallas as pl
from jax.experimental.pallas import tpu as pltpu
from jax.sharding import PartitionSpec as P

TP, DP = "tp", "dp"
D = 3072
ROWS = 128
TOK = 2 * 8 * ROWS
HEADS, HD = 4, 96
SEQS = 4
BM, BN = 384, 512
BF, F32 = jnp.bfloat16, jnp.float32
ANY = pl.ANY
VMEM_LIMIT = 66_900_000
GELU_C = 0.7978845608028654
Q_ORDER = (3, 1, 2, 0)
FIRST, MID, TOP, LAST = range(4)
N_FIRST, N_LN, N_RES, N_BWD2, N_BWD1 = range(5)
QKV, UP, DACT, DCTX = range(4)
WIDTH = (1152, 1536, 1536, 384)


def dims(lhs, rhs, lc, rc):
    return lax.dot_general(lhs, rhs, (((lc,), (rc,)), ((), ())), preferred_element_type=F32)


def peers():
    me = lax.axis_index(TP)
    dp = lax.axis_index(DP)
    core = me + 1 - 2 * lax.rem(me, 2)
    x = me + 2 - 4 * lax.rem(lax.div(me, 2), 2)
    y = me + 4 - 8 * lax.div(me, 4)
    return (dp, core), (dp, x), (dp, y)


def say_here(devices):
    for dev in devices:
        pl.semaphore_signal(pltpu.get_barrier_semaphore(), inc=1, device_id=dev, device_id_type=pl.DeviceIdType.MESH)


def await_peers(n=3):
    pl.semaphore_wait(pltpu.get_barrier_semaphore(), n)


def remote(src, dst, send, recv, dev):
    return pltpu.make_async_remote_copy(src_ref=src, dst_ref=dst, send_sem=send, recv_sem=recv, device_id=dev, device_id_type=pl.DeviceIdType.MESH)


class Pieces:
    def __init__(self, src, dst, sem, n):
        self.src, self.dst, self.sem, self.n = src, dst, sem, n

    def start(self):
        src, dst = self.src, self.dst
        step = src.shape[-2] // self.n
        for i in range(self.n):
            at = pl.ds(i * step, step)
            if len(src.shape) == 3:
                for j in range(src.shape[0]):
                    pltpu.make_async_copy(src.at[j, at], dst.at[j, at], self.sem).start()
            else:
                pltpu.make_async_copy(src.at[at], dst.at[at], self.sem).start()
        return self

    def wait(self):
        pltpu.make_async_copy(self.src, self.dst, self.sem).wait()


def call(name, cid, body, ins, outs, scratch, small):
    names = [list(vars(a)) for a in (ins, outs, scratch)]

    def kernel(*refs):
        body(SimpleNamespace(**dict(zip(sum(names, []), refs))))

    def spec(n):
        return pl.BlockSpec(memory_space=pltpu.VMEM if n in small else ANY)

    res = pl.pallas_call(
        kernel,
        name=name,
        out_shape=list(vars(outs).values()),
        in_specs=[spec(n) for n in names[0]],
        out_specs=[spec(n) for n in names[1]],
        scratch_shapes=list(vars(scratch).values()),
        compiler_params=pltpu.CompilerParams(vmem_limit_bytes=VMEM_LIMIT, collective_id=cid, has_side_effects=True),
    )(*vars(ins).values())
    return SimpleNamespace(**dict(zip(names[1], res)))


def fused(name, cid, kind, norm, arrays, vec, rs=None, ag=None, fills=(), bm=384, plan=()):
    ins, outs, sc = SimpleNamespace(**arrays), SimpleNamespace(), SimpleNamespace()
    dma = pltpu.SemaphoreType.DMA
    n_in = 2 if norm in (N_BWD2, N_BWD1) else 1
    n_acc = {N_BWD2: 4, N_BWD1: 2}.get(norm, 0)
    if norm != N_FIRST:
        outs.out0 = jax.ShapeDtypeStruct((2, ROWS, D), F32)
        sc.nout = pltpu.VMEM((ROWS, D), F32)
    if norm == N_RES:
        outs.out1 = jax.ShapeDtypeStruct((2, ROWS, D), F32)
        sc.nout1 = pltpu.VMEM((ROWS, D), F32)
    sc.nin = pltpu.VMEM((n_in, ROWS, D), F32)
    sc.nsem = dma((4,))
    if n_acc:
        outs.vo = jax.ShapeDtypeStruct((8, D), F32)
        sc.acc = pltpu.VMEM((n_acc, 8, D), F32)
    if rs:
        k1 = rs[1]
        tile1 = D if k1 <= 384 else 1024
        tiles1 = D // tile1
        sc.w1 = pltpu.VMEM((D, k1) if rs[2] else (k1, D), BF)
        sc.lhs = pltpu.VMEM((2, 2, ROWS, k1), BF)
        sc.own = pltpu.VMEM((2, 4, ROWS, D), BF)
        sc.snd = pltpu.VMEM((4, ROWS, D), BF)
        sc.drx = pltpu.VMEM((2, 4, ROWS, D), BF)
        sc.hx = pltpu.VMEM((2, 64, D), BF)
        sc.hy = pltpu.VMEM((2, 64, D), BF)
        sc.rx = pltpu.VMEM((2, ROWS, D), BF)
        sc.ry = pltpu.VMEM((2, ROWS, D), BF)
        sc.w1_sem = dma((tiles1,))
        sc.lhs_sem = dma((2,))
        sc.rs_send = dma((2, 10))
        sc.rs_recv = dma((2, 10))
    if ag:
        what = ag[0]
        n2 = WIDTH[what]
        outs.full = jax.ShapeDtypeStruct((2, 8, ROWS, D), BF)
        outs.res = jax.ShapeDtypeStruct((2, 8, ROWS, n2), BF)
        sc.w2 = pltpu.VMEM((D, n2) if what == UP else (n2, D), BF)
        sc.g = pltpu.VMEM((2, ROWS, D), BF)
        sc.agin = pltpu.VMEM((2, 2, ROWS, D), BF)
        sc.w2_sem = dma
        sc.g_sem = dma((2,))
        sc.agin_sem = dma((2,))
        sc.ag_send = dma((2, 10))
        sc.ag_recv = dma((2, 10))
        sc.res_st = pltpu.VMEM((2, 2, ROWS, n2), BF)
        sc.res_sem = dma((2,))
        if what == UP:
            outs.pre = jax.ShapeDtypeStruct((2, 8, ROWS, n2), F32)
        if what == DACT:
            outs.bup = jax.ShapeDtypeStruct((1, n2), F32)
            sc.bacc = pltpu.VMEM((8, n2), F32)
        if what in (UP, DACT):
            sc.pre_st = pltpu.VMEM((2, 2, ROWS, n2), F32)
            sc.pre_sem = dma((2,))
    if fills:
        sc.f_lhs = pltpu.VMEM((TOK, bm), BF)
        sc.f_at = pltpu.VMEM((bm, TOK), BF)
        sc.f_rhs = pltpu.VMEM((2, TOK, BN), BF)
        sc.f_out = pltpu.VMEM((2, bm, BN), BF)
        sc.f_sem = dma((5,))
        outs.g0 = jax.ShapeDtypeStruct(fills[0], BF)
        outs.g1 = jax.ShapeDtypeStruct(fills[1], BF)

    def body(r):
        core, px, py = peers()

        def begin(src, dst, sem, n=4):
            return Pieces(src, dst, sem, n).start()

        def norm_load(h):
            return [begin(x.at[h], r.nin.at[i], r.nsem.at[i]) for i, x in enumerate((r.in0, r.in1) if n_in == 2 else (r.in0,))]

        def vrow(row):
            return r.vec[row[0], row[1] : row[1] + 1, :]

        out_copy = []

        def norm_half(h, loads):
            for c in loads:
                c.wait()
            while out_copy:
                out_copy.pop().wait()

            def rows(i, _):
                at = pl.ds(pl.multiple_of(i * 16, 16), 16)
                x = r.nin[0, at, :]
                if rs:
                    o = r.own[h, 0, at, :].astype(F32) + r.rx[h, at, :].astype(F32) + r.ry[h, at, :].astype(F32)
                    o = o.astype(BF).astype(F32)
                if norm in (N_LN, N_RES):
                    x = x + o + vrow(vec.bias)
                    r.nout[at, :] = x
                if norm == N_RES:
                    r.nout1[at, :] = r.g[h, at, :].astype(F32)
                    return 0
                mean = jnp.sum(x, axis=-1, keepdims=True) * (1.0 / D)
                cen = x - mean
                var = jnp.sum(cen * cen, axis=-1, keepdims=True) * (1.0 / D)
                rstd = lax.rsqrt(var + 1e-5)
                if norm in (N_FIRST, N_LN):
                    r.g[h, at, :] = (cen * rstd * vrow(vec.gain) + vrow(vec.shift)).astype(BF)
                    return 0
                xh = cen * rstd
                dxh = o * vrow(vec.gain)
                m1 = jnp.sum(dxh, axis=-1, keepdims=True) * (1.0 / D)
                m2 = jnp.sum(dxh * xh, axis=-1, keepdims=True) * (1.0 / D)
                base = r.nin[1, at, :]
                res = base + rstd * (dxh - m1 - xh * m2)
                r.nout[at, :] = res
                if ag:
                    r.g[h, at, :] = res.astype(BF)
                sums = [o * xh, o] + ([res, base] if norm == N_BWD2 else [])
                for j, s in enumerate(sums):
                    r.acc[j] += s[0:8] + s[8:16]
                return 0

            lax.fori_loop(0, ROWS // 16, rows, 0)
            if norm != N_FIRST:
                out_copy.append(begin(r.nout, r.out0.at[h], r.nsem.at[2]))
            if norm == N_RES:
                out_copy.append(begin(r.nout1, r.out1.at[h], r.nsem.at[3]))

        top, bot = pl.ds(0, 64), pl.ds(64, 64)
        if rs:
            seq = [(h, q) for h in (0, 1) for q in Q_ORDER]
            lhs_loads, rs_copy, w1_loads = {}, {}, []

            def w1_load():
                for n in range(tiles1):
                    at = pl.ds(n * tile1, tile1)
                    src, dst = r.wa.at[rs[0]], r.w1
                    src, dst = (src.at[at], dst.at[at]) if rs[2] else (src.at[:, at], dst.at[:, at])
                    w1_loads.append(begin(src, dst, r.w1_sem.at[n]))

            def lhs_load(i):
                h, q = seq[i]
                lhs_loads[i] = begin(r.lhs1.at[h, pl.ds(2 * q, 2)], r.lhs.at[i % 2], r.lhs_sem.at[i % 2])

            def rs_start(h, j, src, dst, dev):
                c = remote(src, dst, r.rs_send.at[h, j], r.rs_recv.at[h, j], dev)
                c.start()
                rs_copy[h, j] = c

            def partial(i, between=None):
                h, q = seq[i]
                lhs_loads[i].wait()
                if h == 1:
                    rs_copy[0, q].wait_send()

                def tile(n, _):
                    at = pl.ds(pl.multiple_of(n * tile1, tile1), tile1)
                    x = r.lhs[i % 2].reshape(2 * ROWS, k1)
                    y = dims(x, r.w1[at, :], 1, 1) if rs[2] else dims(x, r.w1[:, at], 1, 0)
                    y = y.astype(BF)
                    r.own[h, q, :, at] = y[0:ROWS]
                    r.snd[q, :, at] = y[ROWS:]
                    return 0

                if i == 0:
                    for n in range(tiles1):
                        w1_loads[n].wait()
                        tile(n, 0)
                    await_peers()
                else:
                    tile(0, 0)
                    if between:
                        between()
                    if tiles1 > 1:
                        lax.fori_loop(1, tiles1, tile, 0)
                if i + 2 < len(seq):
                    lhs_load(i + 2)
                rs_start(h, q, r.snd.at[q], r.drx.at[h, q], core)

            def add_into(dst, src, n):
                def rows(i, _):
                    at = pl.ds(pl.multiple_of(i * 16, 16), 16)
                    dst[at, :] = (dst[at, :].astype(F32) + src[at, :].astype(F32)).astype(BF)
                    return 0

                lax.fori_loop(0, n // 16, rows, 0)

            def merge(h, q):
                rs_copy[h, q].wait_recv()
                add_into(r.own.at[h, q], r.drx.at[h, q], ROWS)

            def first_sends(h, q):
                if q == 3:
                    rs_start(h, 4, r.own.at[h, 3, top], r.hx.at[h], px)
                    rs_start(h, 5, r.own.at[h, 3, bot], r.hy.at[h], py)
                if q == 1:
                    rs_start(h, 6, r.own.at[h, 1, top], r.rx.at[h, top], px)
                if q == 2:
                    rs_start(h, 7, r.own.at[h, 2, bot], r.ry.at[h, bot], py)

            def third_sends(h):
                rs_copy[h, 5].wait_recv()
                add_into(r.own.at[h, 1, bot], r.hy.at[h], 64)
                rs_start(h, 8, r.own.at[h, 1, bot], r.rx.at[h, bot], px)
                rs_copy[h, 4].wait_recv()
                add_into(r.own.at[h, 2, top], r.hx.at[h], 64)
                rs_start(h, 9, r.own.at[h, 2, top], r.ry.at[h, top], py)

            def rs_done(h):
                for j in (6, 7, 8, 9):
                    rs_copy[h, j].wait_recv()

            def step(i, send=True):
                def between():
                    h, q = seq[i - 1]
                    merge(h, q)
                    if send:
                        first_sends(h, q)

                partial(i, between if i % 4 else None)

        if ag:
            full = r.full
            ag_copy, g_copy, ready_loads, res_out, w2_ready, count = {}, {}, {}, {}, [], [0]

            def ag_start(h, j, src, dst, dev):
                c = remote(src, dst, r.ag_send.at[h, j], r.ag_recv.at[h, j], dev)
                c.start()
                ag_copy[h, j] = c

            def own_sends(h):
                g = r.g
                ag_start(h, 1, g.at[h, top], full.at[h, 2, top], px)
                ag_start(h, 3, g.at[h, bot], full.at[h, 4, bot], py)
                ag_start(h, 2, g.at[h, bot], full.at[h, 2, bot], px)
                ag_start(h, 4, g.at[h, top], full.at[h, 4, top], py)
                ag_start(h, 0, g.at[h], full.at[h, 1], core)
                g_copy[h] = begin(g.at[h], full.at[h, 0], r.g_sem.at[h])

            def forward(h):
                ag_copy[h, 1].wait_recv()
                ag_start(h, 5, full.at[h, 2, top], full.at[h, 6, top], py)
                ag_copy[h, 3].wait_recv()
                ag_start(h, 6, full.at[h, 4, bot], full.at[h, 6, bot], px)

            def cross(h):
                ag_copy[h, 2].wait_recv()
                ag_start(h, 7, full.at[h, 2], full.at[h, 3], core)
                ag_copy[h, 4].wait_recv()
                ag_start(h, 8, full.at[h, 4], full.at[h, 5], core)

            def cross_far(h):
                ag_copy[h, 5].wait_recv()
                ag_copy[h, 6].wait_recv()
                ag_start(h, 9, full.at[h, 6], full.at[h, 7], core)

            def ready(h, q):
                s = count[0] % 2
                count[0] += 1
                if q == 0:
                    g_copy.pop(h).wait()
                    ag_copy[h, 0].wait_recv()
                else:
                    ag_copy[h, {1: 7, 2: 8, 3: 9}[q]].wait_recv()
                pair = pl.ds(2 * q, 2)
                loads = [begin(full.at[h, pair], r.agin.at[s], r.agin_sem.at[s])]
                if what == DACT:
                    loads.append(begin(r.pre.at[h, pair], r.pre_st.at[s], r.pre_sem.at[s]))
                ready_loads[h, q] = (s, loads)

            def product(h, q):
                if (h, q) not in ready_loads:
                    ready(h, q)
                s, loads = ready_loads.pop((h, q))
                pair = pl.ds(2 * q, 2)
                if not w2_ready:
                    w2_copy.wait()
                    w2_ready.append(1)
                for c in res_out.pop(s, ()):
                    c.wait()
                for c in loads:
                    c.wait()
                nt = 384 if what in (QKV, DCTX) else 512

                def tile(n, _):
                    at = pl.ds(pl.multiple_of(n * nt, nt), nt)
                    x = r.agin[s].reshape(2 * ROWS, D)
                    y = dims(x, r.w2[:, at], 1, 0) if what == UP else dims(x, r.w2[at, :], 1, 1)
                    if what == UP:
                        u = y + r.b_up[ag[1] : ag[1] + 1, at]
                        r.pre_st[s, :, :, at] = u.reshape(2, ROWS, nt)
                        y = u * (0.5 * (1.0 + jnp.tanh(GELU_C * (u + 0.044715 * (u * u * u)))))
                    if what == DACT:
                        u = r.pre_st[s, :, :, at].reshape(2 * ROWS, nt)
                        y = y.astype(BF).astype(F32)
                        t = jnp.tanh(GELU_C * (u + 0.044715 * (u * u * u)))
                        slope = 0.5 * (1.0 + t) + (0.5 * GELU_C) * u * (1.0 - t * t) * (1.0 + (3 * 0.044715) * (u * u))
                        y = y * slope
                        r.bacc[:, at] += jnp.sum(y.reshape(2 * ROWS // 8, 8, nt), axis=0)
                    r.res_st[s, :, :, at] = y.astype(BF).reshape(2, ROWS, nt)
                    return 0

                if n2 == nt:
                    tile(0, 0)
                else:
                    lax.fori_loop(0, n2 // nt, tile, 0)
                res_out[s] = [begin(r.res_st.at[s], r.res.at[h, pair], r.res_sem.at[s])]
                if what == UP:
                    res_out[s].append(begin(r.pre_st.at[s], r.pre.at[h, pair], r.pre_sem.at[s]))

        todo = []
        if fills:
            jobs = ((r.f0l, r.f0r, r.g0), (r.f1l, r.f1r, r.g1))
            todo = [[job, f[0] // bm, f[1] // BN, 0] for job, f in zip(jobs, fills)]

        def fill(n):
            while n > 0 and todo:
                (lhs, rhs, out), blocks, tiles, done = todo[0]
                count_all = blocks * tiles

                def lhs_copy(b):
                    return Pieces(lhs.at[:, pl.ds(pl.multiple_of(b * bm, bm), bm)], r.f_lhs, r.f_sem.at[0], 8)

                def rhs_copy(u):
                    t, s = lax.rem(u, tiles), lax.rem(u, 2)
                    return Pieces(rhs.at[:, pl.ds(pl.multiple_of(t * BN, BN), BN)], r.f_rhs.at[s], r.f_sem.at[1 + s], 8)

                def put_copy(u):
                    b, t, s = lax.div(u, tiles), lax.rem(u, tiles), lax.rem(u, 2)
                    dst = out.at[pl.ds(pl.multiple_of(b * bm, bm), bm), pl.ds(pl.multiple_of(t * BN, BN), BN)]
                    return Pieces(r.f_out.at[s], dst, r.f_sem.at[3 + s], 3)

                if done == 0:
                    lhs_copy(jnp.int32(0)).start()
                    rhs_copy(jnp.int32(0)).start()
                upto = min(count_all, done + n)

                def unit(u, _):
                    b, t, s = lax.div(u, tiles), lax.rem(u, tiles), lax.rem(u, 2)

                    @pl.when(t == 0)
                    def _():
                        lhs_copy(b).wait()
                        for k in range(TOK // 256):
                            r.f_at[:, k * 256 : (k + 1) * 256] = r.f_lhs[k * 256 : (k + 1) * 256, :].T

                        @pl.when(b + 1 < blocks)
                        def _():
                            lhs_copy(b + 1).start()

                    rhs_copy(u).wait()

                    @pl.when(u + 1 < count_all)
                    def _():
                        rhs_copy(u + 1).start()

                    @pl.when(u >= 2)
                    def _():
                        put_copy(u - 2).wait()

                    r.f_out[s] = dims(r.f_at[...], r.f_rhs[s], 1, 0).astype(BF)
                    put_copy(u).start()
                    return 0

                lax.fori_loop(done, upto, unit, 0)
                n -= upto - done
                todo[0][3] = upto
                if upto == count_all:
                    for u in range(max(0, count_all - 2), count_all):
                        put_copy(jnp.int32(u)).wait()
                    todo.pop(0)

        steps = list(plan)

        def fill_next():
            if steps:
                fill(steps.pop(0))

        say_here((core, px, py))
        if rs:
            lhs_load(0)
            w1_load()
            lhs_load(1)
        if kind == TOP:
            srcs = [begin(r.src.at[h], r.g.at[h], r.g_sem.at[h]) for h in (0, 1)]
        loads = norm_load(0)
        if ag:
            w2_copy = begin(r.wb.at[ag[1]], r.w2, r.w2_sem, 8)
        for j in range(n_acc):
            r.acc[j] = jnp.zeros((8, D), F32)
        if ag and what == DACT:
            r.bacc[...] = jnp.zeros((8, n2), F32)

        def both_halves():
            for i in range(4):
                step(i)
            merge(0, 0)
            third_sends(0)
            for i in range(4, 8):
                step(i)
            merge(1, 0)
            fill_next()
            rs_done(0)
            norm_half(0, loads)

        if kind == FIRST:
            norm_half(0, loads)
            loads = norm_load(1)
            await_peers()
            own_sends(0)
            norm_half(1, loads)
            product(0, 0)
            forward(0)
            own_sends(1)
            ready(1, 0)
            cross(0)
            product(1, 0)
            ready(0, 1)
            ready(0, 2)
            product(0, 1)
            product(0, 2)
            cross_far(0)
            product(0, 3)
            forward(1)
            cross(1)
            ready(1, 1)
            ready(1, 2)
            product(1, 1)
            product(1, 2)
            cross_far(1)
            product(1, 3)
        elif kind == LAST:
            both_halves()
            loads = norm_load(1)
            fill_next()
            third_sends(1)
            fill(1 << 20)
            rs_done(1)
            norm_half(1, loads)
        elif kind == MID:
            both_halves()
            loads = norm_load(1)
            fill_next()
            third_sends(1)
            own_sends(0)
            fill_next()
            ready(0, 0)
            product(0, 0)
            fill_next()
            rs_done(1)
            norm_half(1, loads)
            fill_next()
            forward(0)
            own_sends(1)
            fill_next()
            ready(1, 0)
            product(1, 0)
            fill_next()
            cross(0)
            fill_next()
            ready(0, 1)
            ready(0, 2)
            product(0, 1)
            product(0, 2)
            cross_far(0)
            fill(1 << 20)
            product(0, 3)
            forward(1)
            cross(1)
            ready(1, 1)
            ready(1, 2)
            product(1, 1)
            product(1, 2)
            cross_far(1)
            product(1, 3)
        elif kind == TOP:
            for c in srcs:
                c.wait()
            partial(0)
            own_sends(0)
            step(1, False)
            step(2, False)
            step(3, False)
            forward(0)
            own_sends(1)
            merge(0, 0)
            ready(0, 0)
            product(0, 0)
            cross(0)
            ready(1, 0)
            product(1, 0)
            ready(0, 1)
            ready(0, 2)
            product(0, 1)
            product(0, 2)
            forward(1)
            cross_far(0)
            for q in (3, 1, 2):
                first_sends(0, q)
            partial(4)
            product(0, 3)
            cross(1)
            step(5, False)
            ready(1, 1)
            ready(1, 2)
            product(1, 1)
            cross_far(1)
            product(1, 2)
            third_sends(0)
            for q in (3, 1):
                if q == 1:
                    merge(1, 1)
                first_sends(1, q)
            partial(6)
            merge(1, 2)
            first_sends(1, 2)
            partial(7)
            merge(1, 0)
            ready(1, 3)
            rs_done(0)
            norm_half(0, loads)
            loads = norm_load(1)
            product(1, 3)
            third_sends(1)
            rs_done(1)
            norm_half(1, loads)

        for j in range(n_acc):
            r.vo[j : j + 1, :] = jnp.sum(r.acc[j], axis=0, keepdims=True)
        if n_acc:
            r.vo[n_acc:8, :] = jnp.zeros((8 - n_acc, D), F32)
        if ag and what == DACT:
            r.bup[...] = jnp.sum(r.bacc[...], axis=0, keepdims=True)
        for c in out_copy:
            c.wait()
        if rs:
            for (h, j), c in rs_copy.items():
                if not (h == 0 and j < 4):
                    c.wait_send()
        if ag:
            for c in ag_copy.values():
                c.wait_send()
            for cs in res_out.values():
                for c in cs:
                    c.wait()

    small = ["vec", "b_up", "vo", "bup"]
    return call(name, cid, body, ins, outs, sc, small)


def visible(me, length):
    row = lax.broadcasted_iota(jnp.int32, (ROWS, ROWS), 0)
    col = lax.broadcasted_iota(jnp.int32, (ROWS, ROWS), 1)
    row_pos = lax.bitwise_or(lax.shift_left(lax.bitwise_xor(lax.shift_right_logical(row, 4), me), 4), lax.bitwise_and(row, 15))
    col_pos = lax.bitwise_or(lax.shift_left(lax.bitwise_xor(lax.shift_right_logical(col, 4), me), 4), lax.bitwise_and(col, 15))
    return (col_pos <= row_pos) & (col_pos < length)


def head_parts(x, h):
    return x[:, h * HD : (h + 1) * HD], x[:, 384 + h * HD : 384 + (h + 1) * HD], x[:, 768 + h * HD : 768 + (h + 1) * HD]


def probs(q, k, mask):
    s = dims(q, k, 1, 1) * (HD**-0.5)
    s = jnp.where(mask, s, -1e30)
    e = jnp.exp(s - jnp.max(s, axis=-1, keepdims=True))
    return e * (1.0 / jnp.sum(e, axis=-1, keepdims=True))


def attn_fwd_kernel(info, qkv, ctx):
    for i in range(SEQS):
        mask = visible(info[16], info[pl.program_id(0) * SEQS + i])
        x = qkv[:, i].reshape(ROWS, 1152)
        parts = []
        for h in range(HEADS):
            q, k, v = head_parts(x, h)
            parts.append(dims(probs(q, k, mask).astype(BF), v, 1, 0).astype(BF))
        ctx[:, i] = jnp.concatenate(parts, axis=-1).reshape(8, 16, 384)


def attn_bwd_one(info, i, qkv, dctx, out):
    mask = visible(info[16], info[pl.program_id(0) * SEQS + i])
    x = qkv[:, i].reshape(ROWS, 1152)
    dc = dctx[:, i].reshape(ROWS, 384)
    dqs, dks, dvs = [], [], []
    for h in range(HEADS):
        q, k, v = head_parts(x, h)
        d = dc[:, h * HD : (h + 1) * HD]
        p = probs(q, k, mask)
        dp = dims(d, v, 1, 1).astype(BF).astype(F32)
        dvs.append(dims(p.astype(BF), d, 0, 0).astype(BF))
        ds = p * (dp - jnp.sum(dp * p, axis=-1, keepdims=True))
        ds = (ds * (HD**-0.5)).astype(BF)
        dqs.append(dims(ds, k, 1, 0).astype(BF))
        dks.append(dims(ds, q, 0, 0).astype(BF))
    out[:, i] = jnp.concatenate(dqs + dks + dvs, axis=-1).reshape(8, 16, 1152)


def seq_spec(n):
    return pl.BlockSpec((None, 8, SEQS, 16, n), lambda i, info: (i // (8 // SEQS), 0, i % (8 // SEQS), 0, 0))


def by_seq(a):
    return a.reshape(2, 8, 8, 16, a.shape[-1])


def attn_fwd(info, qkv):
    grid_spec = pltpu.PrefetchScalarGridSpec(num_scalar_prefetch=1, grid=(16 // SEQS,), in_specs=[seq_spec(1152)], out_specs=seq_spec(384))
    out = pl.pallas_call(attn_fwd_kernel, name="attn_fwd", out_shape=jax.ShapeDtypeStruct((2, 8, 8, 16, 384), BF), grid_spec=grid_spec)(info, by_seq(qkv))
    return out.reshape(2, 8, ROWS, 384)


def stacking(puts, stacks, n):
    used = sorted({p[1] for p in puts})
    shapes = [jax.ShapeDtypeStruct((n,) + next(p[0].shape for p in puts if p[1] == k), BF) for k in used]
    given = [k for k in used if stacks[k] is not None]
    return used, shapes, given


def attn_bwd(info, qkv, dctx, puts, stacks, n):
    used, shapes, given = stacking(puts, stacks, n)
    m = len(puts)

    def kernel(info, qkv, dctx, *refs):
        grads, refs = refs[:m], refs[m + len(given) :]
        out, outs, bounce, sem = refs[0], refs[1 : 1 + len(used)], refs[1 + len(used) : -1], refs[-1]
        step = pl.program_id(0)

        def load(i):
            return Pieces(grads[i], bounce[i], sem.at[0, i], 8)

        def put(i):
            return Pieces(bounce[i], outs[used.index(puts[i][1])].at[puts[i][2]], sem.at[1, i], 8)

        @pl.when(step == 0)
        def _():
            for i in range(m):
                load(i).start()

        for at, some in ((1, range(m // 2)), (2, range(m // 2, m))):

            @pl.when(step == at)
            def _(some=some):
                for i in some:
                    load(i).wait()
                    put(i).start()

        for i in range(SEQS):
            attn_bwd_one(info, i, qkv, dctx, out)

        @pl.when(step == 16 // SEQS - 1)
        def _():
            for i in range(m):
                put(i).wait()

    hbm = pl.BlockSpec(memory_space=ANY)
    grid_spec = pltpu.PrefetchScalarGridSpec(
        num_scalar_prefetch=1,
        grid=(16 // SEQS,),
        in_specs=[seq_spec(1152), seq_spec(384)] + [hbm] * (m + len(given)),
        out_specs=[seq_spec(1152)] + [hbm] * len(used),
        scratch_shapes=[pltpu.VMEM(p[0].shape, BF) for p in puts] + [pltpu.SemaphoreType.DMA((2, m))],
    )
    res = pl.pallas_call(
        kernel,
        name="attn_bwd",
        out_shape=[jax.ShapeDtypeStruct((2, 8, 8, 16, 1152), BF)] + shapes,
        grid_spec=grid_spec,
        input_output_aliases={3 + m + j: 1 + used.index(k) for j, k in enumerate(given)},
        compiler_params=pltpu.CompilerParams(vmem_limit_bytes=VMEM_LIMIT),
    )(info, by_seq(qkv), by_seq(dctx), *[p[0] for p in puts], *[stacks[k] for k in given])
    for k, a in zip(used, res[1:]):
        stacks[k] = a
    return res[0].reshape(2, 8, ROWS, 1152)


def put_last(puts, stacks):
    m = len(puts)

    def kernel(*refs):
        grads, outs, bounce, sem = refs[:m], refs[2 * m : 3 * m], refs[3 * m : -1], refs[-1]
        loads = [Pieces(grads[i], bounce[i], sem.at[0, i], 8).start() for i in range(m)]
        stores = []
        for i in range(m):
            loads[i].wait()
            stores.append(Pieces(bounce[i], outs[i].at[puts[i][2]], sem.at[1, i], 8).start())
        for c in stores:
            c.wait()

    hbm = pl.BlockSpec(memory_space=ANY)
    olds = [stacks[p[1]] for p in puts]
    res = pl.pallas_call(
        kernel,
        name="put_last",
        out_shape=[jax.ShapeDtypeStruct(a.shape, a.dtype) for a in olds],
        in_specs=[hbm] * (2 * m),
        out_specs=[hbm] * m,
        scratch_shapes=[pltpu.VMEM(p[0].shape, BF) for p in puts] + [pltpu.SemaphoreType.DMA((2, m))],
        input_output_aliases={m + i: i for i in range(m)},
        compiler_params=pltpu.CompilerParams(vmem_limit_bytes=VMEM_LIMIT),
    )(*[p[0] for p in puts], *olds)
    for p, a in zip(puts, res):
        stacks[p[1]] = a


def sum_rows(parts, cid):
    n, half = len(parts), D // 2
    rows = -(-6 * n // 8) * 8
    ins = SimpleNamespace()
    for l, (a, b) in enumerate(parts):
        setattr(ins, f"a{l}", a)
        setattr(ins, f"b{l}", b)

    def body(r):
        core, px, py = peers()
        say_here((core, px, py))
        me = lax.axis_index(TP)
        mine = pl.ds(pl.multiple_of(lax.rem(me, 2) * half, half), half)
        for l in range(n):
            r.v[6 * l : 6 * l + 2, :] = getattr(r, f"a{l}")[0:2, :]
            r.v[6 * l + 2 : 6 * l + 6, :] = getattr(r, f"b{l}")[0:4, :]
        if rows > 6 * n:
            r.v[6 * n :, :] = jnp.zeros((rows - 6 * n, D), F32)
        await_peers()
        c = remote(r.v, r.a, r.send.at[0], r.recv.at[0], core)
        c.start()
        c.wait()
        r.s[0] = r.v[:, mine] + r.a[:, mine]
        for i, dev in ((0, px), (1, py)):
            c = remote(r.s.at[i], r.b.at[i], r.send.at[1 + i], r.recv.at[1 + i], dev)
            c.start()
            c.wait()
            r.s[i + 1] = r.s[i] + r.b[i]
        c = remote(r.s.at[2], r.t.at[:, mine], r.send.at[3], r.recv.at[3], core)
        c.start()
        r.u[:, mine] = r.s[2]
        c.wait()
        first = lax.broadcasted_iota(jnp.int32, (1, D), 1) < half
        keep = first == (lax.rem(me, 2) == 0)
        for l in range(n):
            at = slice(6 * l, 6 * l + 6)
            r.o[l] = jnp.where(keep, r.u[at, :], r.t[at, :])

    dma = pltpu.SemaphoreType.DMA
    scratch = SimpleNamespace(
        v=pltpu.VMEM((rows, D), F32),
        a=pltpu.VMEM((rows, D), F32),
        s=pltpu.VMEM((3, rows, half), F32),
        b=pltpu.VMEM((2, rows, half), F32),
        t=pltpu.VMEM((rows, D), F32),
        u=pltpu.VMEM((rows, D), F32),
        send=dma((4,)),
        recv=dma((4,)),
    )
    outs = SimpleNamespace(o=jax.ShapeDtypeStruct((n, 6, D), F32))
    return call("sum_rows", cid, body, ins, outs, scratch, list(vars(ins)) + ["o"]).o


def group_body(x_loc, dy_loc, len_loc, wqkv, wout, wup, bup, wdown, vec):
    n = wqkv.shape[0]
    ids = iter(range(64))
    x = x_loc.reshape(2, ROWS, D)
    dy = dy_loc.reshape(2, ROWS, D)
    wq = jnp.transpose(wqkv, (0, 2, 3, 4, 1)).reshape(n, 1152, D)
    wo = wout.reshape(n, 384, D)
    info = jnp.concatenate([len_loc, lax.axis_index(TP).reshape(1).astype(jnp.int32)])

    def flat(a):
        return a.reshape(TOK, a.shape[-1])

    def ln(layer, row, bias=None):
        return SimpleNamespace(gain=(layer, row), shift=(layer, row + 1), bias=bias)

    saved = [SimpleNamespace() for _ in range(n)]
    r = fused("first", next(ids), FIRST, N_FIRST, dict(in0=x, wb=wq, vec=vec), ln(0, 0), ag=(QKV, 0))
    s = saved[0]
    s.x, s.a, s.qkv = x, r.full, r.res
    for l in range(n):
        s = saved[l]
        s.ctx = attn_fwd(info, s.qkv)
        arrays = dict(lhs1=s.ctx, wa=wo, wb=wup, in0=s.x, vec=vec, b_up=bup)
        r = fused(f"mlp_in_{l}", next(ids), MID, N_LN, arrays, ln(l, 2, (l, 4)), rs=(l, 384, False), ag=(UP, l))
        s.hid, s.m, s.act, s.pre = r.out0, r.full, r.res, r.pre
        if l + 1 < n:
            arrays = dict(lhs1=s.act, wa=wdown, wb=wq, in0=s.hid, vec=vec)
            r = fused(f"attn_in_{l + 1}", next(ids), MID, N_LN, arrays, ln(l + 1, 0, (l, 5)), rs=(l, 1536, False), ag=(QKV, l + 1))
            s = saved[l + 1]
            s.x, s.a, s.qkv = r.out0, r.full, r.res
    s = saved[n - 1]
    arrays = dict(lhs1=s.act, wa=wdown, wb=wdown, in0=s.hid, vec=vec, src=dy, pre=s.pre)
    r = fused("top", next(ids), TOP, N_RES, arrays, ln(0, 0, (n - 1, 5)), rs=(n - 1, 1536, False), ag=(DACT, n - 1))
    y, d_cur, d_full, d_pre = r.out0, r.out1, r.full, r.res
    g_bup, rows, puts, stacks = [r.bup], [], [], [None] * 4
    for l in reversed(range(n)):
        s = saved[l]
        arrays = dict(lhs1=d_pre, wa=wup, wb=wo, in0=s.hid, in1=d_cur, vec=vec, f0l=flat(s.act), f0r=flat(d_full), f1l=flat(s.m), f1r=flat(d_pre))
        r = fused(
            f"d_mlp_{l}", next(ids), MID, N_BWD2, arrays, ln(l, 2), rs=(l, 1536, True), ag=(DCTX, l),
            fills=((1536, D), (D, 1536)), bm=768, plan=(4, 2, 2, 7, 2, 1, 2, 2),
        )
        d_hid, d_attn, v3 = r.out0, r.full, r.vo
        puts += [(r.g0, 3, l), (r.g1, 2, l)]
        d_qkv = attn_bwd(info, s.qkv, r.res, puts, stacks, n)
        arrays = dict(lhs1=d_qkv, wa=wq, in0=s.x, in1=d_hid, vec=vec, f0l=flat(s.ctx), f0r=flat(d_attn), f1l=flat(d_qkv), f1r=flat(s.a))
        common = dict(rs=(l, 1152, False), fills=((384, D), (1152, D)))
        if l:
            arrays.update(wb=wdown, pre=saved[l - 1].pre)
            r = fused(f"d_attn_{l}", next(ids), MID, N_BWD1, arrays, ln(l, 0), ag=(DACT, l - 1), plan=(9, 4, 1, 7, 1, 1, 1), **common)
            g_bup.append(r.bup)
            d_full, d_pre = r.full, r.res
        else:
            r = fused(f"d_attn_{l}", next(ids), LAST, N_BWD1, arrays, ln(l, 0), plan=(9, 5), **common)
        puts = [(r.g0, 1, l), (r.g1, 0, l)]
        rows.append((r.vo, v3))
        d_cur = r.out0
    put_last(puts, stacks)
    g_vec = sum_rows(rows[::-1], next(ids))
    g_qkv = jnp.transpose(stacks[0].reshape(n, 3, HEADS, HD, D), (0, 4, 1, 2, 3))
    g_out = stacks[1].reshape(n, HEADS, HD, D)
    shape = x_loc.shape
    return y.reshape(shape), d_cur.reshape(shape), g_qkv, g_out, stacks[2], jnp.concatenate(g_bup[::-1]), stacks[3], g_vec


def solution(mesh):
    act_spec = P(DP, TP, None)
    in_specs = (act_spec, act_spec, P(DP), P(None, None, None, TP, None), P(None, TP, None, None), P(None, None, TP), P(None, TP), P(None, TP, None), P())
    out_specs = (act_spec, act_spec, P(DP, None, None, TP, None), P(DP, TP, None, None), P(DP, None, TP), P(DP, TP), P(DP, TP, None), P(DP, None, None))
    return jax.shard_map(group_body, mesh=mesh, in_specs=in_specs, out_specs=out_specs, check_vma=False)
```

time: 2570 us -> 1790 us (0.70)
  Pallas kernels: 0 us -> 1770 us
  waiting for transfers between devices: 1520 us -> 0 us
  matrix products: 848 us -> 0 us
  other arithmetic: 140 us -> 1.87 us
  local copies, waits for them, and re-layouts: 41.2 us -> 6.63 us
    pallas_call x0 -> x21, Pallas kernels: none -> 1770 us  [the longest x14 1590 us: call(): pl.pallas_call(kernel, name=name, out_shape=list(vars(outs).values()), in...]
    dot_general x54 -> x0, matrix products: 848 us -> none  [the longest x3 105 us: layer_bwd(): jnp.einsum('bsd,fd->bsf', d_mlp, w_down, preferred_element_type=jnp.float32)]
    reduce_scatter x12 -> x0, waiting for transfers between devices: 830 us -> none  [the longest x3 248 us: layer_fwd(): lax.psum_scatter(attn_part, TENSOR_AXIS, scatter_dimension=1, tiled=True)]
    all_gather x12 -> x0, waiting for transfers between devices: 650 us -> none  [the longest x3 202 us: layer_fwd(): a_full = lax.all_gather(a_shard, TENSOR_AXIS, axis=1, tiled=True)]
    reduce_sum x29 -> x0, other arithmetic: 57.8 us -> none  [the longest x12 29.7 us: layer_norm(): return centered * lax.rsqrt(row_var + 1e-05) * gain_vec + shift_vec]
    another operation x6 -> x0, other arithmetic: 52.6 us -> none  [group_body(): jnp.stack([grad_set[grad_pos] for grad_set in layer_grads])]
    psum x1 -> x0, waiting for transfers between devices: 37.6 us -> none  [group_body(): g_vec = lax.psum(stacked[5], TENSOR_AXIS)]
    unnamed x315 -> x13, local copies, waits for them, and re-layouts: 37 us -> 6.63 us
  transfers between devices with their start and end apart: 25 -> 0, of which waited for: 23 -> 0; matrix products, arithmetic and copies ran while one was open for 14% -> 0% of each run, Pallas kernels for 0% -> 0%
where the time goes in v1:
time: 1790 us; the launch traced here: 1780 us
  Pallas kernels  1770 us (99%)
    pallas_call x14, Pallas kernels, call(): pl.pallas_call(kernel, name=name, out_shape=list(vars(outs).values()), in...  1590 us
    pallas_call x3, Pallas kernels, attn_bwd(): pl.pallas_call(kernel, name='attn_bwd', out_shape=[jax.ShapeDtypeStruct((...  95.1 us
    pallas_call x3, Pallas kernels, attn_fwd(): pl.pallas_call(attn_fwd_kernel, name='attn_fwd', out_shape=jax.ShapeDtype...  75.2 us

profile of v1, /device:TPU:0, one launch (start us, length us, event | category | flops | bytes accessed | tf_op | source)
XLA Modules:
  0.0 1781.2 jit_solution(17131394607883728934)
XLA Ops:
  0.6 1.2 pad_add_fusion.info
  1.9 70.3 %first.1 = (bf16[2,8,128,3072]{3,2,1,0:T(8,128)(2,1)}, bf16[2,8,128,1152]{3,2,1,0:T(8,128)(2,1)}) custom-call(f32[2,128,3072]{2,1,0:T(8,128)} %bitcast.62, bf16[3,1152,3072]{2,1,0:T(8,128)(2,1)} %bitcast.49, f32[3,6,3072]{2,1,0:T(8,128)} %refs_4_.17), custom_call_target="tpu_custom_call" | custom-call | tf_op jit(solution)/shard_map/first/pallas_call | solution.py:83
  72.2 25.0 %attn_fwd.3 = bf16[2,8,8,16,384]{4,3,2,1,0:T(8,128)(2,1)} custom-call(s32[17]{0:T(128)} %pad_add_fusion.info, bf16[2,8,8,16,1152]{4,3,2,1,0:T(8,128)(2,1)} %bitcast.78), custom_call_target="tpu_custom_call" | custom-call | tf_op jit(solution)/shard_map/attn_fwd/pallas_call | solution.py:699
  97.2 121.7 %mlp_in_0.1 = (f32[2,128,3072]{2,1,0:T(8,128)}, bf16[2,8,128,3072]{3,2,1,0:T(8,128)(2,1)}, bf16[2,8,128,1536]{3,2,1,0:T(8,128)(2,1)}, f32[2,8,128,1536]{3,2,1,0:T(8,128)}) custom-call(bf16[2,8,128,384]{3,2,1,0:T(8,128)(2,1)} %bitcast.84, bf16[3,384,3072]{2,1,0:T(8,128)(2,1)} %bitcast.55, bf16[3,3072,1536]{2,1,0:T(8,128)(2,1)} %refs_1_.11, ...), custom_call_target="tpu_custom_call" | custom-call | tf_op jit(solution)/shard_map/mlp_in_0/pallas_call | solution.py:83
  218.9 124.4 %attn_in_1.1 = (f32[2,128,3072]{2,1,0:T(8,128)}, bf16[2,8,128,3072]{3,2,1,0:T(8,128)(2,1)}, bf16[2,8,128,1152]{3,2,1,0:T(8,128)(2,1)}) custom-call(bf16[2,8,128,1536]{3,2,1,0:T(8,128)(2,1)} %get-tuple-element.85.refs_0_, bf16[3,1536,3072]{2,1,0:T(8,128)(2,1)} %refs_9_.3, bf16[3,1152,3072]{2,1,0:T(8,128)(2,1)} %bitcast.50, ...), custom_call_target="tpu_custom_call" | custom-call | tf_op jit(solution)/shard_map/attn_in_1/pallas_call | solution.py:83
  343.3 25.0 %attn_fwd.4 = bf16[2,8,8,16,384]{4,3,2,1,0:T(8,128)(2,1)} custom-call(s32[17]{0:T(128)} %pad_add_fusion.info, bf16[2,8,8,16,1152]{4,3,2,1,0:T(8,128)(2,1)} %bitcast.80), custom_call_target="tpu_custom_call" | custom-call | tf_op jit(solution)/shard_map/attn_fwd/pallas_call | solution.py:699
  368.3 121.9 %mlp_in_1.1 = (f32[2,128,3072]{2,1,0:T(8,128)}, bf16[2,8,128,3072]{3,2,1,0:T(8,128)(2,1)}, bf16[2,8,128,1536]{3,2,1,0:T(8,128)(2,1)}, f32[2,8,128,1536]{3,2,1,0:T(8,128)}) custom-call(bf16[2,8,128,384]{3,2,1,0:T(8,128)(2,1)} %bitcast.86, bf16[3,384,3072]{2,1,0:T(8,128)(2,1)} %bitcast.56, bf16[3,3072,1536]{2,1,0:T(8,128)(2,1)} %refs_1_.11, ...), custom_call_target="tpu_custom_call" | custom-call | tf_op jit(solution)/shard_map/mlp_in_1/pallas_call | solution.py:83
  490.2 124.1 %attn_in_2.1 = (f32[2,128,3072]{2,1,0:T(8,128)}, bf16[2,8,128,3072]{3,2,1,0:T(8,128)(2,1)}, bf16[2,8,128,1152]{3,2,1,0:T(8,128)(2,1)}) custom-call(bf16[2,8,128,1536]{3,2,1,0:T(8,128)(2,1)} %get-tuple-element.89.refs_0_, bf16[3,1536,3072]{2,1,0:T(8,128)(2,1)} %refs_9_.3, bf16[3,1152,3072]{2,1,0:T(8,128)(2,1)} %bitcast.51, ...), custom_call_target="tpu_custom_call" | custom-call | tf_op jit(solution)/shard_map/attn_in_2/pallas_call | solution.py:83
  614.3 25.2 %attn_fwd.5 = bf16[2,8,8,16,384]{4,3,2,1,0:T(8,128)(2,1)} custom-call(s32[17]{0:T(128)} %pad_add_fusion.info, bf16[2,8,8,16,1152]{4,3,2,1,0:T(8,128)(2,1)} %bitcast.82), custom_call_target="tpu_custom_call" | custom-call | tf_op jit(solution)/shard_map/attn_fwd/pallas_call | solution.py:699
  639.5 121.2 %mlp_in_2.1 = (f32[2,128,3072]{2,1,0:T(8,128)}, bf16[2,8,128,3072]{3,2,1,0:T(8,128)(2,1)}, bf16[2,8,128,1536]{3,2,1,0:T(8,128)(2,1)}, f32[2,8,128,1536]{3,2,1,0:T(8,128)}) custom-call(bf16[2,8,128,384]{3,2,1,0:T(8,128)(2,1)} %bitcast.88, bf16[3,384,3072]{2,1,0:T(8,128)(2,1)} %bitcast.57, bf16[3,3072,1536]{2,1,0:T(8,128)(2,1)} %refs_1_.11, ...), custom_call_target="tpu_custom_call" | custom-call | tf_op jit(solution)/shard_map/mlp_in_2/pallas_call | solution.py:83
  760.7 118.3 %top.1 = (f32[2,128,3072]{2,1,0:T(8,128)}, f32[2,128,3072]{2,1,0:T(8,128)}, bf16[2,8,128,3072]{3,2,1,0:T(8,128)(2,1)}, bf16[2,8,128,1536]{3,2,1,0:T(8,128)(2,1)}, f32[1,1536]{1,0:T(1,128)}) custom-call(bf16[2,8,128,1536]{3,2,1,0:T(8,128)(2,1)} %get-tuple-element.93.refs_0_, bf16[3,1536,3072]{2,1,0:T(8,128)(2,1)} %refs_9_.3, bf16[3,1536,3072]{2,1,0:T(8,128)(2,1)} %refs_9_.3, ...), custom_call_target="tpu_custom_call" | custom-call | tf_op jit(solution)/shard_map/top/pallas_call | solution.py:83
  879.1 135.6 %d_mlp_2.1 = (f32[2,128,3072]{2,1,0:T(8,128)}, f32[8,3072]{1,0:T(8,128)}, bf16[2,8,128,3072]{3,2,1,0:T(8,128)(2,1)}, bf16[2,8,128,384]{3,2,1,0:T(8,128)(2,1)}, b...) custom-call(bf16[2,8,128,1536]{3,2,1,0:T(8,128)(2,1)} %get-tuple-element.97.refs_0_, ...), custom_call_target="tpu_custom_call" | custom-call | tf_op jit(solution)/shard_map/d_mlp_2/pallas_call | solution.py:83
  1014.6 31.5 %attn_bwd.3 = (bf16[2,8,8,16,1152]{4,3,2,1,0:T(8,128)(2,1)}, bf16[3,3072,1536]{2,1,0:T(8,128)(2,1)}, bf16[3,1536,3072]{2,1,0:T(8,128)(2,1)}) custom-call(s32[17]{0:T(128)} %pad_add_fusion.info, bf16[2,8,8,16,1152]{4,3,2,1,0:T(8,128)(2,1)} %bitcast.83, bf16[2,8,8,16,384]{4,3,2,1,0:T(8,128)(2,1)} %bitcast.107, bf16[1536,3072]{1,0:T(8,128)(2,1)} %get-tuple-element.102.refs_0_, ...), custom_call_target="tpu_custom_call" | custom-call | tf_op jit(solution)/shard_map/attn_bwd/pallas_call | solution.py:754
  1046.1 141.5 %d_attn_2.1 = (f32[2,128,3072]{2,1,0:T(8,128)}, f32[8,3072]{1,0:T(8,128)}, bf16[2,8,128,3072]{3,2,1,0:T(8,128)(2,1)}, bf16[2,8,128,1536]{3,2,1,0:T(8,128)(2,1)},...) custom-call(bf16[2,8,128,1152]{3,2,1,0:T(8,128)(2,1)} %bitcast.76, ...), custom_call_target="tpu_custom_call" | custom-call | tf_op jit(solution)/shard_map/d_attn_2/pallas_call | solution.py:83
  1187.6 135.1 %d_mlp_1.1 = (f32[2,128,3072]{2,1,0:T(8,128)}, f32[8,3072]{1,0:T(8,128)}, bf16[2,8,128,3072]{3,2,1,0:T(8,128)(2,1)}, bf16[2,8,128,384]{3,2,1,0:T(8,128)(2,1)}, b...) custom-call(bf16[2,8,128,1536]{3,2,1,0:T(8,128)(2,1)} %get-tuple-element.109.refs_0_, ...), custom_call_target="tpu_custom_call" | custom-call | tf_op jit(solution)/shard_map/d_mlp_1/pallas_call | solution.py:83
  1322.7 32.0 %attn_bwd.4 = (bf16[2,8,8,16,1152]{4,3,2,1,0:T(8,128)(2,1)}, bf16[3,1152,3072]{2,1,0:T(8,128)(2,1)}, bf16[3,384,3072]{2,1,0:T(8,128)(2,1)}, bf16[3,3072,1536]{2,1,0:T(8,128)(2,1)}, bf16[3,1536,3072]{2,1,0:T(8,128)(2,1)}) custom-call(s32[17]{0:T(128)} %pad_add_fusion.info, ...), custom_call_target="tpu_custom_call", output_to_operand_aliasing={{3}: (7, {}), {4}: (8, {})} | custom-call | tf_op jit(solution)/shard_map/attn_bwd/pallas_call | solution.py:754
  1354.7 141.2 %d_attn_1.1 = (f32[2,128,3072]{2,1,0:T(8,128)}, f32[8,3072]{1,0:T(8,128)}, bf16[2,8,128,3072]{3,2,1,0:T(8,128)(2,1)}, bf16[2,8,128,1536]{3,2,1,0:T(8,128)(2,1)},...) custom-call(bf16[2,8,128,1152]{3,2,1,0:T(8,128)(2,1)} %bitcast.72, ...), custom_call_target="tpu_custom_call" | custom-call | tf_op jit(solution)/shard_map/d_attn_1/pallas_call | solution.py:83
  1495.9 135.3 %d_mlp_0.1 = (f32[2,128,3072]{2,1,0:T(8,128)}, f32[8,3072]{1,0:T(8,128)}, bf16[2,8,128,3072]{3,2,1,0:T(8,128)(2,1)}, bf16[2,8,128,384]{3,2,1,0:T(8,128)(2,1)}, b...) custom-call(bf16[2,8,128,1536]{3,2,1,0:T(8,128)(2,1)} %get-tuple-element.125.refs_0_, ...), custom_call_target="tpu_custom_call" | custom-call | tf_op jit(solution)/shard_map/d_mlp_0/pallas_call | solution.py:83
  1631.2 31.6 %attn_bwd.5 = (bf16[2,8,8,16,1152]{4,3,2,1,0:T(8,128)(2,1)}, bf16[3,1152,3072]{2,1,0:T(8,128)(2,1)}, bf16[3,384,3072]{2,1,0:T(8,128)(2,1)}, bf16[3,3072,1536]{2,1,0:T(8,128)(2,1)}, bf16[3,1536,3072]{2,1,0:T(8,128)(2,1)}) custom-call(s32[17]{0:T(128)} %pad_add_fusion.info, ...), custom_call_target="tpu_custom_call", output_to_operand_aliasing={{1}: (7, {}), {2}: (8, {}), {3}: (9, {}), {4}: (10, {})} | custom-call | tf_op jit(solution)/shard_map/attn_bwd/pallas_call | solution.py:754
  1662.8 88.2 %d_attn_0.1 = (f32[2,128,3072]{2,1,0:T(8,128)}, f32[8,3072]{1,0:T(8,128)}, bf16[384,3072]{1,0:T(8,128)(2,1)}, bf16[1152,3072]{1,0:T(8,128)(2,1)}) custom-call(bf16[2,8,128,1152]{3,2,1,0:T(8,128)(2,1)} %bitcast.74, bf16[3,1152,3072]{2,1,0:T(8,128)(2,1)} %bitcast.54, f32[2,128,3072]{2,1,0:T(8,128)} %bitcast.64, f32[2,128,3072]{2,1,0:T(8,128)} %get-tuple-element.139.refs_3_, ...), custom_call_target="tpu_custom_call" | custom-call | tf_op jit(solution)/shard_map/d_attn_0/pallas_call | solution.py:83
  1751.0 14.9 sum_rows.1
  1765.9 7.5 put_last.1
  1774.1 4.2 copy.36
  1778.4 1.7 copy.37
  (12 shorter events, 1.4 us)
Async XLA Ops:
  1765.9 7.6 copy-start.2
  1765.9 7.6 copy-start.3
  1765.9 7.6 copy-start.4
  1773.4 4.9 copy-start
  1773.5 6.6 copy-start.1

commit v2 on v1

v2 whole, which is shorter than its diff:
```python
from functools import partial
from types import SimpleNamespace

import jax
import jax.numpy as jnp
from jax import lax
from jax.experimental import pallas as pl
from jax.experimental.pallas import tpu as pltpu
from jax.sharding import PartitionSpec as P

TP, DP = "tp", "dp"
D, FF, INNER, QKV_N = 3072, 1536, 384, 1152
ROWS, HALF_ROWS, GROUP = 128, 64, 16
LANES, SUBL = 128, 8
A, B = HALVES = range(2)
PEERS = 8
TOK = len(HALVES) * PEERS * ROWS
HEADS, HD = 4, 96
SEQS, ALL_SEQS = 4, 16
BM, BN, KT = 384, 512, 256
BF, F32 = jnp.bfloat16, jnp.float32
ANY = pl.ANY
VMEM_LIMIT = 66_900_000
GELU_C, GELU_D = 0.7978845608028654, 0.044715
EPS, NEG = 1e-5, -1e30
ONE, TWO, HALF = 1.0, 2, 0.5
OWN, XN, YN, FAR = PAIRS = range(4)
Q_ORDER = (FAR, XN, YN, OWN)
R_X, R_Y, R_FAR = 2, 4, 6
X_FAR, Y_FAR, X_RAW, Y_RAW, X_SUM, Y_SUM, N_RS = range(4, 11)
G_CORE, G_XT, G_XB, G_YB, G_YT, G_FT, G_FB, G_C3, G_C5, G_C7, N_AG = range(11)
CROSSING = {XN: G_C3, YN: G_C5, FAR: G_C7}
FIRST, MID, TOP, LAST = range(4)
N_FIRST, N_LN, N_RES, N_BWD2, N_BWD1 = range(5)
QKV, UP, DACT, DCTX = range(4)
WIDTH = (QKV_N, FF, FF, INNER)
ALL = 1 << 20


def dims(lhs, rhs, lc, rc):
    return lax.dot_general(lhs, rhs, (((lc,), (rc,)), ((), ())), preferred_element_type=F32)


def peers():
    me = lax.axis_index(TP)
    dp = lax.axis_index(DP)

    def flip(bit):
        return me + bit - TWO * bit * lax.rem(lax.div(me, bit), TWO)

    return [(dp, flip(1 << k)) for k in range(3)]


def say_here(devices):
    for dev in devices:
        pl.semaphore_signal(pltpu.get_barrier_semaphore(), inc=1, device_id=dev, device_id_type=pl.DeviceIdType.MESH)


def await_peers(n=3):
    pl.semaphore_wait(pltpu.get_barrier_semaphore(), n)


def remote(src, dst, send, recv, dev):
    return pltpu.make_async_remote_copy(src_ref=src, dst_ref=dst, send_sem=send, recv_sem=recv, device_id=dev, device_id_type=pl.DeviceIdType.MESH)


class Pieces:
    def __init__(self, src, dst, sem, n):
        self.src, self.dst, self.sem, self.n = src, dst, sem, n

    def start(self):
        src, dst = self.src, self.dst
        step = src.shape[-2] // self.n
        for i in range(self.n):
            at = pl.ds(i * step, step)
            if len(src.shape) == 3:
                for j in range(src.shape[0]):
                    pltpu.make_async_copy(src.at[j, at], dst.at[j, at], self.sem).start()
            else:
                pltpu.make_async_copy(src.at[at], dst.at[at], self.sem).start()
        return self

    def wait(self):
        pltpu.make_async_copy(self.src, self.dst, self.sem).wait()


def call(name, cid, body, ins, outs, scratch, small):
    names = [list(vars(a)) for a in (ins, outs, scratch)]

    def kernel(*refs):
        body(SimpleNamespace(**dict(zip(sum(names, []), refs))))

    def spec(n):
        return pl.BlockSpec(memory_space=pltpu.VMEM if n in small else ANY)

    res = pl.pallas_call(
        kernel,
        name=name,
        out_shape=list(vars(outs).values()),
        in_specs=[spec(n) for n in names[0]],
        out_specs=[spec(n) for n in names[1]],
        scratch_shapes=list(vars(scratch).values()),
        compiler_params=pltpu.CompilerParams(vmem_limit_bytes=VMEM_LIMIT, collective_id=cid, has_side_effects=True),
    )(*vars(ins).values())
    return SimpleNamespace(**dict(zip(names[1], res)))


def fused(name, cid, kind, norm, arrays, vec, rs=None, ag=None, fills=(), plan=()):
    ins, outs, sc = SimpleNamespace(**arrays), SimpleNamespace(), SimpleNamespace()
    dma = pltpu.SemaphoreType.DMA
    n_in = len([k for k in arrays if k in ("in0", "in1")])
    n_acc = {N_BWD2: 4, N_BWD1: TWO}.get(norm, 0)
    shard = jax.ShapeDtypeStruct((TWO, ROWS, D), F32)
    if norm != N_FIRST:
        outs.out0 = shard
        sc.nout = pltpu.VMEM((ROWS, D), F32)
    if norm == N_RES:
        outs.out1 = shard
        sc.nout1 = pltpu.VMEM((ROWS, D), F32)
    sc.nin = pltpu.VMEM((n_in, ROWS, D), F32)
    sc.nsem = dma((n_in + TWO,))
    if n_acc:
        outs.vo = jax.ShapeDtypeStruct((SUBL, D), F32)
        sc.acc = pltpu.VMEM((n_acc, SUBL, D), F32)
    if rs:
        k1 = rs[1]
        tile1 = 1024
        tiles1 = D // tile1
        halves = (TWO, ROWS, D)
        sc.w1 = pltpu.VMEM((D, k1) if rs[2] else (k1, D), BF)
        sc.lhs = pltpu.VMEM((TWO, TWO, ROWS, k1), BF)
        sc.own = pltpu.VMEM((TWO, len(PAIRS), ROWS, D), BF)
        sc.snd = pltpu.VMEM((len(PAIRS), ROWS, D), BF)
        sc.drx = pltpu.VMEM((TWO, len(PAIRS), ROWS, D), BF)
        sc.hx = pltpu.VMEM((TWO, HALF_ROWS, D), BF)
        sc.hy = pltpu.VMEM((TWO, HALF_ROWS, D), BF)
        sc.rx = pltpu.VMEM(halves, BF)
        sc.ry = pltpu.VMEM(halves, BF)
        sc.w1_sem = dma((tiles1,))
        sc.lhs_sem = dma((TWO,))
        sc.rs_send = dma((TWO, N_RS))
        sc.rs_recv = dma((TWO, N_RS))
        sc.far_send = dma((tiles1, len(PAIRS)))
        sc.far_recv = dma((tiles1, len(PAIRS)))
    if ag:
        what = ag[0]
        n2 = WIDTH[what]
        outs.full = jax.ShapeDtypeStruct((TWO, PEERS, ROWS, D), BF)
        outs.res = jax.ShapeDtypeStruct((TWO, PEERS, ROWS, n2), BF)
        pairs_of = (TWO, TWO, ROWS, n2)
        sc.w2 = pltpu.VMEM((D, n2) if what == UP else (n2, D), BF)
        sc.g = pltpu.VMEM((TWO, ROWS, D), BF)
        sc.agin = pltpu.VMEM((TWO, TWO, ROWS, D), BF)
        sc.last = pltpu.VMEM((TWO, ROWS, D), BF)
        sc.w2_sem = dma
        sc.g_sem = dma((TWO,))
        sc.agin_sem = dma((TWO,))
        sc.last_sem = dma((TWO,))
        sc.ag_send = dma((TWO, N_AG))
        sc.ag_recv = dma((TWO, N_AG))
        sc.res_st = pltpu.VMEM(pairs_of, BF)
        sc.res_sem = dma((TWO,))
        if what == UP:
            outs.pre = jax.ShapeDtypeStruct((TWO, PEERS, ROWS, n2), F32)
        if what == DACT:
            outs.bup = jax.ShapeDtypeStruct((1, n2), F32)
            sc.bacc = pltpu.VMEM((SUBL, n2), F32)
        if what in (UP, DACT):
            sc.pre_st = pltpu.VMEM(pairs_of, F32)
            sc.pre_sem = dma((TWO,))
    if fills:
        sub_most = max(f[2] for f in fills)
        sc.f_lhs = pltpu.VMEM((TOK, BM), BF)
        sc.f_at = pltpu.VMEM((sub_most, BM, TOK), BF)
        sc.f_rhs = pltpu.VMEM((TWO, TOK, BN), BF)
        sc.f_out = pltpu.VMEM((TWO, BM, BN), BF)
        sc.fl_sem = dma
        sc.fr_sem = dma((TWO,))
        sc.fo_sem = dma((TWO,))
        outs.g0 = jax.ShapeDtypeStruct(fills[0][:2], BF)
        outs.g1 = jax.ShapeDtypeStruct(fills[1][:2], BF)

    def body(r):
        core, px, py = peers()

        def begin(src, dst, sem, n=4):
            return Pieces(src, dst, sem, n).start()

        def norm_load(h):
            some = (r.in0, r.in1) if n_in == TWO else (r.in0,)
            return [begin(x.at[h], r.nin.at[i], r.nsem.at[i]) for i, x in enumerate(some)]

        def vrow(row):
            return r.vec[row[0], pl.ds(row[1], 1), :]

        out_copy = []

        def mean(x):
            return jnp.sum(x, axis=-1, keepdims=True) * (ONE / D)

        def norm_half(h, loads):
            for c in loads:
                c.wait()
            while out_copy:
                out_copy.pop().wait()

            def rows(i, carry):
                at = pl.ds(pl.multiple_of(i * GROUP, GROUP), GROUP)
                x = r.nin[0, at, :]
                if rs:
                    o = r.own[h, OWN, at, :].astype(F32) + r.rx[h, at, :].astype(F32) + r.ry[h, at, :].astype(F32)
                    o = o.astype(BF).astype(F32)
                if norm in (N_LN, N_RES):
                    x = x + o + vrow(vec.bias)
                    r.nout[at, :] = x
                if norm == N_RES:
                    r.nout1[at, :] = r.g[h, at, :].astype(F32)
                    return carry
                cen = x - mean(x)
                rstd = lax.rsqrt(mean(cen * cen) + EPS)
                if norm in (N_FIRST, N_LN):
                    r.g[h, at, :] = (cen * rstd * vrow(vec.gain) + vrow(vec.shift)).astype(BF)
                    return carry
                xh = cen * rstd
                dxh = o * vrow(vec.gain)
                base = r.nin[1, at, :]
                res = base + rstd * (dxh - mean(dxh) - xh * mean(dxh * xh))
                r.nout[at, :] = res
                if ag:
                    r.g[h, at, :] = res.astype(BF)
                sums = [o * xh, o] + ([res, base] if norm == N_BWD2 else [])
                for j, v in enumerate(sums):
                    r.acc[j] += v[:SUBL] + v[SUBL:]
                return carry

            lax.fori_loop(0, ROWS // GROUP, rows, 0)
            if norm != N_FIRST:
                out_copy.append(begin(r.nout, r.out0.at[h], r.nsem.at[n_in]))
            if norm == N_RES:
                out_copy.append(begin(r.nout1, r.out1.at[h], r.nsem.at[n_in + 1]))

        top, bot = pl.ds(0, HALF_ROWS), pl.ds(HALF_ROWS, HALF_ROWS)
        if rs:
            seq = [(h, q) for h in HALVES for q in Q_ORDER]
            lhs_loads, rs_copy, far_copy, w1_loads = {}, {}, {}, []
            own = r.own

            def w1_load():
                for n in range(tiles1):
                    at = pl.ds(n * tile1, tile1)
                    src, dst = r.wa.at[rs[0]], r.w1
                    src, dst = (src.at[at], dst.at[at]) if rs[2] else (src.at[:, at], dst.at[:, at])
                    w1_loads.append(begin(src, dst, r.w1_sem.at[n]))

            def lhs_load(i):
                h, q = seq[i]
                s = i % TWO
                lhs_loads[i] = begin(r.lhs1.at[h, pl.ds(TWO * q, TWO)], r.lhs.at[s], r.lhs_sem.at[s])

            def rs_start(h, j, src, dst, dev):
                c = remote(src, dst, r.rs_send.at[h, j], r.rs_recv.at[h, j], dev)
                c.start()
                rs_copy[h, j] = c

            def far_start(n, j, src, dst, dev):
                c = remote(src, dst, r.far_send.at[n, j], r.far_recv.at[n, j], dev)
                c.start()
                far_copy[n, j] = c

            def add_into(dst, src, n, at_cols=slice(None)):
                def rows(i, carry):
                    at = pl.ds(pl.multiple_of(i * GROUP, GROUP), GROUP)
                    dst[at, at_cols] = (dst[at, at_cols].astype(F32) + src[at, at_cols].astype(F32)).astype(BF)
                    return carry

                lax.fori_loop(0, n // GROUP, rows, 0)

            def far_merge(n, send):
                cols = pl.ds(n * tile1, tile1)
                far_copy[n, 0].wait_recv()
                add_into(own.at[A, FAR], r.drx.at[A, FAR], ROWS, cols)
                if send:
                    far_sends(n)

            def far_sends(n):
                cols = pl.ds(n * tile1, tile1)
                far_start(n, 1, own.at[A, FAR, top, cols], r.hx.at[A, :, cols], px)
                far_start(n, 2, own.at[A, FAR, bot, cols], r.hy.at[A, :, cols], py)

            def product_in(i, between=None, send=True):
                h, q = seq[i]
                s = i % TWO
                lhs_loads[i].wait()
                if i == len(PAIRS):
                    for n in range(tiles1):
                        far_copy[n, 0].wait_send()
                elif h == B:
                    rs_copy[A, q].wait_send()

                def tile(n, carry):
                    at = pl.ds(pl.multiple_of(n * tile1, tile1), tile1)
                    x = r.lhs[s].reshape(TWO * ROWS, k1)
                    y = dims(x, r.w1[at, :], 1, 1) if rs[2] else dims(x, r.w1[:, at], 1, 0)
                    y = y.astype(BF)
                    own[h, q, :, at] = y[:ROWS]
                    r.snd[q, :, at] = y[ROWS:]
                    return carry

                if i == 0:
                    for n in range(tiles1):
                        cols = pl.ds(n * tile1, tile1)
                        w1_loads[n].wait()
                        tile(n, 0)
                        if n == 0:
                            await_peers()
                        far_start(n, 0, r.snd.at[FAR, :, cols], r.drx.at[A, FAR, :, cols], core)
                        if n:
                            far_merge(n - 1, send)
                else:
                    tile(0, 0)
                    if between:
                        between()
                    lax.fori_loop(1, tiles1, tile, 0)
                if i + TWO < len(seq):
                    lhs_load(i + TWO)
                if i:
                    rs_start(h, q, r.snd.at[q], r.drx.at[h, q], core)

            def merge(h, q):
                rs_copy[h, q].wait_recv()
                add_into(own.at[h, q], r.drx.at[h, q], ROWS)

            def first_sends(h, q):
                if q == FAR:
                    rs_start(h, X_FAR, own.at[h, q, top], r.hx.at[h], px)
                    rs_start(h, Y_FAR, own.at[h, q, bot], r.hy.at[h], py)
                if q == XN:
                    rs_start(h, X_RAW, own.at[h, q, top], r.rx.at[h, top], px)
                if q == YN:
                    rs_start(h, Y_RAW, own.at[h, q, bot], r.ry.at[h, bot], py)

            def far_wait(h, j):
                if h == A:
                    for n in range(tiles1):
                        far_copy[n, 1 + j].wait_recv()
                else:
                    rs_copy[h, X_FAR + j].wait_recv()

            def third_sends(h):
                far_wait(h, 1)
                add_into(own.at[h, XN, bot], r.hy.at[h], HALF_ROWS)
                rs_start(h, X_SUM, own.at[h, XN, bot], r.rx.at[h, bot], px)
                far_wait(h, 0)
                add_into(own.at[h, YN, top], r.hx.at[h], HALF_ROWS)
                rs_start(h, Y_SUM, own.at[h, YN, top], r.ry.at[h, top], py)

            def rs_done(h):
                for j in (X_RAW, Y_RAW, X_SUM, Y_SUM):
                    rs_copy[h, j].wait_recv()

            def step(i, send=True):
                def between():
                    h, q = seq[i - 1]
                    if i == 1:
                        far_merge(tiles1 - 1, send)
                        return
                    merge(h, q)
                    if send:
                        first_sends(h, q)

                product_in(i, between if i % len(PAIRS) else None, send)

        if ag:
            full = r.full
            ag_copy, g_copy, ready_loads, res_out, w2_ready, last_copy = {}, {}, {}, {}, [], []

            def ag_start(h, j, src, dst, dev):
                c = remote(src, dst, r.ag_send.at[h, j], r.ag_recv.at[h, j], dev)
                c.start()
                ag_copy[h, j] = c

            def own_sends(h):
                g = r.g
                ag_start(h, G_XT, g.at[h, top], full.at[h, R_X, top], px)
                ag_start(h, G_YB, g.at[h, bot], full.at[h, R_Y, bot], py)
                ag_start(h, G_XB, g.at[h, bot], full.at[h, R_X, bot], px)
                ag_start(h, G_YT, g.at[h, top], full.at[h, R_Y, top], py)
                ag_start(h, G_CORE, g.at[h], full.at[h, 1], core)
                g_copy[h] = begin(g.at[h], full.at[h, 0], r.g_sem.at[h])

            def far_place(h, other):
                return full.at[h, R_FAR + other] if h == A else r.last.at[other]

            def forward(h):
                ag_copy[h, G_XT].wait_recv()
                ag_start(h, G_FT, full.at[h, R_X, top], far_place(h, 0).at[top], py)
                ag_copy[h, G_YB].wait_recv()
                ag_start(h, G_FB, full.at[h, R_Y, bot], far_place(h, 0).at[bot], px)

            def cross(h):
                ag_copy[h, G_XB].wait_recv()
                ag_start(h, G_C3, full.at[h, R_X], full.at[h, R_X + 1], core)
                ag_copy[h, G_YT].wait_recv()
                ag_start(h, G_C5, full.at[h, R_Y], full.at[h, R_Y + 1], core)

            def cross_far(h):
                ag_copy[h, G_FT].wait_recv()
                ag_copy[h, G_FB].wait_recv()
                ag_start(h, G_C7, far_place(h, 0), far_place(h, 1), core)
                if h == B:
                    last_copy.append(begin(r.last.at[0], full.at[h, R_FAR], r.last_sem.at[0]))

            def ready(h, q):
                s = (len(PAIRS) * h + (OWN, XN, YN, FAR).index(q)) % TWO
                pair = pl.ds(TWO * q, TWO)
                loads = []
                if what == DACT:
                    loads.append(begin(r.pre.at[h, pair], r.pre_st.at[s], r.pre_sem.at[s]))
                if q == OWN:
                    g_copy.pop(h).wait()
                    ag_copy[h, G_CORE].wait_recv()
                else:
                    ag_copy[h, CROSSING[q]].wait_recv()
                if (h, q) == (B, FAR):
                    last_copy.append(begin(r.last.at[1], full.at[h, R_FAR + 1], r.last_sem.at[1]))
                else:
                    loads.append(begin(full.at[h, pair], r.agin.at[s], r.agin_sem.at[s]))
                ready_loads[h, q] = (s, loads)

            def product(h, q):
                if (h, q) not in ready_loads:
                    ready(h, q)
                s, loads = ready_loads.pop((h, q))
                pair = pl.ds(TWO * q, TWO)
                if not w2_ready:
                    w2_copy.wait()
                    w2_ready.append(s)
                for c in res_out.pop(s, ()):
                    c.wait()
                for c in loads:
                    c.wait()
                nt = BM if what in (QKV, DCTX) else BN

                def tile(n, carry):
                    at = pl.ds(pl.multiple_of(n * nt, nt), nt)
                    x = r.last[...] if (h, q) == (B, FAR) else r.agin[s]
                    x = x.reshape(TWO * ROWS, D)
                    y = dims(x, r.w2[:, at], 1, 0) if what == UP else dims(x, r.w2[at, :], 1, 1)
                    if what == UP:
                        u = y + r.b_up[pl.ds(ag[1], 1), at]
                        r.pre_st[s, :, :, at] = u.reshape(TWO, ROWS, nt)
                        y = u * (HALF * (ONE + jnp.tanh(GELU_C * (u + GELU_D * (u * u * u)))))
                    if what == DACT:
                        u = r.pre_st[s, :, :, at].reshape(TWO * ROWS, nt)
                        y = y.astype(BF).astype(F32)
                        t = jnp.tanh(GELU_C * (u + GELU_D * (u * u * u)))
                        y = y * (HALF * (ONE + t) + (HALF * GELU_C) * u * (ONE - t * t) * (ONE + (3 * GELU_D) * (u * u)))
                        r.bacc[:, at] += jnp.sum(y.reshape(-1, SUBL, nt), axis=0)
                    r.res_st[s, :, :, at] = y.astype(BF).reshape(TWO, ROWS, nt)
                    return carry

                if n2 == nt:
                    tile(0, 0)
                else:
                    lax.fori_loop(0, n2 // nt, tile, 0)
                res_out[s] = [begin(r.res_st.at[s], r.res.at[h, pair], r.res_sem.at[s])]
                if what == UP:
                    res_out[s].append(begin(r.pre_st.at[s], r.pre.at[h, pair], r.pre_sem.at[s]))

        jobs = []
        if fills:
            refs = ((r.f0l, r.f0r, r.g0), (r.f1l, r.f1r, r.g1))
            jobs = [SimpleNamespace(lhs=f[0], rhs=f[1], out=f[2], blocks=c[0] // BM // c[2], tiles=c[1] // BN, sub=c[2], done=0) for f, c in zip(refs, fills)]

        def lhs_copy(j, k):
            return Pieces(j.lhs.at[:, pl.ds(pl.multiple_of(k * BM, BM), BM)], r.f_lhs, r.fl_sem, PEERS)

        def rhs_copy(j, v):
            s = lax.rem(v, TWO)
            return Pieces(j.rhs.at[:, pl.ds(pl.multiple_of(lax.rem(v, j.tiles) * BN, BN), BN)], r.f_rhs.at[s], r.fr_sem.at[s], PEERS)

        def put_copy(j, u):
            s, v = lax.rem(u, TWO), lax.div(u, j.sub)
            row = lax.div(v, j.tiles) * j.sub + lax.rem(u, j.sub)
            dst = j.out.at[pl.ds(pl.multiple_of(row * BM, BM), BM), pl.ds(pl.multiple_of(lax.rem(v, j.tiles) * BN, BN), BN)]
            return Pieces(r.f_out.at[s], dst, r.fo_sem.at[s], 3)

        def job_begin(j):
            lhs_copy(j, jnp.int32(0)).start()
            rhs_copy(j, jnp.int32(0)).start()

        def fill(n):
            while n > 0 and jobs:
                j = jobs[0]
                rhs_all = j.blocks * j.tiles
                count = rhs_all * j.sub

                def unit(u, carry):
                    v, b, s = lax.div(u, j.sub), lax.rem(u, j.sub), lax.rem(u, TWO)
                    vs, t = lax.rem(v, TWO), lax.rem(v, j.tiles)
                    k = lax.div(v, j.tiles) * j.sub + b

                    @pl.when(t == 0)
                    def _():
                        lhs_copy(j, k).wait()
                        for i in range(TOK // KT):
                            r.f_at[b, :, i * KT : (i + 1) * KT] = r.f_lhs[i * KT : (i + 1) * KT, :].T

                        @pl.when(k + 1 < j.blocks * j.sub)
                        def _():
                            lhs_copy(j, k + 1).start()

                    @pl.when(b == 0)
                    def _():
                        rhs_copy(j, v).wait()

                        @pl.when(v + 1 < rhs_all)
                        def _():
                            rhs_copy(j, v + 1).start()

                    @pl.when(u >= TWO)
                    def _():
                        put_copy(j, u - TWO).wait()

                    r.f_out[s] = dims(r.f_at[b], r.f_rhs[vs], 1, 0).astype(BF)
                    put_copy(j, u).start()
                    return carry

                upto = min(count, j.done + n)
                n -= upto - j.done
                lax.fori_loop(j.done, upto, unit, 0)
                j.done = upto
                if upto == count:
                    for u in (count - TWO, count - 1):
                        put_copy(j, jnp.int32(u)).wait()
                    jobs.pop(0)
                    if jobs:
                        job_begin(jobs[0])

        steps = list(plan)

        def fill_next():
            if steps:
                fill(steps.pop(0))

        say_here((core, px, py))
        if rs:
            lhs_load(0)
            w1_load()
            lhs_load(1)
        if kind == TOP:
            srcs = [begin(r.src.at[h], r.g.at[h], r.g_sem.at[h]) for h in HALVES]
        loads = norm_load(A)
        if ag:
            w2_copy = begin(r.wb.at[ag[1]], r.w2, r.w2_sem, PEERS)
        if jobs:
            job_begin(jobs[0])
        for j in range(n_acc):
            r.acc[j] = jnp.zeros((SUBL, D), F32)
        if ag and what == DACT:
            r.bacc[...] = jnp.zeros((SUBL, n2), F32)

        def both_halves():
            for i in range(len(PAIRS)):
                step(i)
            merge(A, OWN)
            third_sends(A)
            for i in range(len(PAIRS), len(seq)):
                step(i)
            merge(B, OWN)
            fill_next()
            rs_done(A)
            norm_half(A, loads)

        def products(h):
            cross(h)
            fill_next()
            ready(h, XN)
            ready(h, YN)
            product(h, XN)
            product(h, YN)
            fill_next()
            cross_far(h)

        if kind == FIRST:
            norm_half(A, loads)
            loads = norm_load(B)
            await_peers()
            own_sends(A)
            norm_half(B, loads)
            product(A, OWN)
            forward(A)
            own_sends(B)
            ready(B, OWN)
            product(B, OWN)
            products(A)
            product(A, FAR)
            forward(B)
            products(B)
            product(B, FAR)
        elif kind == LAST:
            both_halves()
            loads = norm_load(B)
            fill_next()
            third_sends(B)
            fill(ALL)
            rs_done(B)
            norm_half(B, loads)
        elif kind == MID:
            both_halves()
            loads = norm_load(B)
            fill_next()
            third_sends(B)
            own_sends(A)
            fill_next()
            product(A, OWN)
            fill_next()
            rs_done(B)
            norm_half(B, loads)
            fill_next()
            forward(A)
            own_sends(B)
            fill_next()
            product(B, OWN)
            fill_next()
            products(A)
            fill(ALL)
            product(A, FAR)
            forward(B)
            products(B)
            product(B, FAR)
        elif kind == TOP:
            for c in srcs:
                c.wait()
            product_in(0, send=False)
            own_sends(A)
            for i in range(1, len(PAIRS)):
                step(i, False)
            forward(A)
            own_sends(B)
            merge(A, OWN)
            product(A, OWN)
            ready(B, OWN)
            cross(A)
            product(B, OWN)
            ready(A, XN)
            ready(A, YN)
            product(A, XN)
            product(A, YN)
            forward(B)
            cross_far(A)
            for n in range(tiles1):
                far_sends(n)
            first_sends(A, XN)
            first_sends(A, YN)
            product_in(4)
            product(A, FAR)
            cross(B)
            step(5, False)
            ready(B, XN)
            ready(B, YN)
            product(B, XN)
            cross_far(B)
            product(B, YN)
            third_sends(A)
            first_sends(B, FAR)
            merge(B, XN)
            first_sends(B, XN)
            product_in(6)
            merge(B, YN)
            first_sends(B, YN)
            product_in(7)
            merge(B, OWN)
            rs_done(A)
            norm_half(A, loads)
            loads = norm_load(B)
            product(B, FAR)
            third_sends(B)
            rs_done(B)
            norm_half(B, loads)

        for j in range(n_acc):
            r.vo[pl.ds(j, 1), :] = jnp.sum(r.acc[j], axis=0, keepdims=True)
        if n_acc:
            r.vo[n_acc:, :] = jnp.zeros((SUBL - n_acc, D), F32)
        if ag and what == DACT:
            r.bup[...] = jnp.sum(r.bacc[...], axis=0, keepdims=True)
        for c in out_copy:
            c.wait()
        if rs:
            for (h, j), c in rs_copy.items():
                if h == B or j > OWN + YN + 1:
                    c.wait_send()
            for (n, j), c in far_copy.items():
                if j:
                    c.wait_send()
        if ag:
            for c in ag_copy.values():
                c.wait_send()
            for cs in res_out.values():
                for c in cs:
                    c.wait()
            for c in last_copy:
                c.wait()

    return call(name, cid, body, ins, outs, sc, ("vec", "b_up", "vo", "bup"))


def positions(me):
    def pos(axis):
        i = lax.broadcasted_iota(jnp.int32, (ROWS, ROWS), axis)
        return lax.bitwise_xor(lax.div(i, GROUP), me) * GROUP + lax.rem(i, GROUP)

    return pos(0), pos(1)


def heads_of(x, part, h):
    at = part * INNER + h * HD
    return x[:, at : at + HD]


def softmax(s):
    e = jnp.exp(s - jnp.max(s, axis=-1, keepdims=True))
    return e * (ONE / jnp.sum(e, axis=-1, keepdims=True))


def attn_fwd_kernel(group, info, qkv, ctx, s_ref, p_ref):
    row, col = positions(info[ALL_SEQS])
    for first in range(0, SEQS, group):
        some = [(i, h) for i in range(first, first + group) for h in range(HEADS)]
        xs = {i: qkv[:, i].reshape(ROWS, QKV_N) for i, _ in some}
        for n, (i, h) in enumerate(some):
            mask = (col <= row) & (col < info[pl.program_id(0) * SEQS + i])
            score = dims(heads_of(xs[i], 0, h), heads_of(xs[i], 1, h), 1, 1) * HD**-HALF
            s_ref[n] = jnp.where(mask, score, NEG)
        p_ref[...] = softmax(s_ref[...]).astype(BF)
        out = {i: [] for i in xs}
        for n, (i, h) in enumerate(some):
            out[i].append(dims(p_ref[n], heads_of(xs[i], TWO, h), 1, 0).astype(BF))
        for i, parts in out.items():
            ctx[:, i] = jnp.concatenate(parts, axis=-1).reshape(PEERS, GROUP, INNER)


def attn_bwd_steps(group, info, qkv, dctx, out, s_ref, dp_ref, p_ref, ds_ref):
    row, col = positions(info[ALL_SEQS])
    for first in range(0, SEQS, group):
        some = [(i, h) for i in range(first, first + group) for h in range(HEADS)]
        xs = {i: (qkv[:, i].reshape(ROWS, QKV_N), dctx[:, i].reshape(ROWS, INNER)) for i, _ in some}
        for n, (i, h) in enumerate(some):
            x, d = xs[i]
            mask = (col <= row) & (col < info[pl.program_id(0) * SEQS + i])
            score = dims(heads_of(x, 0, h), heads_of(x, 1, h), 1, 1) * HD**-HALF
            s_ref[n] = jnp.where(mask, score, NEG)
            dp_ref[n] = dims(heads_of(d, 0, h), heads_of(x, TWO, h), 1, 1).astype(BF)
        p = softmax(s_ref[...])
        dp = dp_ref[...].astype(F32)
        p_ref[...] = p.astype(BF)
        ds = p * (dp - jnp.sum(dp * p, axis=-1, keepdims=True))
        ds_ref[...] = (ds * HD**-HALF).astype(BF)
        grads = {i: ([], [], []) for i in xs}
        for n, (i, h) in enumerate(some):
            x, d = xs[i]
            dq, dk, dv = grads[i]
            dq.append(dims(ds_ref[n], heads_of(x, 1, h), 1, 0).astype(BF))
            dk.append(dims(ds_ref[n], heads_of(x, 0, h), 0, 0).astype(BF))
            dv.append(dims(p_ref[n], heads_of(d, 0, h), 0, 0).astype(BF))
        for i, parts in grads.items():
            out[:, i] = jnp.concatenate(sum(parts, []), axis=-1).reshape(PEERS, GROUP, QKV_N)


def seq_spec(n):
    per_half = PEERS // SEQS
    return pl.BlockSpec((None, PEERS, SEQS, GROUP, n), lambda i, info: (lax.div(i, per_half), 0, lax.rem(i, per_half), 0, 0))


def by_seq(a):
    return a.reshape(TWO, PEERS, PEERS, GROUP, a.shape[-1])


def seq_shape(n):
    return jax.ShapeDtypeStruct((TWO, PEERS, PEERS, GROUP, n), BF)


def attn_tiles(group, *types):
    return [pltpu.VMEM((group * HEADS, ROWS, ROWS), t) for t in types]


def attn_fwd(info, qkv, group):
    grid_spec = pltpu.PrefetchScalarGridSpec(
        num_scalar_prefetch=1, grid=(ALL_SEQS // SEQS,), in_specs=[seq_spec(QKV_N)], out_specs=seq_spec(INNER), scratch_shapes=attn_tiles(group, F32, BF)
    )
    out = pl.pallas_call(partial(attn_fwd_kernel, group), name="attn_fwd", out_shape=seq_shape(INNER), grid_spec=grid_spec)(info, by_seq(qkv))
    return out.reshape(TWO, PEERS, ROWS, INNER)


def stacking(puts, stacks, n):
    used = sorted({p[1] for p in puts})
    shapes = [jax.ShapeDtypeStruct((n,) + next(p[0].shape for p in puts if p[1] == k), BF) for k in used]
    given = [k for k in used if stacks[k] is not None]
    return used, shapes, given


def attn_bwd(info, qkv, dctx, puts, stacks, n, group):
    used, shapes, given = stacking(puts, stacks, n)
    m = len(puts)

    def kernel(info, qkv, dctx, *refs):
        grads, refs = refs[:m], refs[m + len(given) :]
        out, outs, refs = refs[0], refs[1 : 1 + len(used)], refs[1 + len(used) :]
        bounce, load_sem, put_sem, tiles = refs[:m], refs[m], refs[m + 1], refs[m + TWO :]
        step = pl.program_id(0)

        def load(i):
            return Pieces(grads[i], bounce[i], load_sem.at[i], PEERS)

        def put(i):
            return Pieces(bounce[i], outs[used.index(puts[i][1])].at[puts[i][TWO]], put_sem.at[i], PEERS)

        @pl.when(step == 0)
        def _():
            for i in range(m):
                load(i).start()

        for at, some in ((1, range(m // TWO)), (TWO, range(m // TWO, m))):

            @pl.when(step == at)
            def _(some=some):
                for i in some:
                    load(i).wait()
                    put(i).start()

        attn_bwd_steps(group, info, qkv, dctx, out, *tiles)

        @pl.when(step == ALL_SEQS // SEQS - 1)
        def _():
            for i in range(m):
                put(i).wait()

    hbm = pl.BlockSpec(memory_space=ANY)
    dma = pltpu.SemaphoreType.DMA
    grid_spec = pltpu.PrefetchScalarGridSpec(
        num_scalar_prefetch=1,
        grid=(ALL_SEQS // SEQS,),
        in_specs=[seq_spec(QKV_N), seq_spec(INNER)] + [hbm] * (m + len(given)),
        out_specs=[seq_spec(QKV_N)] + [hbm] * len(used),
        scratch_shapes=[pltpu.VMEM(p[0].shape, BF) for p in puts] + [dma((m,)), dma((m,))] + attn_tiles(group, F32, BF, BF, BF),
    )
    res = pl.pallas_call(
        kernel,
        name="attn_bwd",
        out_shape=[seq_shape(QKV_N)] + shapes,
        grid_spec=grid_spec,
        input_output_aliases={3 + m + j: 1 + used.index(k) for j, k in enumerate(given)},
        compiler_params=pltpu.CompilerParams(vmem_limit_bytes=VMEM_LIMIT),
    )(info, by_seq(qkv), by_seq(dctx), *[p[0] for p in puts], *[stacks[k] for k in given])
    for k, a in zip(used, res[1:]):
        stacks[k] = a
    return res[0].reshape(TWO, PEERS, ROWS, QKV_N)


def put_last(puts, stacks):
    m = len(puts)

    def kernel(*refs):
        grads, outs, refs = refs[:m], refs[m + m : m + m + m], refs[m + m + m :]
        bounce, load_sem, put_sem = refs[:m], refs[m], refs[m + 1]
        loads = [Pieces(grads[i], bounce[i], load_sem.at[i], PEERS).start() for i in range(m)]
        stores = []
        for i in range(m):
            loads[i].wait()
            stores.append(Pieces(bounce[i], outs[i].at[puts[i][TWO]], put_sem.at[i], PEERS).start())
        for c in stores:
            c.wait()

    hbm = pl.BlockSpec(memory_space=ANY)
    dma = pltpu.SemaphoreType.DMA
    olds = [stacks[p[1]] for p in puts]
    res = pl.pallas_call(
        kernel,
        name="put_last",
        out_shape=[jax.ShapeDtypeStruct(a.shape, a.dtype) for a in olds],
        in_specs=[hbm] * (m + m),
        out_specs=[hbm] * m,
        scratch_shapes=[pltpu.VMEM(p[0].shape, BF) for p in puts] + [dma((m,)), dma((m,))],
        input_output_aliases={m + i: i for i in range(m)},
        compiler_params=pltpu.CompilerParams(vmem_limit_bytes=VMEM_LIMIT),
    )(*[p[0] for p in puts], *olds)
    for p, a in zip(puts, res):
        stacks[p[1]] = a


def sum_rows(parts, cid):
    n, half = len(parts), D // TWO
    per = 6
    rows = -(-per * n // SUBL) * SUBL
    ins = SimpleNamespace()
    for l, (a, b) in enumerate(parts):
        setattr(ins, f"a{l}", a)
        setattr(ins, f"b{l}", b)

    def body(r):
        core, px, py = peers()
        say_here((core, px, py))
        odd = lax.rem(lax.axis_index(TP), TWO)
        mine = pl.ds(pl.multiple_of(odd * half, half), half)
        for l in range(n):
            at = per * l
            r.v[at : at + TWO, :] = getattr(r, f"a{l}")[:TWO, :]
            r.v[at + TWO : at + per, :] = getattr(r, f"b{l}")[: per - TWO, :]
        if rows > per * n:
            r.v[per * n :, :] = jnp.zeros((rows - per * n, D), F32)
        await_peers()

        def send(src, dst, i, dev):
            c = remote(src, dst, r.send.at[i], r.recv.at[i], dev)
            c.start()
            return c

        send(r.v, r.a, 0, core).wait()
        r.s[0] = r.v[:, mine] + r.a[:, mine]
        for i, dev in enumerate((px, py)):
            send(r.s.at[i], r.b.at[i], 1 + i, dev).wait()
            r.s[i + 1] = r.s[i] + r.b[i]
        c = send(r.s.at[TWO], r.t.at[:, mine], 3, core)
        r.u[:, mine] = r.s[TWO]
        c.wait()
        first = lax.broadcasted_iota(jnp.int32, (1, D), 1) < half
        keep = first == (odd == 0)
        for l in range(n):
            at = slice(per * l, per * (l + 1))
            r.o[l] = jnp.where(keep, r.u[at, :], r.t[at, :])

    dma = pltpu.SemaphoreType.DMA
    whole, part = pltpu.VMEM((rows, D), F32), (rows, half)
    scratch = SimpleNamespace(v=whole, a=whole, t=whole, u=whole, s=pltpu.VMEM((3,) + part, F32), b=pltpu.VMEM((TWO,) + part, F32), send=dma((4,)), recv=dma((4,)))
    outs = SimpleNamespace(o=jax.ShapeDtypeStruct((n, per, D), F32))
    return call("sum_rows", cid, body, ins, outs, scratch, list(vars(ins)) + ["o"]).o


def group_body(x_loc, dy_loc, len_loc, wqkv, wout, wup, bup, wdown, vec):
    n = wqkv.shape[0]
    ids = iter(range(ROWS))
    shape = x_loc.shape
    x = x_loc.reshape(TWO, ROWS, D)
    dy = dy_loc.reshape(TWO, ROWS, D)
    wq = jnp.transpose(wqkv, (0, 2, 3, 4, 1)).reshape(n, QKV_N, D)
    wo = wout.reshape(n, INNER, D)
    info = jnp.concatenate([len_loc, lax.axis_index(TP).reshape(1).astype(jnp.int32)])

    def flat(a):
        return a.reshape(TOK, a.shape[-1])

    def row(layer, i, bias=None):
        return SimpleNamespace(gain=(layer, i), shift=(layer, i + 1), bias=bias)

    ln2, bias1, bias2 = TWO, 4, 5
    groups = (TWO, 1, 4)
    saved = [SimpleNamespace() for _ in range(n)]
    r = fused("first", next(ids), FIRST, N_FIRST, dict(in0=x, wb=wq, vec=vec), row(0, 0), ag=(QKV, 0))
    s = saved[0]
    s.x, s.a, s.qkv = x, r.full, r.res
    for l in range(n):
        s = saved[l]
        s.ctx = attn_fwd(info, s.qkv, groups[l])
        arrays = dict(lhs1=s.ctx, wa=wo, wb=wup, in0=s.x, vec=vec, b_up=bup)
        r = fused(f"mlp_in_{l}", next(ids), MID, N_LN, arrays, row(l, ln2, (l, bias1)), rs=(l, INNER, False), ag=(UP, l))
        s.hid, s.m, s.act, s.pre = r.out0, r.full, r.res, r.pre
        if l + 1 < n:
            arrays = dict(lhs1=s.act, wa=wdown, wb=wq, in0=s.hid, vec=vec)
            r = fused(f"attn_in_{l + 1}", next(ids), MID, N_LN, arrays, row(l + 1, 0, (l, bias2)), rs=(l, FF, False), ag=(QKV, l + 1))
            s = saved[l + 1]
            s.x, s.a, s.qkv = r.out0, r.full, r.res
    s = saved[n - 1]
    arrays = dict(lhs1=s.act, wa=wdown, wb=wdown, in0=s.hid, vec=vec, src=dy, pre=s.pre)
    r = fused("top", next(ids), TOP, N_RES, arrays, row(0, 0, (n - 1, bias2)), rs=(n - 1, FF, False), ag=(DACT, n - 1))
    y, d_cur, d_full, d_pre = r.out0, r.out1, r.full, r.res
    g_bup, rows, puts, stacks = [r.bup], [], [], [None] * 4
    mlp_plans = ((10, 5, 0, 15, 5, 0, 6, 1, 5), (6, 3, 0, 10, 3, 0, 4, 1, 4), (8, 4, 0, 13, 4, 0, 5, 1, 5))
    attn_plans = ((6, 4), (4, 3, 0, 6, 2, 0, 1, 1, 2), (6, 4, 0, 8, 3, 0, 1, 1))
    groups = (4, TWO, 1)
    for l in reversed(range(n)):
        s = saved[l]
        arrays = dict(lhs1=d_pre, wa=wup, wb=wo, in0=s.hid, in1=d_cur, vec=vec, f0l=flat(s.act), f0r=flat(d_full), f1l=flat(s.m), f1r=flat(d_pre))
        fills = ((FF, D, 4), (D, FF, 4))
        r = fused(f"d_mlp_{l}", next(ids), MID, N_BWD2, arrays, row(l, ln2), rs=(l, FF, True), ag=(DCTX, l), fills=fills, plan=mlp_plans[l])
        d_hid, d_attn, v3 = r.out0, r.full, r.vo
        puts += [(r.g0, 3, l), (r.g1, 2, l)]
        d_qkv = attn_bwd(info, s.qkv, r.res, puts, stacks, n, groups[l])
        arrays = dict(lhs1=d_qkv, wa=wq, in0=s.x, in1=d_hid, vec=vec, f0l=flat(s.ctx), f0r=flat(d_attn), f1l=flat(d_qkv), f1r=flat(s.a))
        common = dict(rs=(l, QKV_N, False), fills=((INNER, D, 1), (QKV_N, D, 3)), plan=attn_plans[l])
        if l:
            arrays.update(wb=wdown, pre=saved[l - 1].pre)
            r = fused(f"d_attn_{l}", next(ids), MID, N_BWD1, arrays, row(l, 0), ag=(DACT, l - 1), **common)
            g_bup.append(r.bup)
            d_full, d_pre = r.full, r.res
        else:
            r = fused(f"d_attn_{l}", next(ids), LAST, N_BWD1, arrays, row(l, 0), **common)
        puts = [(r.g0, 1, l), (r.g1, 0, l)]
        rows.append((r.vo, v3))
        d_cur = r.out0
    put_last(puts, stacks)
    g_vec = sum_rows(rows[::-1], next(ids))
    g_qkv = jnp.transpose(stacks[0].reshape(n, 3, HEADS, HD, D), (0, 4, 1, 2, 3))
    g_out = stacks[1].reshape(n, HEADS, HD, D)
    return y.reshape(shape), d_cur.reshape(shape), g_qkv, g_out, stacks[2], jnp.concatenate(g_bup[::-1]), stacks[3], g_vec


def solution(mesh):
    act_spec = P(DP, TP, None)
    in_specs = (act_spec, act_spec, P(DP), P(None, None, None, TP, None), P(None, TP, None, None), P(None, None, TP), P(None, TP), P(None, TP, None), P())
    out_specs = (act_spec, act_spec, P(DP, None, None, TP, None), P(DP, TP, None, None), P(DP, None, TP), P(DP, TP), P(DP, TP, None), P(DP, None, None))
    return jax.shard_map(group_body, mesh=mesh, in_specs=in_specs, out_specs=out_specs, check_vma=False)
```

time: 1790 us -> 1690 us (0.944)
  Pallas kernels: 1770 us -> 1670 us
    pallas_call x6, Pallas kernels: 170 us -> 106 us  [the longest x3 67.5 us: attn_bwd(): pl.pallas_call(kernel, name='attn_bwd', out_shape=[seq_shape(QKV_N)] + sh...]
    pallas_call x14, Pallas kernels: 1590 us -> 1550 us  [call(): pl.pallas_call(kernel, name=name, out_shape=list(vars(outs).values()), in...]
where the time goes in v2:
time: 1690 us; the launch traced here: 1680 us
  Pallas kernels  1670 us (99%)
    pallas_call x14, Pallas kernels, call(): pl.pallas_call(kernel, name=name, out_shape=list(vars(outs).values()), in...  1550 us
    pallas_call x3, Pallas kernels, attn_bwd(): pl.pallas_call(kernel, name='attn_bwd', out_shape=[seq_shape(QKV_N)] + sh...  67.5 us
    pallas_call x3, Pallas kernels, attn_fwd(): pl.pallas_call(partial(attn_fwd_kernel, group), name='attn_fwd', out_shap...  38.2 us

profile of v2, /device:TPU:0, one launch (start us, length us, event | category | flops | bytes accessed | tf_op | source)
XLA Modules:
  0.0 1677.7 jit_solution(8978667704806569576)
XLA Ops:
  0.6 1.2 pad_add_fusion.info
  1.9 69.0 %first.1 = (bf16[2,8,128,3072]{3,2,1,0:T(8,128)(2,1)}, bf16[2,8,128,1152]{3,2,1,0:T(8,128)(2,1)}) custom-call(f32[2,128,3072]{2,1,0:T(8,128)} %bitcast.62, bf16[3,1152,3072]{2,1,0:T(8,128)(2,1)} %bitcast.49, f32[3,6,3072]{2,1,0:T(8,128)} %refs_4_.17), custom_call_target="tpu_custom_call" | custom-call | tf_op jit(solution)/shard_map/first/pallas_call | solution.py:96
  70.8 13.0 attn_fwd.3
  83.8 116.4 %mlp_in_0.1 = (f32[2,128,3072]{2,1,0:T(8,128)}, bf16[2,8,128,3072]{3,2,1,0:T(8,128)(2,1)}, bf16[2,8,128,1536]{3,2,1,0:T(8,128)(2,1)}, f32[2,8,128,1536]{3,2,1,0:T(8,128)}) custom-call(bf16[2,8,128,384]{3,2,1,0:T(8,128)(2,1)} %bitcast.84, bf16[3,384,3072]{2,1,0:T(8,128)(2,1)} %bitcast.55, bf16[3,3072,1536]{2,1,0:T(8,128)(2,1)} %refs_1_.11, ...), custom_call_target="tpu_custom_call" | custom-call | tf_op jit(solution)/shard_map/mlp_in_0/pallas_call | solution.py:96
  200.2 120.6 %attn_in_1.1 = (f32[2,128,3072]{2,1,0:T(8,128)}, bf16[2,8,128,3072]{3,2,1,0:T(8,128)(2,1)}, bf16[2,8,128,1152]{3,2,1,0:T(8,128)(2,1)}) custom-call(bf16[2,8,128,1536]{3,2,1,0:T(8,128)(2,1)} %get-tuple-element.85.refs_0_, bf16[3,1536,3072]{2,1,0:T(8,128)(2,1)} %refs_9_.3, bf16[3,1152,3072]{2,1,0:T(8,128)(2,1)} %bitcast.50, ...), custom_call_target="tpu_custom_call" | custom-call | tf_op jit(solution)/shard_map/attn_in_1/pallas_call | solution.py:96
  320.9 15.1 attn_fwd.4
  336.0 118.0 %mlp_in_1.1 = (f32[2,128,3072]{2,1,0:T(8,128)}, bf16[2,8,128,3072]{3,2,1,0:T(8,128)(2,1)}, bf16[2,8,128,1536]{3,2,1,0:T(8,128)(2,1)}, f32[2,8,128,1536]{3,2,1,0:T(8,128)}) custom-call(bf16[2,8,128,384]{3,2,1,0:T(8,128)(2,1)} %bitcast.86, bf16[3,384,3072]{2,1,0:T(8,128)(2,1)} %bitcast.56, bf16[3,3072,1536]{2,1,0:T(8,128)(2,1)} %refs_1_.11, ...), custom_call_target="tpu_custom_call" | custom-call | tf_op jit(solution)/shard_map/mlp_in_1/pallas_call | solution.py:96
  454.0 119.2 %attn_in_2.1 = (f32[2,128,3072]{2,1,0:T(8,128)}, bf16[2,8,128,3072]{3,2,1,0:T(8,128)(2,1)}, bf16[2,8,128,1152]{3,2,1,0:T(8,128)(2,1)}) custom-call(bf16[2,8,128,1536]{3,2,1,0:T(8,128)(2,1)} %get-tuple-element.89.refs_0_, bf16[3,1536,3072]{2,1,0:T(8,128)(2,1)} %refs_9_.3, bf16[3,1152,3072]{2,1,0:T(8,128)(2,1)} %bitcast.51, ...), custom_call_target="tpu_custom_call" | custom-call | tf_op jit(solution)/shard_map/attn_in_2/pallas_call | solution.py:96
  573.2 10.1 attn_fwd.5
  583.3 117.5 %mlp_in_2.1 = (f32[2,128,3072]{2,1,0:T(8,128)}, bf16[2,8,128,3072]{3,2,1,0:T(8,128)(2,1)}, bf16[2,8,128,1536]{3,2,1,0:T(8,128)(2,1)}, f32[2,8,128,1536]{3,2,1,0:T(8,128)}) custom-call(bf16[2,8,128,384]{3,2,1,0:T(8,128)(2,1)} %bitcast.88, bf16[3,384,3072]{2,1,0:T(8,128)(2,1)} %bitcast.57, bf16[3,3072,1536]{2,1,0:T(8,128)(2,1)} %refs_1_.11, ...), custom_call_target="tpu_custom_call" | custom-call | tf_op jit(solution)/shard_map/mlp_in_2/pallas_call | solution.py:96
  700.8 118.9 %top.1 = (f32[2,128,3072]{2,1,0:T(8,128)}, f32[2,128,3072]{2,1,0:T(8,128)}, bf16[2,8,128,3072]{3,2,1,0:T(8,128)(2,1)}, bf16[2,8,128,1536]{3,2,1,0:T(8,128)(2,1)}, f32[1,1536]{1,0:T(1,128)}) custom-call(bf16[2,8,128,1536]{3,2,1,0:T(8,128)(2,1)} %get-tuple-element.93.refs_0_, bf16[3,1536,3072]{2,1,0:T(8,128)(2,1)} %refs_9_.3, bf16[3,1536,3072]{2,1,0:T(8,128)(2,1)} %refs_9_.3, ...), custom_call_target="tpu_custom_call" | custom-call | tf_op jit(solution)/shard_map/top/pallas_call | solution.py:96
  819.7 140.6 %d_mlp_2.1 = (f32[2,128,3072]{2,1,0:T(8,128)}, f32[8,3072]{1,0:T(8,128)}, bf16[2,8,128,3072]{3,2,1,0:T(8,128)(2,1)}, bf16[2,8,128,384]{3,2,1,0:T(8,128)(2,1)}, b...) custom-call(bf16[2,8,128,1536]{3,2,1,0:T(8,128)(2,1)} %get-tuple-element.97.refs_0_, ...), custom_call_target="tpu_custom_call" | custom-call | tf_op jit(solution)/shard_map/d_mlp_2/pallas_call | solution.py:96
  960.4 20.6 %attn_bwd.3 = (bf16[2,8,8,16,1152]{4,3,2,1,0:T(8,128)(2,1)}, bf16[3,3072,1536]{2,1,0:T(8,128)(2,1)}, bf16[3,1536,3072]{2,1,0:T(8,128)(2,1)}) custom-call(s32[17]{0:T(128)} %pad_add_fusion.info, bf16[2,8,8,16,1152]{4,3,2,1,0:T(8,128)(2,1)} %bitcast.83, bf16[2,8,8,16,384]{4,3,2,1,0:T(8,128)(2,1)} %bitcast.107, bf16[1536,3072]{1,0:T(8,128)(2,1)} %get-tuple-element.102.refs_0_, ...), custom_call_target="tpu_custom_call" | custom-call | tf_op jit(solution)/shard_map/attn_bwd/pallas_call | solution.py:848
  980.9 132.0 %d_attn_2.1 = (f32[2,128,3072]{2,1,0:T(8,128)}, f32[8,3072]{1,0:T(8,128)}, bf16[2,8,128,3072]{3,2,1,0:T(8,128)(2,1)}, bf16[2,8,128,1536]{3,2,1,0:T(8,128)(2,1)},...) custom-call(bf16[2,8,128,1152]{3,2,1,0:T(8,128)(2,1)} %bitcast.76, ...), custom_call_target="tpu_custom_call" | custom-call | tf_op jit(solution)/shard_map/d_attn_2/pallas_call | solution.py:96
  1113.0 139.1 %d_mlp_1.1 = (f32[2,128,3072]{2,1,0:T(8,128)}, f32[8,3072]{1,0:T(8,128)}, bf16[2,8,128,3072]{3,2,1,0:T(8,128)(2,1)}, bf16[2,8,128,384]{3,2,1,0:T(8,128)(2,1)}, b...) custom-call(bf16[2,8,128,1536]{3,2,1,0:T(8,128)(2,1)} %get-tuple-element.109.refs_0_, ...), custom_call_target="tpu_custom_call" | custom-call | tf_op jit(solution)/shard_map/d_mlp_1/pallas_call | solution.py:96
  1252.1 23.3 %attn_bwd.4 = (bf16[2,8,8,16,1152]{4,3,2,1,0:T(8,128)(2,1)}, bf16[3,1152,3072]{2,1,0:T(8,128)(2,1)}, bf16[3,384,3072]{2,1,0:T(8,128)(2,1)}, bf16[3,3072,1536]{2,1,0:T(8,128)(2,1)}, bf16[3,1536,3072]{2,1,0:T(8,128)(2,1)}) custom-call(s32[17]{0:T(128)} %pad_add_fusion.info, ...), custom_call_target="tpu_custom_call", output_to_operand_aliasing={{3}: (7, {}), {4}: (8, {})} | custom-call | tf_op jit(solution)/shard_map/attn_bwd/pallas_call | solution.py:848
  1275.4 129.4 %d_attn_1.1 = (f32[2,128,3072]{2,1,0:T(8,128)}, f32[8,3072]{1,0:T(8,128)}, bf16[2,8,128,3072]{3,2,1,0:T(8,128)(2,1)}, bf16[2,8,128,1536]{3,2,1,0:T(8,128)(2,1)},...) custom-call(bf16[2,8,128,1152]{3,2,1,0:T(8,128)(2,1)} %bitcast.72, ...), custom_call_target="tpu_custom_call" | custom-call | tf_op jit(solution)/shard_map/d_attn_1/pallas_call | solution.py:96
  1404.9 140.7 %d_mlp_0.1 = (f32[2,128,3072]{2,1,0:T(8,128)}, f32[8,3072]{1,0:T(8,128)}, bf16[2,8,128,3072]{3,2,1,0:T(8,128)(2,1)}, bf16[2,8,128,384]{3,2,1,0:T(8,128)(2,1)}, b...) custom-call(bf16[2,8,128,1536]{3,2,1,0:T(8,128)(2,1)} %get-tuple-element.125.refs_0_, ...), custom_call_target="tpu_custom_call" | custom-call | tf_op jit(solution)/shard_map/d_mlp_0/pallas_call | solution.py:96
  1545.5 23.6 %attn_bwd.5 = (bf16[2,8,8,16,1152]{4,3,2,1,0:T(8,128)(2,1)}, bf16[3,1152,3072]{2,1,0:T(8,128)(2,1)}, bf16[3,384,3072]{2,1,0:T(8,128)(2,1)}, bf16[3,3072,1536]{2,1,0:T(8,128)(2,1)}, bf16[3,1536,3072]{2,1,0:T(8,128)(2,1)}) custom-call(s32[17]{0:T(128)} %pad_add_fusion.info, ...), custom_call_target="tpu_custom_call", output_to_operand_aliasing={{1}: (7, {}), {2}: (8, {}), {3}: (9, {}), {4}: (10, {})} | custom-call | tf_op jit(solution)/shard_map/attn_bwd/pallas_call | solution.py:848
  1569.1 78.2 %d_attn_0.1 = (f32[2,128,3072]{2,1,0:T(8,128)}, f32[8,3072]{1,0:T(8,128)}, bf16[384,3072]{1,0:T(8,128)(2,1)}, bf16[1152,3072]{1,0:T(8,128)(2,1)}) custom-call(bf16[2,8,128,1152]{3,2,1,0:T(8,128)(2,1)} %bitcast.74, bf16[3,1152,3072]{2,1,0:T(8,128)(2,1)} %bitcast.54, f32[2,128,3072]{2,1,0:T(8,128)} %bitcast.64, f32[2,128,3072]{2,1,0:T(8,128)} %get-tuple-element.139.refs_3_, ...), custom_call_target="tpu_custom_call" | custom-call | tf_op jit(solution)/shard_map/d_attn_0/pallas_call | solution.py:96
  1647.3 15.1 sum_rows.1
  1662.4 7.5 put_last.1
  1670.6 4.2 copy.36
  1674.8 1.7 copy.37
  (12 shorter events, 1.4 us)
Async XLA Ops:
  1662.4 7.6 copy-start.2
  1662.4 7.6 copy-start.3
  1662.4 7.6 copy-start.4
  1669.9 4.9 copy-start
  1669.9 6.6 copy-start.1

commit v3 on v2

--- a/solution.py
+++ b/solution.py
@@ -105,7 +105,7 @@
     return SimpleNamespace(**dict(zip(names[1], res)))
 
 
-def fused(name, cid, kind, norm, arrays, vec, rs=None, ag=None, fills=(), plan=()):
+def fused(name, cid, kind, norm, arrays, vec, rs=None, ag=None, fills=(), bm=BM, flat_t=False, plan=()):
     ins, outs, sc = SimpleNamespace(**arrays), SimpleNamespace(), SimpleNamespace()
     dma = pltpu.SemaphoreType.DMA
     n_in = len([k for k in arrays if k in ("in0", "in1")])
@@ -161,20 +161,26 @@
         sc.res_st = pltpu.VMEM(pairs_of, BF)
         sc.res_sem = dma((TWO,))
         if what == UP:
-            outs.pre = jax.ShapeDtypeStruct((TWO, PEERS, ROWS, n2), F32)
+            outs.slope = jax.ShapeDtypeStruct((TWO, PEERS, ROWS, n2), F32)
+            outs.full_t = jax.ShapeDtypeStruct((D, TOK), BF)
+            outs.res_t = jax.ShapeDtypeStruct((n2, TOK), BF)
+            sc.full_ts = pltpu.VMEM((D, KT), BF)
+            sc.res_ts = pltpu.VMEM((n2, KT), BF)
+            sc.t_sem = dma((TWO,))
         if what == DACT:
             outs.bup = jax.ShapeDtypeStruct((1, n2), F32)
             sc.bacc = pltpu.VMEM((SUBL, n2), F32)
         if what in (UP, DACT):
-            sc.pre_st = pltpu.VMEM(pairs_of, F32)
-            sc.pre_sem = dma((TWO,))
+            sc.slope_st = pltpu.VMEM(pairs_of, F32)
+            sc.slope_sem = dma((TWO,))
     if fills:
-        sub_most = max(f[2] for f in fills)
-        sc.f_lhs = pltpu.VMEM((TOK, BM), BF)
-        sc.f_at = pltpu.VMEM((sub_most, BM, TOK), BF)
+        slots = TWO if flat_t else max(f[2] for f in fills)
+        sc.f_at = pltpu.VMEM((slots, bm, TOK), BF)
         sc.f_rhs = pltpu.VMEM((TWO, TOK, BN), BF)
-        sc.f_out = pltpu.VMEM((TWO, BM, BN), BF)
-        sc.fl_sem = dma
+        sc.f_out = pltpu.VMEM((TWO, bm, BN), BF)
+        if not flat_t:
+            sc.f_lhs = pltpu.VMEM((TOK, bm), BF)
+        sc.fl_sem = dma((slots,))
         sc.fr_sem = dma((TWO,))
         sc.fo_sem = dma((TWO,))
         outs.g0 = jax.ShapeDtypeStruct(fills[0][:2], BF)
@@ -415,7 +421,7 @@
                 pair = pl.ds(TWO * q, TWO)
                 loads = []
                 if what == DACT:
-                    loads.append(begin(r.pre.at[h, pair], r.pre_st.at[s], r.pre_sem.at[s]))
+                    loads.append(begin(r.slope.at[h, pair], r.slope_st.at[s], r.slope_sem.at[s]))
                 if q == OWN:
                     g_copy.pop(h).wait()
                     ag_copy[h, G_CORE].wait_recv()
@@ -426,6 +432,20 @@
                 else:
                     loads.append(begin(full.at[h, pair], r.agin.at[s], r.agin_sem.at[s]))
                 ready_loads[h, q] = (s, loads)
+
+            flipped = {}
+
+            def flip(src, stage, dst, i):
+                if i in flipped:
+                    flipped[i].wait()
+
+                def block(k, carry):
+                    at = pl.ds(pl.multiple_of(k * KT, KT), KT)
+                    stage[at, :] = src[:, :, at].reshape(KT, KT).T
+                    return carry
+
+                lax.fori_loop(0, stage.shape[0] // KT, block, 0)
+                flipped[i] = begin(stage, dst, r.t_sem.at[i])
 
             def product(h, q):
                 if (h, q) not in ready_loads:
@@ -448,13 +468,12 @@
                     y = dims(x, r.w2[:, at], 1, 0) if what == UP else dims(x, r.w2[at, :], 1, 1)
                     if what == UP:
                         u = y + r.b_up[pl.ds(ag[1], 1), at]
-                        r.pre_st[s, :, :, at] = u.reshape(TWO, ROWS, nt)
-                        y = u * (HALF * (ONE + jnp.tanh(GELU_C * (u + GELU_D * (u * u * u)))))
+                        t = jnp.tanh(GELU_C * (u + GELU_D * (u * u * u)))
+                        slope = HALF * (ONE + t) + (HALF * GELU_C) * u * (ONE - t * t) * (ONE + (3 * GELU_D) * (u * u))
+                        r.slope_st[s, :, :, at] = slope.reshape(TWO, ROWS, nt)
+                        y = u * (HALF * (ONE + t))
                     if what == DACT:
-                        u = r.pre_st[s, :, :, at].reshape(TWO * ROWS, nt)
-                        y = y.astype(BF).astype(F32)
-                        t = jnp.tanh(GELU_C * (u + GELU_D * (u * u * u)))
-                        y = y * (HALF * (ONE + t) + (HALF * GELU_C) * u * (ONE - t * t) * (ONE + (3 * GELU_D) * (u * u)))
+                        y = y.astype(BF).astype(F32) * r.slope_st[s, :, :, at].reshape(TWO * ROWS, nt)
                         r.bacc[:, at] += jnp.sum(y.reshape(-1, SUBL, nt), axis=0)
                     r.res_st[s, :, :, at] = y.astype(BF).reshape(TWO, ROWS, nt)
                     return carry
@@ -465,15 +484,23 @@
                     lax.fori_loop(0, n2 // nt, tile, 0)
                 res_out[s] = [begin(r.res_st.at[s], r.res.at[h, pair], r.res_sem.at[s])]
                 if what == UP:
-                    res_out[s].append(begin(r.pre_st.at[s], r.pre.at[h, pair], r.pre_sem.at[s]))
+                    res_out[s].append(begin(r.slope_st.at[s], r.slope.at[h, pair], r.slope_sem.at[s]))
+                    cols = pl.ds((h * PEERS + TWO * q) * ROWS, KT)
+                    gathered = r.last if (h, q) == (B, FAR) else r.agin.at[s]
+                    flip(gathered, r.full_ts, r.full_t.at[:, cols], 0)
+                    flip(r.res_st.at[s], r.res_ts, r.res_t.at[:, cols], 1)
 
         jobs = []
         if fills:
             refs = ((r.f0l, r.f0r, r.g0), (r.f1l, r.f1r, r.g1))
-            jobs = [SimpleNamespace(lhs=f[0], rhs=f[1], out=f[2], blocks=c[0] // BM // c[2], tiles=c[1] // BN, sub=c[2], done=0) for f, c in zip(refs, fills)]
+            jobs = [SimpleNamespace(lhs=f[0], rhs=f[1], out=f[2], blocks=c[0] // bm // c[2], tiles=c[1] // BN, sub=c[2], done=0) for f, c in zip(refs, fills)]
 
         def lhs_copy(j, k):
-            return Pieces(j.lhs.at[:, pl.ds(pl.multiple_of(k * BM, BM), BM)], r.f_lhs, r.fl_sem, PEERS)
+            at = pl.ds(pl.multiple_of(k * bm, bm), bm)
+            if flat_t:
+                s = lax.rem(k, TWO)
+                return Pieces(j.lhs.at[at], r.f_at.at[s], r.fl_sem.at[s], PEERS)
+            return Pieces(j.lhs.at[:, at], r.f_lhs, r.fl_sem.at[0], PEERS)
 
         def rhs_copy(j, v):
             s = lax.rem(v, TWO)
@@ -482,11 +509,13 @@
         def put_copy(j, u):
             s, v = lax.rem(u, TWO), lax.div(u, j.sub)
             row = lax.div(v, j.tiles) * j.sub + lax.rem(u, j.sub)
-            dst = j.out.at[pl.ds(pl.multiple_of(row * BM, BM), BM), pl.ds(pl.multiple_of(lax.rem(v, j.tiles) * BN, BN), BN)]
+            dst = j.out.at[pl.ds(pl.multiple_of(row * bm, bm), bm), pl.ds(pl.multiple_of(lax.rem(v, j.tiles) * BN, BN), BN)]
             return Pieces(r.f_out.at[s], dst, r.fo_sem.at[s], 3)
 
         def job_begin(j):
             lhs_copy(j, jnp.int32(0)).start()
+            if flat_t:
+                lhs_copy(j, jnp.int32(1)).start()
             rhs_copy(j, jnp.int32(0)).start()
 
         def fill(n):
@@ -503,6 +532,8 @@
                     @pl.when(t == 0)
                     def _():
                         lhs_copy(j, k).wait()
+                        if flat_t:
+                            return
                         for i in range(TOK // KT):
                             r.f_at[b, :, i * KT : (i + 1) * KT] = r.f_lhs[i * KT : (i + 1) * KT, :].T
 
@@ -522,8 +553,14 @@
                     def _():
                         put_copy(j, u - TWO).wait()
 
-                    r.f_out[s] = dims(r.f_at[b], r.f_rhs[vs], 1, 0).astype(BF)
+                    r.f_out[s] = dims(r.f_at[lax.rem(k, TWO) if flat_t else b], r.f_rhs[vs], 1, 0).astype(BF)
                     put_copy(j, u).start()
+                    if flat_t:
+
+                        @pl.when((t == j.tiles - 1) & (k + TWO < j.blocks * j.sub))
+                        def _():
+                            lhs_copy(j, k + TWO).start()
+
                     return carry
 
                 upto = min(count, j.done + n)
@@ -624,10 +661,12 @@
             product(B, OWN)
             fill_next()
             products(A)
-            fill(ALL)
+            fill_next()
             product(A, FAR)
             forward(B)
+            fill_next()
             products(B)
+            fill(ALL)
             product(B, FAR)
         elif kind == TOP:
             for c in srcs:
@@ -700,7 +739,7 @@
             for cs in res_out.values():
                 for c in cs:
                     c.wait()
-            for c in last_copy:
+            for c in last_copy + list(flipped.values()):
                 c.wait()
 
     return call(name, cid, body, ins, outs, sc, ("vec", "b_up", "vo", "bup"))
@@ -793,15 +832,18 @@
     return out.reshape(TWO, PEERS, ROWS, INNER)
 
 
-def stacking(puts, stacks, n):
+def stacking(puts, stacks):
     used = sorted({p[1] for p in puts})
-    shapes = [jax.ShapeDtypeStruct((n,) + next(p[0].shape for p in puts if p[1] == k), BF) for k in used]
+    first = [next(p for p in puts if p[1] == k) for k in used]
+    shapes = [jax.ShapeDtypeStruct((p[3],) + p[0].shape, p[0].dtype) for p in first]
     given = [k for k in used if stacks[k] is not None]
-    return used, shapes, given
-
-
-def attn_bwd(info, qkv, dctx, puts, stacks, n, group):
-    used, shapes, given = stacking(puts, stacks, n)
+    dma = pltpu.SemaphoreType.DMA
+    scratch = [pltpu.VMEM(p[0].shape, p[0].dtype) for p in puts] + [dma((len(puts),)), dma((len(puts),))]
+    return used, shapes, given, scratch
+
+
+def attn_bwd(info, qkv, dctx, puts, stacks, group):
+    used, shapes, given, scratch = stacking(puts, stacks)
     m = len(puts)
 
     def kernel(info, qkv, dctx, *refs):
@@ -837,13 +879,12 @@
                 put(i).wait()
 
     hbm = pl.BlockSpec(memory_space=ANY)
-    dma = pltpu.SemaphoreType.DMA
     grid_spec = pltpu.PrefetchScalarGridSpec(
         num_scalar_prefetch=1,
         grid=(ALL_SEQS // SEQS,),
         in_specs=[seq_spec(QKV_N), seq_spec(INNER)] + [hbm] * (m + len(given)),
         out_specs=[seq_spec(QKV_N)] + [hbm] * len(used),
-        scratch_shapes=[pltpu.VMEM(p[0].shape, BF) for p in puts] + [dma((m,)), dma((m,))] + attn_tiles(group, F32, BF, BF, BF),
+        scratch_shapes=scratch + attn_tiles(group, F32, BF, BF, BF),
     )
     res = pl.pallas_call(
         kernel,
@@ -859,34 +900,34 @@
 
 
 def put_last(puts, stacks):
+    used, shapes, given, scratch = stacking(puts, stacks)
     m = len(puts)
 
     def kernel(*refs):
-        grads, outs, refs = refs[:m], refs[m + m : m + m + m], refs[m + m + m :]
+        grads, refs = refs[:m], refs[m + len(given) :]
+        outs, refs = refs[: len(used)], refs[len(used) :]
         bounce, load_sem, put_sem = refs[:m], refs[m], refs[m + 1]
         loads = [Pieces(grads[i], bounce[i], load_sem.at[i], PEERS).start() for i in range(m)]
         stores = []
-        for i in range(m):
+        for i, p in enumerate(puts):
             loads[i].wait()
-            stores.append(Pieces(bounce[i], outs[i].at[puts[i][TWO]], put_sem.at[i], PEERS).start())
+            stores.append(Pieces(bounce[i], outs[used.index(p[1])].at[p[TWO]], put_sem.at[i], PEERS).start())
         for c in stores:
             c.wait()
 
     hbm = pl.BlockSpec(memory_space=ANY)
-    dma = pltpu.SemaphoreType.DMA
-    olds = [stacks[p[1]] for p in puts]
     res = pl.pallas_call(
         kernel,
         name="put_last",
-        out_shape=[jax.ShapeDtypeStruct(a.shape, a.dtype) for a in olds],
-        in_specs=[hbm] * (m + m),
-        out_specs=[hbm] * m,
-        scratch_shapes=[pltpu.VMEM(p[0].shape, BF) for p in puts] + [dma((m,)), dma((m,))],
-        input_output_aliases={m + i: i for i in range(m)},
+        out_shape=shapes,
+        in_specs=[hbm] * (m + len(given)),
+        out_specs=[hbm] * len(used),
+        scratch_shapes=scratch,
+        input_output_aliases={m + j: used.index(k) for j, k in enumerate(given)},
         compiler_params=pltpu.CompilerParams(vmem_limit_bytes=VMEM_LIMIT),
-    )(*[p[0] for p in puts], *olds)
-    for p, a in zip(puts, res):
-        stacks[p[1]] = a
+    )(*[p[0] for p in puts], *[stacks[k] for k in given])
+    for k, a in zip(used, res):
+        stacks[k] = a
 
 
 def sum_rows(parts, cid):
@@ -954,55 +995,53 @@
         return SimpleNamespace(gain=(layer, i), shift=(layer, i + 1), bias=bias)
 
     ln2, bias1, bias2 = TWO, 4, 5
-    groups = (TWO, 1, 4)
     saved = [SimpleNamespace() for _ in range(n)]
     r = fused("first", next(ids), FIRST, N_FIRST, dict(in0=x, wb=wq, vec=vec), row(0, 0), ag=(QKV, 0))
     s = saved[0]
     s.x, s.a, s.qkv = x, r.full, r.res
     for l in range(n):
         s = saved[l]
-        s.ctx = attn_fwd(info, s.qkv, groups[l])
+        s.ctx = attn_fwd(info, s.qkv, SEQS)
         arrays = dict(lhs1=s.ctx, wa=wo, wb=wup, in0=s.x, vec=vec, b_up=bup)
         r = fused(f"mlp_in_{l}", next(ids), MID, N_LN, arrays, row(l, ln2, (l, bias1)), rs=(l, INNER, False), ag=(UP, l))
-        s.hid, s.m, s.act, s.pre = r.out0, r.full, r.res, r.pre
+        s.hid, s.act, s.slope, s.m_t, s.act_t = r.out0, r.res, r.slope, r.full_t, r.res_t
         if l + 1 < n:
             arrays = dict(lhs1=s.act, wa=wdown, wb=wq, in0=s.hid, vec=vec)
             r = fused(f"attn_in_{l + 1}", next(ids), MID, N_LN, arrays, row(l + 1, 0, (l, bias2)), rs=(l, FF, False), ag=(QKV, l + 1))
             s = saved[l + 1]
             s.x, s.a, s.qkv = r.out0, r.full, r.res
     s = saved[n - 1]
-    arrays = dict(lhs1=s.act, wa=wdown, wb=wdown, in0=s.hid, vec=vec, src=dy, pre=s.pre)
+    arrays = dict(lhs1=s.act, wa=wdown, wb=wdown, in0=s.hid, vec=vec, src=dy, slope=s.slope)
     r = fused("top", next(ids), TOP, N_RES, arrays, row(0, 0, (n - 1, bias2)), rs=(n - 1, FF, False), ag=(DACT, n - 1))
     y, d_cur, d_full, d_pre = r.out0, r.out1, r.full, r.res
-    g_bup, rows, puts, stacks = [r.bup], [], [], [None] * 4
-    mlp_plans = ((10, 5, 0, 15, 5, 0, 6, 1, 5), (6, 3, 0, 10, 3, 0, 4, 1, 4), (8, 4, 0, 13, 4, 0, 5, 1, 5))
-    attn_plans = ((6, 4), (4, 3, 0, 6, 2, 0, 1, 1, 2), (6, 4, 0, 8, 3, 0, 1, 1))
-    groups = (4, TWO, 1)
+    g_bup, rows, puts, stacks = [r.bup], [], [(y.reshape(KT, D), 4, 0, 1)], [None] * 6
+    mlp_plans = ((3, 2, 0, 6, 2, 0, 2, 0, 2, 2, 3, 0, 2), (2, 1, 0, 4, 1, 0, 2, 0, 2, 3, 4, 1, 2), (3, 1, 0, 5, 1, 0, 2, 0, 2, 2, 3, 0, 2))
+    attn_plans = ((4, 3), (2, 1, 0, 4, 1, 0, 1, 1, 2, 2, 4, 1, 2), (3, 2, 0, 5, 1, 0, 1, 1, 1, 1, 3, 1, 2))
     for l in reversed(range(n)):
         s = saved[l]
-        arrays = dict(lhs1=d_pre, wa=wup, wb=wo, in0=s.hid, in1=d_cur, vec=vec, f0l=flat(s.act), f0r=flat(d_full), f1l=flat(s.m), f1r=flat(d_pre))
-        fills = ((FF, D, 4), (D, FF, 4))
-        r = fused(f"d_mlp_{l}", next(ids), MID, N_BWD2, arrays, row(l, ln2), rs=(l, FF, True), ag=(DCTX, l), fills=fills, plan=mlp_plans[l])
+        arrays = dict(lhs1=d_pre, wa=wup, wb=wo, in0=s.hid, in1=d_cur, vec=vec, f0l=s.act_t, f0r=flat(d_full), f1l=s.m_t, f1r=flat(d_pre))
+        common = dict(fills=((FF, D, TWO), (D, FF, 1)), bm=BM + BM, flat_t=True, plan=mlp_plans[l])
+        r = fused(f"d_mlp_{l}", next(ids), MID, N_BWD2, arrays, row(l, ln2), rs=(l, FF, True), ag=(DCTX, l), **common)
         d_hid, d_attn, v3 = r.out0, r.full, r.vo
-        puts += [(r.g0, 3, l), (r.g1, 2, l)]
-        d_qkv = attn_bwd(info, s.qkv, r.res, puts, stacks, n, groups[l])
+        puts += [(r.g0, 3, l, n), (r.g1, TWO, l, n)]
+        d_qkv = attn_bwd(info, s.qkv, r.res, puts, stacks, TWO if l else 1)
         arrays = dict(lhs1=d_qkv, wa=wq, in0=s.x, in1=d_hid, vec=vec, f0l=flat(s.ctx), f0r=flat(d_attn), f1l=flat(d_qkv), f1r=flat(s.a))
         common = dict(rs=(l, QKV_N, False), fills=((INNER, D, 1), (QKV_N, D, 3)), plan=attn_plans[l])
         if l:
-            arrays.update(wb=wdown, pre=saved[l - 1].pre)
+            arrays.update(wb=wdown, slope=saved[l - 1].slope)
             r = fused(f"d_attn_{l}", next(ids), MID, N_BWD1, arrays, row(l, 0), ag=(DACT, l - 1), **common)
             g_bup.append(r.bup)
             d_full, d_pre = r.full, r.res
         else:
             r = fused(f"d_attn_{l}", next(ids), LAST, N_BWD1, arrays, row(l, 0), **common)
-        puts = [(r.g0, 1, l), (r.g1, 0, l)]
+        puts = [(r.g0, 1, l, n), (r.g1, 0, l, n)]
         rows.append((r.vo, v3))
         d_cur = r.out0
-    put_last(puts, stacks)
+    put_last(puts + [(d_cur.reshape(KT, D), 5, 0, 1)], stacks)
     g_vec = sum_rows(rows[::-1], next(ids))
     g_qkv = jnp.transpose(stacks[0].reshape(n, 3, HEADS, HD, D), (0, 4, 1, 2, 3))
     g_out = stacks[1].reshape(n, HEADS, HD, D)
-    return y.reshape(shape), d_cur.reshape(shape), g_qkv, g_out, stacks[2], jnp.concatenate(g_bup[::-1]), stacks[3], g_vec
+    return stacks[4].reshape(shape), stacks[5].reshape(shape), g_qkv, g_out, stacks[2], jnp.concatenate(g_bup[::-1]), stacks[3], g_vec
 
 
 def solution(mesh):

time: 1690 us -> 1650 us (0.976)
  Pallas kernels: 1670 us -> 1630 us
    pallas_call x14, Pallas kernels: 1550 us -> 1530 us  [call(): pl.pallas_call(kernel, name=name, out_shape=list(vars(outs).values()), in...]
where the time goes in v3:
time: 1650 us; the launch traced here: 1640 us
  Pallas kernels  1630 us (99%)
    pallas_call x14, Pallas kernels, call(): pl.pallas_call(kernel, name=name, out_shape=list(vars(outs).values()), in...  1530 us
    pallas_call x3, Pallas kernels, attn_bwd(): pl.pallas_call(kernel, name='attn_bwd', out_shape=[seq_shape(QKV_N)] + sh...  66.8 us

profile of v3, /device:TPU:0, one launch (start us, length us, event | category | flops | bytes accessed | tf_op | source)
XLA Modules:
  0.0 1638.0 jit_solution(5003819844038566881)
XLA Ops:
  0.6 1.2 pad_add_fusion.info
  1.9 69.0 %first.1 = (bf16[2,8,128,3072]{3,2,1,0:T(8,128)(2,1)}, bf16[2,8,128,1152]{3,2,1,0:T(8,128)(2,1)}) custom-call(f32[2,128,3072]{2,1,0:T(8,128)} %bitcast.58, bf16[3,1152,3072]{2,1,0:T(8,128)(2,1)} %bitcast.45, f32[3,6,3072]{2,1,0:T(8,128)} %refs_4_.17), custom_call_target="tpu_custom_call" | custom-call | tf_op jit(solution)/shard_map/first/pallas_call | solution.py:96
  70.9 10.0 attn_fwd.3
  80.9 122.0 %mlp_in_0.1 = (f32[2,128,3072]{2,1,0:T(8,128)}, bf16[2,8,128,3072]{3,2,1,0:T(8,128)(2,1)}, bf16[2,8,128,1536]{3,2,1,0:T(8,128)(2,1)}, f32[2,8,128,1536]{3,2,1,0:...) custom-call(bf16[2,8,128,384]{3,2,1,0:T(8,128)(2,1)} %bitcast.77, bf16[3,384,3072]{2,1,0:T(8,128)(2,1)} %bitcast.51, ...), custom_call_target="tpu_custom_call" | custom-call | tf_op jit(solution)/shard_map/mlp_in_0/pallas_call | solution.py:96
  202.9 120.5 %attn_in_1.1 = (f32[2,128,3072]{2,1,0:T(8,128)}, bf16[2,8,128,3072]{3,2,1,0:T(8,128)(2,1)}, bf16[2,8,128,1152]{3,2,1,0:T(8,128)(2,1)}) custom-call(bf16[2,8,128,1536]{3,2,1,0:T(8,128)(2,1)} %get-tuple-element.90.refs_0_, bf16[3,1536,3072]{2,1,0:T(8,128)(2,1)} %refs_9_.3, bf16[3,1152,3072]{2,1,0:T(8,128)(2,1)} %bitcast.46, ...), custom_call_target="tpu_custom_call" | custom-call | tf_op jit(solution)/shard_map/attn_in_1/pallas_call | solution.py:96
  323.4 10.1 attn_fwd.4
  333.4 123.1 %mlp_in_1.1 = (f32[2,128,3072]{2,1,0:T(8,128)}, bf16[2,8,128,3072]{3,2,1,0:T(8,128)(2,1)}, bf16[2,8,128,1536]{3,2,1,0:T(8,128)(2,1)}, f32[2,8,128,1536]{3,2,1,0:...) custom-call(bf16[2,8,128,384]{3,2,1,0:T(8,128)(2,1)} %bitcast.79, bf16[3,384,3072]{2,1,0:T(8,128)(2,1)} %bitcast.52, ...), custom_call_target="tpu_custom_call" | custom-call | tf_op jit(solution)/shard_map/mlp_in_1/pallas_call | solution.py:96
  456.5 119.2 %attn_in_2.1 = (f32[2,128,3072]{2,1,0:T(8,128)}, bf16[2,8,128,3072]{3,2,1,0:T(8,128)(2,1)}, bf16[2,8,128,1152]{3,2,1,0:T(8,128)(2,1)}) custom-call(bf16[2,8,128,1536]{3,2,1,0:T(8,128)(2,1)} %get-tuple-element.94.refs_0_, bf16[3,1536,3072]{2,1,0:T(8,128)(2,1)} %refs_9_.3, bf16[3,1152,3072]{2,1,0:T(8,128)(2,1)} %bitcast.47, ...), custom_call_target="tpu_custom_call" | custom-call | tf_op jit(solution)/shard_map/attn_in_2/pallas_call | solution.py:96
  575.8 10.1 attn_fwd.5
  585.8 123.2 %mlp_in_2.1 = (f32[2,128,3072]{2,1,0:T(8,128)}, bf16[2,8,128,3072]{3,2,1,0:T(8,128)(2,1)}, bf16[2,8,128,1536]{3,2,1,0:T(8,128)(2,1)}, f32[2,8,128,1536]{3,2,1,0:...) custom-call(bf16[2,8,128,384]{3,2,1,0:T(8,128)(2,1)} %bitcast.81, bf16[3,384,3072]{2,1,0:T(8,128)(2,1)} %bitcast.53, ...), custom_call_target="tpu_custom_call" | custom-call | tf_op jit(solution)/shard_map/mlp_in_2/pallas_call | solution.py:96
  709.0 119.0 %top.1 = (f32[2,128,3072]{2,1,0:T(8,128)}, f32[2,128,3072]{2,1,0:T(8,128)}, bf16[2,8,128,3072]{3,2,1,0:T(8,128)(2,1)}, bf16[2,8,128,1536]{3,2,1,0:T(8,128)(2,1)}, f32[1,1536]{1,0:T(1,128)}) custom-call(bf16[2,8,128,1536]{3,2,1,0:T(8,128)(2,1)} %get-tuple-element.98.refs_0_, bf16[3,1536,3072]{2,1,0:T(8,128)(2,1)} %refs_9_.3, bf16[3,1536,3072]{2,1,0:T(8,128)(2,1)} %refs_9_.3, ...), custom_call_target="tpu_custom_call" | custom-call | tf_op jit(solution)/shard_map/top/pallas_call | solution.py:96
  828.1 124.8 %d_mlp_2.1 = (f32[2,128,3072]{2,1,0:T(8,128)}, f32[8,3072]{1,0:T(8,128)}, bf16[2,8,128,3072]{3,2,1,0:T(8,128)(2,1)}, bf16[2,8,128,384]{3,2,1,0:T(8,128)(2,1)}, b...) custom-call(bf16[2,8,128,1536]{3,2,1,0:T(8,128)(2,1)} %get-tuple-element.101.refs_0_, ...), custom_call_target="tpu_custom_call" | custom-call | tf_op jit(solution)/shard_map/d_mlp_2/pallas_call | solution.py:96
  952.9 19.6 %attn_bwd.3 = (bf16[2,8,8,16,1152]{4,3,2,1,0:T(8,128)(2,1)}, bf16[3,3072,1536]{2,1,0:T(8,128)(2,1)}, bf16[3,1536,3072]{2,1,0:T(8,128)(2,1)}, f32[1,256,3072]{2,1,0:T(8,128)}) custom-call(s32[17]{0:T(128)} %pad_add_fusion.info, bf16[2,8,8,16,1152]{4,3,2,1,0:T(8,128)(2,1)} %bitcast.76, bf16[2,8,8,16,384]{4,3,2,1,0:T(8,128)(2,1)} %bitcast.97, ...), custom_call_target="tpu_custom_call" | custom-call | tf_op jit(solution)/shard_map/attn_bwd/pallas_call | solution.py:889
  972.5 128.7 %d_attn_2.1 = (f32[2,128,3072]{2,1,0:T(8,128)}, f32[8,3072]{1,0:T(8,128)}, bf16[2,8,128,3072]{3,2,1,0:T(8,128)(2,1)}, bf16[2,8,128,1536]{3,2,1,0:T(8,128)(2,1)},...) custom-call(bf16[2,8,128,1152]{3,2,1,0:T(8,128)(2,1)} %bitcast.69, ...), custom_call_target="tpu_custom_call" | custom-call | tf_op jit(solution)/shard_map/d_attn_2/pallas_call | solution.py:96
  1101.2 129.3 %d_mlp_1.1 = (f32[2,128,3072]{2,1,0:T(8,128)}, f32[8,3072]{1,0:T(8,128)}, bf16[2,8,128,3072]{3,2,1,0:T(8,128)(2,1)}, bf16[2,8,128,384]{3,2,1,0:T(8,128)(2,1)}, b...) custom-call(bf16[2,8,128,1536]{3,2,1,0:T(8,128)(2,1)} %get-tuple-element.116.refs_0_, ...), custom_call_target="tpu_custom_call" | custom-call | tf_op jit(solution)/shard_map/d_mlp_1/pallas_call | solution.py:96
  1230.5 23.7 %attn_bwd.4 = (bf16[2,8,8,16,1152]{4,3,2,1,0:T(8,128)(2,1)}, bf16[3,1152,3072]{2,1,0:T(8,128)(2,1)}, bf16[3,384,3072]{2,1,0:T(8,128)(2,1)}, bf16[3,3072,1536]{2,1,0:T(8,128)(2,1)}, bf16[3,1536,3072]{2,1,0:T(8,128)(2,1)}) custom-call(s32[17]{0:T(128)} %pad_add_fusion.info, ...), custom_call_target="tpu_custom_call", output_to_operand_aliasing={{3}: (7, {}), {4}: (8, {})} | custom-call | tf_op jit(solution)/shard_map/attn_bwd/pallas_call | solution.py:889
  1254.2 127.3 %d_attn_1.1 = (f32[2,128,3072]{2,1,0:T(8,128)}, f32[8,3072]{1,0:T(8,128)}, bf16[2,8,128,3072]{3,2,1,0:T(8,128)(2,1)}, bf16[2,8,128,1536]{3,2,1,0:T(8,128)(2,1)},...) custom-call(bf16[2,8,128,1152]{3,2,1,0:T(8,128)(2,1)} %bitcast.65, ...), custom_call_target="tpu_custom_call" | custom-call | tf_op jit(solution)/shard_map/d_attn_1/pallas_call | solution.py:96
  1381.5 126.2 %d_mlp_0.1 = (f32[2,128,3072]{2,1,0:T(8,128)}, f32[8,3072]{1,0:T(8,128)}, bf16[2,8,128,3072]{3,2,1,0:T(8,128)(2,1)}, bf16[2,8,128,384]{3,2,1,0:T(8,128)(2,1)}, b...) custom-call(bf16[2,8,128,1536]{3,2,1,0:T(8,128)(2,1)} %get-tuple-element.133.refs_0_, ...), custom_call_target="tpu_custom_call" | custom-call | tf_op jit(solution)/shard_map/d_mlp_0/pallas_call | solution.py:96
  1507.6 23.5 %attn_bwd.5 = (bf16[2,8,8,16,1152]{4,3,2,1,0:T(8,128)(2,1)}, bf16[3,1152,3072]{2,1,0:T(8,128)(2,1)}, bf16[3,384,3072]{2,1,0:T(8,128)(2,1)}, bf16[3,3072,1536]{2,1,0:T(8,128)(2,1)}, bf16[3,1536,3072]{2,1,0:T(8,128)(2,1)}) custom-call(s32[17]{0:T(128)} %pad_add_fusion.info, ...), custom_call_target="tpu_custom_call", output_to_operand_aliasing={{1}: (7, {}), {2}: (8, {}), {3}: (9, {}), {4}: (10, {})} | custom-call | tf_op jit(solution)/shard_map/attn_bwd/pallas_call | solution.py:889
  1531.2 79.6 %d_attn_0.1 = (f32[2,128,3072]{2,1,0:T(8,128)}, f32[8,3072]{1,0:T(8,128)}, bf16[384,3072]{1,0:T(8,128)(2,1)}, bf16[1152,3072]{1,0:T(8,128)(2,1)}) custom-call(bf16[2,8,128,1152]{3,2,1,0:T(8,128)(2,1)} %bitcast.67, bf16[3,1152,3072]{2,1,0:T(8,128)(2,1)} %bitcast.50, f32[2,128,3072]{2,1,0:T(8,128)} %bitcast.60, f32[2,128,3072]{2,1,0:T(8,128)} %get-tuple-element.148.refs_3_, ...), custom_call_target="tpu_custom_call" | custom-call | tf_op jit(solution)/shard_map/d_attn_0/pallas_call | solution.py:96
  1610.8 16.0 sum_rows.1
  1626.8 8.4 put_last.1
  1635.2 0.6 pad_maximum_fusion
  1635.9 1.7 copy.34
  (6 shorter events, 0.0 us)
Async XLA Ops:
  1626.7 8.5 copy-start
  1626.7 8.5 copy-start.1
  1626.7 8.5 copy-start.2

commit v4 on v0

v4 whole, which is shorter than its diff:
```python
from functools import partial
from types import SimpleNamespace

import jax
import jax.numpy as jnp
from jax import lax
from jax.experimental import pallas as pl
from jax.experimental.pallas import tpu as pltpu
from jax.sharding import PartitionSpec as P

TP, DP = "tp", "dp"
D, FF, INNER, QKV_N = 3072, 1536, 384, 1152
ROWS, HALF_ROWS, GROUP = 128, 64, 16
LANES, SUBL = 128, 8
A, B = HALVES = range(2)
PEERS = 8
TOK = len(HALVES) * PEERS * ROWS
HEADS, HD = 4, 96
SEQS, ALL_SEQS = 4, 16
BM, BN, KT = 384, 512, 256
BF, F32 = jnp.bfloat16, jnp.float32
ANY = pl.ANY
VMEM_LIMIT = 66_900_000
GELU_C, GELU_D = 0.7978845608028654, 0.044715
EPS, NEG = 1e-5, -1e30
ONE, TWO, HALF = 1.0, 2, 0.5
OWN, XN, YN, FAR = PAIRS = range(4)
Q_ORDER = (FAR, XN, YN, OWN)
R_X, R_Y, R_FAR = 2, 4, 6
X_FAR, Y_FAR, X_RAW, Y_RAW, X_SUM, Y_SUM, N_RS = range(4, 11)
G_CORE, G_XT, G_XB, G_YB, G_YT, G_FT, G_FB, G_C3, G_C5, G_C7, N_AG = range(11)
CROSSING = {XN: G_C3, YN: G_C5, FAR: G_C7}
FIRST, MID, TOP, LAST = range(4)
N_FIRST, N_LN, N_RES, N_BWD2, N_BWD1 = range(5)
QKV, UP, DACT, DCTX = range(4)
WIDTH = (QKV_N, FF, FF, INNER)
ALL = 1 << 20


def dims(lhs, rhs, lc, rc):
    return lax.dot_general(lhs, rhs, (((lc,), (rc,)), ((), ())), preferred_element_type=F32)


def peers():
    me = lax.axis_index(TP)
    dp = lax.axis_index(DP)

    def flip(bit):
        return me + bit - TWO * bit * lax.rem(lax.div(me, bit), TWO)

    return [(dp, flip(1 << k)) for k in range(3)]


def say_here(devices):
    for dev in devices:
        pl.semaphore_signal(pltpu.get_barrier_semaphore(), inc=1, device_id=dev, device_id_type=pl.DeviceIdType.MESH)


def await_peers(n=3):
    pl.semaphore_wait(pltpu.get_barrier_semaphore(), n)


def remote(src, dst, send, recv, dev):
    return pltpu.make_async_remote_copy(src_ref=src, dst_ref=dst, send_sem=send, recv_sem=recv, device_id=dev, device_id_type=pl.DeviceIdType.MESH)


class Pieces:
    def __init__(self, src, dst, sem, n):
        self.src, self.dst, self.sem, self.n = src, dst, sem, n

    def start(self):
        src, dst = self.src, self.dst
        step = src.shape[-2] // self.n
        for i in range(self.n):
            at = pl.ds(i * step, step)
            if len(src.shape) == 3:
                for j in range(src.shape[0]):
                    pltpu.make_async_copy(src.at[j, at], dst.at[j, at], self.sem).start()
            else:
                pltpu.make_async_copy(src.at[at], dst.at[at], self.sem).start()
        return self

    def wait(self):
        pltpu.make_async_copy(self.src, self.dst, self.sem).wait()


def call(name, cid, body, ins, outs, scratch, small):
    names = [list(vars(a)) for a in (ins, outs, scratch)]

    def kernel(*refs):
        body(SimpleNamespace(**dict(zip(sum(names, []), refs))))

    def spec(n):
        return pl.BlockSpec(memory_space=pltpu.VMEM if n in small else ANY)

    res = pl.pallas_call(
        kernel,
        name=name,
        out_shape=list(vars(outs).values()),
        in_specs=[spec(n) for n in names[0]],
        out_specs=[spec(n) for n in names[1]],
        scratch_shapes=list(vars(scratch).values()),
        compiler_params=pltpu.CompilerParams(vmem_limit_bytes=VMEM_LIMIT, collective_id=cid, has_side_effects=True),
    )(*vars(ins).values())
    return SimpleNamespace(**dict(zip(names[1], res)))


def config(norm, arrays, vec, rs=None, ag=None, fills=(), bm=BM, flat_t=False, plan=(), taken=()):
    return SimpleNamespace(norm=norm, arrays=arrays, vec=vec, rs=rs, ag=ag, fills=fills, bm=bm, flat_t=flat_t, plan=plan, taken=dict(taken))


def declare(c):
    outs, sc = SimpleNamespace(), SimpleNamespace()
    dma = pltpu.SemaphoreType.DMA
    n_in = TWO if c.norm in (N_BWD2, N_BWD1) else 1
    n_acc = {N_BWD2: 4, N_BWD1: TWO}.get(c.norm, 0)
    shard = jax.ShapeDtypeStruct((TWO, ROWS, D), F32)
    if c.norm != N_FIRST:
        outs.out0 = shard
        sc.nout = pltpu.VMEM((ROWS, D), F32)
    if c.norm == N_RES:
        outs.out1 = shard
        sc.nout1 = pltpu.VMEM((ROWS, D), F32)
    sc.nin = pltpu.VMEM((n_in, ROWS, D), F32)
    sc.nsem = dma((n_in + TWO,))
    if n_acc:
        outs.vo = jax.ShapeDtypeStruct((SUBL, D), F32)
        sc.acc = pltpu.VMEM((n_acc, SUBL, D), F32)
    if c.rs:
        k1 = c.rs[1]
        tile1 = 1024
        tiles1 = D // tile1
        halves = (TWO, ROWS, D)
        sc.w1 = pltpu.VMEM((D, k1) if c.rs[2] else (k1, D), BF)
        sc.lhs = pltpu.VMEM((TWO, TWO, ROWS, k1), BF)
        sc.own = pltpu.VMEM((TWO, len(PAIRS), ROWS, D), BF)
        sc.snd = pltpu.VMEM((len(PAIRS), ROWS, D), BF)
        sc.drx = pltpu.VMEM((TWO, len(PAIRS), ROWS, D), BF)
        sc.hx = pltpu.VMEM((TWO, HALF_ROWS, D), BF)
        sc.hy = pltpu.VMEM((TWO, HALF_ROWS, D), BF)
        sc.rx = pltpu.VMEM(halves, BF)
        sc.ry = pltpu.VMEM(halves, BF)
        sc.w1_sem = dma((tiles1,))
        sc.lhs_sem = dma((TWO,))
        sc.rs_send = dma((TWO, N_RS))
        sc.rs_recv = dma((TWO, N_RS))
        sc.far_send = dma((tiles1, len(PAIRS)))
        sc.far_recv = dma((tiles1, len(PAIRS)))
    if c.ag:
        what = c.ag[0]
        n2 = WIDTH[what]
        outs.full = jax.ShapeDtypeStruct((TWO, PEERS, ROWS, D), BF)
        outs.res = jax.ShapeDtypeStruct((TWO, PEERS, ROWS, n2), BF)
        pairs_of = (TWO, TWO, ROWS, n2)
        sc.w2 = pltpu.VMEM((D, n2) if what == UP else (n2, D), BF)
        sc.g = pltpu.VMEM((TWO, ROWS, D), BF)
        sc.agin = pltpu.VMEM((TWO, TWO, ROWS, D), BF)
        sc.last = pltpu.VMEM((TWO, ROWS, D), BF)
        sc.w2_sem = dma
        sc.g_sem = dma((TWO,))
        sc.agin_sem = dma((TWO,))
        sc.last_sem = dma((TWO,))
        sc.ag_send = dma((TWO, N_AG))
        sc.ag_recv = dma((TWO, N_AG))
        sc.res_st = pltpu.VMEM(pairs_of, BF)
        sc.res_sem = dma((TWO,))
        if what == UP:
            outs.slope = jax.ShapeDtypeStruct((TWO, PEERS, ROWS, n2), F32)
            outs.full_t = jax.ShapeDtypeStruct((D, TOK), BF)
            outs.res_t = jax.ShapeDtypeStruct((n2, TOK), BF)
            sc.full_ts = pltpu.VMEM((D, KT), BF)
            sc.res_ts = pltpu.VMEM((n2, KT), BF)
            sc.t_sem = dma((TWO,))
        if what == DACT:
            outs.bup = jax.ShapeDtypeStruct((1, n2), F32)
            sc.bacc = pltpu.VMEM((SUBL, n2), F32)
        if what in (UP, DACT):
            sc.slope_st = pltpu.VMEM(pairs_of, F32)
            sc.slope_sem = dma((TWO,))
    if c.fills:
        slots = TWO if c.flat_t else max(f[2] for f in c.fills)
        sc.f_at = pltpu.VMEM((slots, c.bm, TOK), BF)
        sc.f_rhs = pltpu.VMEM((TWO, TOK, BN), BF)
        sc.f_out = pltpu.VMEM((TWO, c.bm, BN), BF)
        if not c.flat_t:
            sc.f_lhs = pltpu.VMEM((TOK, c.bm), BF)
        sc.fl_sem = dma((slots,))
        sc.fr_sem = dma((TWO,))
        sc.fo_sem = dma((TWO,))
        outs.g0 = jax.ShapeDtypeStruct(c.fills[0][:2], BF)
        outs.g1 = jax.ShapeDtypeStruct(c.fills[1][:2], BF)
    return outs, sc


def stage(c, r):
    norm, vec, rs, ag, fills, bm, flat_t, plan = c.norm, c.vec, c.rs, c.ag, c.fills, c.bm, c.flat_t, c.plan
    n_in = TWO if norm in (N_BWD2, N_BWD1) else 1
    n_acc = {N_BWD2: 4, N_BWD1: TWO}.get(norm, 0)
    if rs:
        k1 = rs[1]
        tile1 = 1024
        tiles1 = D // tile1
    if ag:
        what = ag[0]
        n2 = WIDTH[what]
    core, px, py = peers()
    waiting = [1] if c.first else []
    late = () if c.first else (4, 5)

    def await_once():
        while waiting:
            waiting.pop()
            await_peers()

    def begin(src, dst, sem, n=4):
        return Pieces(src, dst, sem, n).start()

    def norm_load(h):
        some = (r.in0, r.in1) if n_in == TWO else (r.in0,)
        return [begin(x.at[h], r.nin.at[i], r.nsem.at[i]) for i, x in enumerate(some)]

    def vrow(row):
        return r.vec[row[0], pl.ds(row[1], 1), :]

    out_copy = []

    def mean(x):
        return jnp.sum(x, axis=-1, keepdims=True) * (ONE / D)

    def norm_half(h, loads):
        for c in loads:
            c.wait()
        while out_copy:
            out_copy.pop().wait()

        def rows(i, carry):
            at = pl.ds(pl.multiple_of(i * GROUP, GROUP), GROUP)
            x = r.nin[0, at, :]
            if rs:
                o = r.own[h, OWN, at, :].astype(F32) + r.rx[h, at, :].astype(F32) + r.ry[h, at, :].astype(F32)
                o = o.astype(BF).astype(F32)
            if norm in (N_LN, N_RES):
                x = x + o + vrow(vec.bias)
                r.nout[at, :] = x
            if norm == N_RES:
                r.nout1[at, :] = r.g[h, at, :].astype(F32)
                return carry
            cen = x - mean(x)
            rstd = lax.rsqrt(mean(cen * cen) + EPS)
            if norm in (N_FIRST, N_LN):
                r.g[h, at, :] = (cen * rstd * vrow(vec.gain) + vrow(vec.shift)).astype(BF)
                return carry
            xh = cen * rstd
            dxh = o * vrow(vec.gain)
            base = r.nin[1, at, :]
            res = base + rstd * (dxh - mean(dxh) - xh * mean(dxh * xh))
            r.nout[at, :] = res
            if ag:
                r.g[h, at, :] = res.astype(BF)
            sums = [o * xh, o] + ([res, base] if norm == N_BWD2 else [])
            for j, v in enumerate(sums):
                r.acc[j] += v[:SUBL] + v[SUBL:]
            return carry

        lax.fori_loop(0, ROWS // GROUP, rows, 0)
        if norm != N_FIRST:
            out_copy.append(begin(r.nout, r.out0.at[h], r.nsem.at[n_in]))
        if norm == N_RES:
            out_copy.append(begin(r.nout1, r.out1.at[h], r.nsem.at[n_in + 1]))

    top, bot = pl.ds(0, HALF_ROWS), pl.ds(HALF_ROWS, HALF_ROWS)
    if rs:
        seq = [(h, q) for h in HALVES for q in Q_ORDER]
        lhs_loads, rs_copy, far_copy, w1_loads = {}, {}, {}, []
        own = r.own

        def w1_load():
            for n in range(tiles1):
                at = pl.ds(n * tile1, tile1)
                src, dst = r.wa.at[rs[0]], r.w1
                src, dst = (src.at[at], dst.at[at]) if rs[2] else (src.at[:, at], dst.at[:, at])
                w1_loads.append(begin(src, dst, r.w1_sem.at[n]))

        def lhs_load(i):
            h, q = seq[i]
            s = i % TWO
            lhs_loads[i] = begin(r.lhs1.at[h, pl.ds(TWO * q, TWO)], r.lhs.at[s], r.lhs_sem.at[s])

        def lhs_late():
            for i in late:
                lhs_load(i)

        def rs_start(h, j, src, dst, dev):
            c = remote(src, dst, r.rs_send.at[h, j], r.rs_recv.at[h, j], dev)
            c.start()
            rs_copy[h, j] = c

        def far_start(n, j, src, dst, dev):
            c = remote(src, dst, r.far_send.at[n, j], r.far_recv.at[n, j], dev)
            c.start()
            far_copy[n, j] = c

        def add_into(dst, src, n, at_cols=slice(None)):
            def rows(i, carry):
                at = pl.ds(pl.multiple_of(i * GROUP, GROUP), GROUP)
                dst[at, at_cols] = (dst[at, at_cols].astype(F32) + src[at, at_cols].astype(F32)).astype(BF)
                return carry

            lax.fori_loop(0, n // GROUP, rows, 0)

        def far_merge(n, send):
            cols = pl.ds(n * tile1, tile1)
            far_copy[n, 0].wait_recv()
            add_into(own.at[A, FAR], r.drx.at[A, FAR], ROWS, cols)
            if send:
                far_sends(n)

        def far_sends(n):
            cols = pl.ds(n * tile1, tile1)
            far_start(n, 1, own.at[A, FAR, top, cols], r.hx.at[A, :, cols], px)
            far_start(n, 2, own.at[A, FAR, bot, cols], r.hy.at[A, :, cols], py)

        def product_in(i, between=None, send=True):
            h, q = seq[i]
            s = i % TWO
            lhs_loads[i].wait()
            if i == len(PAIRS):
                for n in range(tiles1):
                    far_copy[n, 0].wait_send()
            elif h == B:
                rs_copy[A, q].wait_send()

            def tile(n, carry):
                at = pl.ds(pl.multiple_of(n * tile1, tile1), tile1)
                x = r.lhs[s].reshape(TWO * ROWS, k1)
                y = dims(x, r.w1[at, :], 1, 1) if rs[2] else dims(x, r.w1[:, at], 1, 0)
                y = y.astype(BF)
                own[h, q, :, at] = y[:ROWS]
                r.snd[q, :, at] = y[ROWS:]
                return carry

            if i == 0:
                for n in range(tiles1):
                    cols = pl.ds(n * tile1, tile1)
                    w1_loads[n].wait()
                    tile(n, 0)
                    if n == 0:
                        await_once()
                    far_start(n, 0, r.snd.at[FAR, :, cols], r.drx.at[A, FAR, :, cols], core)
                    if n:
                        far_merge(n - 1, send)
            else:
                tile(0, 0)
                if between:
                    between()
                lax.fori_loop(1, tiles1, tile, 0)
            if i + TWO < len(seq) and i + TWO not in late:
                lhs_load(i + TWO)
            if i:
                rs_start(h, q, r.snd.at[q], r.drx.at[h, q], core)

        def merge(h, q):
            rs_copy[h, q].wait_recv()
            add_into(own.at[h, q], r.drx.at[h, q], ROWS)

        def first_sends(h, q):
            if q == FAR:
                rs_start(h, X_FAR, own.at[h, q, top], r.hx.at[h], px)
                rs_start(h, Y_FAR, own.at[h, q, bot], r.hy.at[h], py)
            if q == XN:
                rs_start(h, X_RAW, own.at[h, q, top], r.rx.at[h, top], px)
            if q == YN:
                rs_start(h, Y_RAW, own.at[h, q, bot], r.ry.at[h, bot], py)

        def far_wait(h, j):
            if h == A:
                for n in range(tiles1):
                    far_copy[n, 1 + j].wait_recv()
            else:
                rs_copy[h, X_FAR + j].wait_recv()

        def third_sends(h):
            far_wait(h, 1)
            add_into(own.at[h, XN, bot], r.hy.at[h], HALF_ROWS)
            rs_start(h, X_SUM, own.at[h, XN, bot], r.rx.at[h, bot], px)
            far_wait(h, 0)
            add_into(own.at[h, YN, top], r.hx.at[h], HALF_ROWS)
            rs_start(h, Y_SUM, own.at[h, YN, top], r.ry.at[h, top], py)

        def rs_done(h):
            for j in (X_RAW, Y_RAW, X_SUM, Y_SUM):
                rs_copy[h, j].wait_recv()

        def step(i, send=True):
            def between():
                h, q = seq[i - 1]
                if i == 1:
                    far_merge(tiles1 - 1, send)
                    return
                merge(h, q)
                if send:
                    first_sends(h, q)

            product_in(i, between if i % len(PAIRS) else None, send)

    if ag:
        full = r.full
        ag_copy, g_copy, ready_loads, res_out, w2_copy, last_copy = {}, {}, {}, {}, [], []

        def w2_load():
            w2_copy.append(begin(r.wb.at[ag[1]], r.w2, r.w2_sem, PEERS))

        def ag_start(h, j, src, dst, dev):
            c = remote(src, dst, r.ag_send.at[h, j], r.ag_recv.at[h, j], dev)
            c.start()
            ag_copy[h, j] = c

        def own_sends(h):
            g = r.g
            ag_start(h, G_XT, g.at[h, top], full.at[h, R_X, top], px)
            ag_start(h, G_YB, g.at[h, bot], full.at[h, R_Y, bot], py)
            ag_start(h, G_XB, g.at[h, bot], full.at[h, R_X, bot], px)
            ag_start(h, G_YT, g.at[h, top], full.at[h, R_Y, top], py)
            ag_start(h, G_CORE, g.at[h], full.at[h, 1], core)
            g_copy[h] = begin(g.at[h], full.at[h, 0], r.g_sem.at[h])

        def far_place(h, other):
            return full.at[h, R_FAR + other] if h == A else r.last.at[other]

        def forward(h):
            ag_copy[h, G_XT].wait_recv()
            ag_start(h, G_FT, full.at[h, R_X, top], far_place(h, 0).at[top], py)
            ag_copy[h, G_YB].wait_recv()
            ag_start(h, G_FB, full.at[h, R_Y, bot], far_place(h, 0).at[bot], px)

        def cross(h):
            ag_copy[h, G_XB].wait_recv()
            ag_start(h, G_C3, full.at[h, R_X], full.at[h, R_X + 1], core)
            ag_copy[h, G_YT].wait_recv()
            ag_start(h, G_C5, full.at[h, R_Y], full.at[h, R_Y + 1], core)

        def cross_far(h):
            ag_copy[h, G_FT].wait_recv()
            ag_copy[h, G_FB].wait_recv()
            ag_start(h, G_C7, far_place(h, 0), far_place(h, 1), core)
            if h == B:
                last_copy.append(begin(r.last.at[0], full.at[h, R_FAR], r.last_sem.at[0]))

        def ready(h, q):
            s = (len(PAIRS) * h + (OWN, XN, YN, FAR).index(q)) % TWO
            pair = pl.ds(TWO * q, TWO)
            loads = []
            if what == DACT:
                loads.append(begin(r.slope.at[h, pair], r.slope_st.at[s], r.slope_sem.at[s]))
            if q == OWN:
                g_copy.pop(h).wait()
                ag_copy[h, G_CORE].wait_recv()
            else:
                ag_copy[h, CROSSING[q]].wait_recv()
            if (h, q) == (B, FAR):
                last_copy.append(begin(r.last.at[1], full.at[h, R_FAR + 1], r.last_sem.at[1]))
            else:
                loads.append(begin(full.at[h, pair], r.agin.at[s], r.agin_sem.at[s]))
            ready_loads[h, q] = (s, loads)

        flipped = {}

        def flip(src, stage, dst, i):
            if i in flipped:
                flipped[i].wait()

            def block(k, carry):
                at = pl.ds(pl.multiple_of(k * KT, KT), KT)
                stage[at, :] = src[:, :, at].reshape(KT, KT).T
                return carry

            lax.fori_loop(0, stage.shape[0] // KT, block, 0)
            flipped[i] = begin(stage, dst, r.t_sem.at[i])

        to_flip = []

        def flip_all():
            while to_flip:
                flip(*to_flip.pop(0))

        def product(h, q):
            if (h, q) not in ready_loads:
                ready(h, q)
            s, loads = ready_loads.pop((h, q))
            pair = pl.ds(TWO * q, TWO)
            while w2_copy:
                w2_copy.pop().wait()
            for c in res_out.pop(s, ()):
                c.wait()
            for c in loads:
                c.wait()
            nt = BM if what in (QKV, DCTX) else BN

            def tile(n, carry):
                at = pl.ds(pl.multiple_of(n * nt, nt), nt)
                x = r.last[...] if (h, q) == (B, FAR) else r.agin[s]
                x = x.reshape(TWO * ROWS, D)
                y = dims(x, r.w2[:, at], 1, 0) if what == UP else dims(x, r.w2[at, :], 1, 1)
                if what == UP:
                    u = y + r.b_up[pl.ds(ag[1], 1), at]
                    t = jnp.tanh(GELU_C * (u + GELU_D * (u * u * u)))
                    slope = HALF * (ONE + t) + (HALF * GELU_C) * u * (ONE - t * t) * (ONE + (3 * GELU_D) * (u * u))
                    r.slope_st[s, :, :, at] = slope.reshape(TWO, ROWS, nt)
                    y = u * (HALF * (ONE + t))
                if what == DACT:
                    y = y.astype(BF).astype(F32) * r.slope_st[s, :, :, at].reshape(TWO * ROWS, nt)
                    r.bacc[:, at] += jnp.sum(y.reshape(-1, SUBL, nt), axis=0)
                r.res_st[s, :, :, at] = y.astype(BF).reshape(TWO, ROWS, nt)
                return carry

            if n2 == nt:
                tile(0, 0)
            else:
                lax.fori_loop(0, n2 // nt, tile, 0)
            res_out[s] = [begin(r.res_st.at[s], r.res.at[h, pair], r.res_sem.at[s])]
            if what == UP:
                res_out[s].append(begin(r.slope_st.at[s], r.slope.at[h, pair], r.slope_sem.at[s]))
                cols = pl.ds((h * PEERS + TWO * q) * ROWS, KT)
                gathered = r.last if (h, q) == (B, FAR) else r.agin.at[s]
                to_flip.append((gathered, r.full_ts, r.full_t.at[:, cols], 0))
                to_flip.append((r.res_st.at[s], r.res_ts, r.res_t.at[:, cols], 1))

    jobs = []
    if fills:
        refs = ((r.f0l, r.f0r, r.g0), (r.f1l, r.f1r, r.g1))
        jobs = [SimpleNamespace(lhs=f[0], rhs=f[1], out=f[2], blocks=c[0] // bm // c[2], tiles=c[1] // BN, sub=c[2], done=0) for f, c in zip(refs, fills)]

    def lhs_copy(j, k):
        at = pl.ds(pl.multiple_of(k * bm, bm), bm)
        if flat_t:
            s = lax.rem(k, TWO)
            return Pieces(j.lhs.at[at], r.f_at.at[s], r.fl_sem.at[s], PEERS)
        return Pieces(j.lhs.at[:, at], r.f_lhs, r.fl_sem.at[0], PEERS)

    def rhs_copy(j, v):
        s = lax.rem(v, TWO)
        return Pieces(j.rhs.at[:, pl.ds(pl.multiple_of(lax.rem(v, j.tiles) * BN, BN), BN)], r.f_rhs.at[s], r.fr_sem.at[s], PEERS)

    def put_copy(j, u):
        s, v = lax.rem(u, TWO), lax.div(u, j.sub)
        row = lax.div(v, j.tiles) * j.sub + lax.rem(u, j.sub)
        dst = j.out.at[pl.ds(pl.multiple_of(row * bm, bm), bm), pl.ds(pl.multiple_of(lax.rem(v, j.tiles) * BN, BN), BN)]
        return Pieces(r.f_out.at[s], dst, r.fo_sem.at[s], 3)

    def job_begin(j):
        lhs_copy(j, jnp.int32(0)).start()
        if flat_t:
            lhs_copy(j, jnp.int32(1)).start()
        rhs_copy(j, jnp.int32(0)).start()

    def fill(n):
        while n > 0 and jobs:
            j = jobs[0]
            rhs_all = j.blocks * j.tiles
            count = rhs_all * j.sub

            def unit(u, carry):
                v, b, s = lax.div(u, j.sub), lax.rem(u, j.sub), lax.rem(u, TWO)
                vs, t = lax.rem(v, TWO), lax.rem(v, j.tiles)
                k = lax.div(v, j.tiles) * j.sub + b

                @pl.when(t == 0)
                def _():
                    lhs_copy(j, k).wait()
                    if flat_t:
                        return
                    for i in range(TOK // KT):
                        r.f_at[b, :, i * KT : (i + 1) * KT] = r.f_lhs[i * KT : (i + 1) * KT, :].T

                    @pl.when(k + 1 < j.blocks * j.sub)
                    def _():
                        lhs_copy(j, k + 1).start()

                @pl.when(b == 0)
                def _():
                    rhs_copy(j, v).wait()

                    @pl.when(v + 1 < rhs_all)
                    def _():
                        rhs_copy(j, v + 1).start()

                @pl.when(u >= TWO)
                def _():
                    put_copy(j, u - TWO).wait()

                r.f_out[s] = dims(r.f_at[lax.rem(k, TWO) if flat_t else b], r.f_rhs[vs], 1, 0).astype(BF)
                put_copy(j, u).start()
                if flat_t:

                    @pl.when((t == j.tiles - 1) & (k + TWO < j.blocks * j.sub))
                    def _():
                        lhs_copy(j, k + TWO).start()

                return carry

            upto = min(count, j.done + n)
            n -= upto - j.done
            lax.fori_loop(j.done, upto, unit, 0)
            j.done = upto
            if upto == count:
                for u in (count - TWO, count - 1):
                    put_copy(j, jnp.int32(u)).wait()
                jobs.pop(0)
                if jobs:
                    job_begin(jobs[0])

    steps = list(plan)

    def fill_next():
        if steps:
            fill(steps.pop(0))

    def prologue():
        if rs:
            lhs_load(0)
            w1_load()
            lhs_load(1)
        if ag:
            w2_load()
        if jobs:
            job_begin(jobs[0])

    def clear():
        for j in range(n_acc):
            r.acc[j] = jnp.zeros((SUBL, D), F32)
        if ag and what == DACT:
            r.bacc[...] = jnp.zeros((SUBL, n2), F32)

    def rs_sent():
        for (h, j), x in rs_copy.items():
            if h == B or j > 3:
                x.wait_send()
        for (n, j), x in far_copy.items():
            if j:
                x.wait_send()
        rs_copy.clear()
        far_copy.clear()

    def rows_out():
        while out_copy:
            out_copy.pop().wait()

    def res_done():
        for s in list(res_out):
            for x in res_out.pop(s):
                x.wait()

    def end():
        for j in range(n_acc):
            r.vo[pl.ds(j, 1), :] = jnp.sum(r.acc[j], axis=0, keepdims=True)
        if n_acc:
            r.vo[n_acc:, :] = jnp.zeros((SUBL - n_acc, D), F32)
        if ag and what == DACT:
            r.bup[...] = jnp.sum(r.bacc[...], axis=0, keepdims=True)
        rows_out()
        if rs:
            rs_sent()
        if ag:
            for x in ag_copy.values():
                x.wait_send()
            res_done()
            for x in last_copy + list(flipped.values()):
                x.wait()

    return SimpleNamespace(**locals())


SHARED = ("own", "snd", "drx", "hx", "hy", "rx", "ry", "nin", "nout", "g", "agin", "last")


def fused(name, cid, kind, *stages):
    ins, outs, scratch, small, views = SimpleNamespace(), SimpleNamespace(), SimpleNamespace(), [], []
    for i, c in enumerate(stages):
        c.first = i == 0
        c_outs, c_sc = declare(c)
        view = {}
        for group, names in ((ins, c.arrays), (outs, vars(c_outs)), (scratch, vars(c_sc))):
            for n, x in names.items():
                view[n] = f"{n}{0 if group is scratch and n in SHARED else i}"
                setattr(group, view[n], x)
                if group is not scratch and n in ("vec", "b_up", "vo", "bup"):
                    small.append(view[n])
        view.update({n: f"{prev}{i - 1}" for n, prev in c.taken.items()})
        views.append(view)
    if len(stages) > 1:
        del scratch.w10
        views[0]["w1"] = views[1]["w2"]

    def body(refs):
        refs = vars(refs)
        st = [stage(c, SimpleNamespace(**{n: refs[x] for n, x in v.items()})) for c, v in zip(stages, views)]
        if len(st) > 1:
            st[0].r.w1 = st[0].r.w1.at[pl.ds(0, stages[0].rs[1])]
        say_here(peers())
        PROGRAMS[kind](*st)

    res = call(name, cid, body, ins, outs, scratch, small)
    return [SimpleNamespace(**{n: getattr(res, x) for n, x in v.items() if hasattr(res, x) and n not in c.taken}) for c, v in zip(stages, views)]


def both_halves(s, loads):
    for i in range(len(PAIRS)):
        s.step(i)
    s.merge(A, OWN)
    s.third_sends(A)
    second_half(s, loads)


def second_half(s, loads):
    for i in range(len(PAIRS), len(s.seq)):
        s.step(i)
    s.merge(B, OWN)
    s.fill_next()
    s.rs_done(A)
    s.norm_half(A, loads)


def products(s, h):
    s.cross(h)
    s.fill_next()
    s.ready(h, XN)
    s.ready(h, YN)
    s.product(h, XN)
    if h == A:
        s.flip_all()
    s.product(h, YN)
    if h == A:
        s.flip_all()
    s.fill_next()
    s.cross_far(h)


def first_program(s):
    s.prologue()
    loads = s.norm_load(A)
    s.norm_half(A, loads)
    loads = s.norm_load(B)
    s.await_once()
    s.own_sends(A)
    s.norm_half(B, loads)
    s.product(A, OWN)
    s.forward(A)
    s.own_sends(B)
    s.ready(B, OWN)
    s.product(B, OWN)
    products(s, A)
    s.product(A, FAR)
    s.forward(B)
    products(s, B)
    s.product(B, FAR)
    s.end()


def last_program(s):
    s.prologue()
    loads = s.norm_load(A)
    s.clear()
    both_halves(s, loads)
    loads = s.norm_load(B)
    s.fill_next()
    s.third_sends(B)
    s.fill(ALL)
    s.rs_done(B)
    s.norm_half(B, loads)
    s.end()


def to_forward(s, next_loads=None):
    loads = s.norm_load(B)
    s.fill_next()
    s.third_sends(B)
    s.own_sends(A)
    s.fill_next()
    s.product(A, OWN)
    s.flip_all()
    s.fill_next()
    s.rs_done(B)
    s.norm_half(B, loads)
    if next_loads:
        next_loads()
    s.fill_next()
    s.forward(A)
    s.own_sends(B)
    s.fill_next()
    s.product(B, OWN)
    s.flip_all()
    s.fill_next()
    products(s, A)
    s.fill_next()
    s.product(A, FAR)
    s.flip_all()
    s.forward(B)


def to_end(s):
    s.fill_next()
    products(s, B)
    s.fill(ALL)
    s.flip_all()
    s.product(B, FAR)
    s.flip_all()
    s.end()


def mid_program(s, z=None):
    s.prologue()
    loads = s.norm_load(A)
    s.clear()
    both_halves(s, loads)
    if z is None:
        to_forward(s)
        to_end(s)
        return

    def next_loads():
        z.w1_load()
        z.w2_load()

    to_forward(s, next_loads)
    s.res_done()
    s.rows_out()
    s.rs_sent()
    z.lhs_load(0)
    z.lhs_load(1)
    loads = z.norm_load(A)
    z.step(0)
    z.step(1)
    s.cross(B)
    z.step(TWO)
    z.step(3)
    s.ready(B, XN)
    s.ready(B, YN)
    z.merge(A, OWN)
    s.cross_far(B)
    s.product(B, XN)
    s.product(B, YN)
    s.flip_all()
    s.product(B, FAR)
    z.third_sends(A)
    s.flip_all()
    s.res_done()
    z.lhs_late()
    for i in range(len(PAIRS), len(z.seq)):
        z.step(i)
    z.merge(B, OWN)
    z.rs_done(A)
    s.end()
    z.norm_half(A, loads)
    to_forward(z)
    to_end(z)


def top_program(s):
    s.prologue()
    loads = s.norm_load(A)
    srcs = [s.begin(s.r.src.at[h], s.r.g.at[h], s.r.g_sem.at[h]) for h in HALVES]
    s.clear()
    for x in srcs:
        x.wait()
    s.await_once()
    s.own_sends(A)
    for i in range(len(PAIRS)):
        s.step(i, False)
        if i == TWO:
            s.forward(A)
            s.own_sends(B)
    s.merge(A, OWN)
    s.product(A, OWN)
    s.ready(B, OWN)
    s.cross(A)
    s.product(B, OWN)
    s.ready(A, XN)
    s.ready(A, YN)
    s.product(A, XN)
    s.product(A, YN)
    s.forward(B)
    s.cross_far(A)
    for n in range(s.tiles1):
        s.far_sends(n)
    s.first_sends(A, XN)
    s.first_sends(A, YN)
    s.product_in(4)
    s.product(A, FAR)
    s.cross(B)
    s.step(5, False)
    s.ready(B, XN)
    s.ready(B, YN)
    s.product(B, XN)
    s.cross_far(B)
    s.product(B, YN)
    s.third_sends(A)
    s.first_sends(B, FAR)
    s.merge(B, XN)
    s.first_sends(B, XN)
    s.product_in(6)
    s.merge(B, YN)
    s.first_sends(B, YN)
    s.product_in(7)
    s.merge(B, OWN)
    s.rs_done(A)
    s.norm_half(A, loads)
    loads = s.norm_load(B)
    s.product(B, FAR)
    s.third_sends(B)
    s.rs_done(B)
    s.norm_half(B, loads)
    s.end()


PROGRAMS = (first_program, mid_program, top_program, last_program)


def positions(me):
    def pos(axis):
        i = lax.broadcasted_iota(jnp.int32, (ROWS, ROWS), axis)
        return lax.bitwise_xor(lax.div(i, GROUP), me) * GROUP + lax.rem(i, GROUP)

    return pos(0), pos(1)


def heads_of(x, part, h):
    at = part * INNER + h * HD
    return x[:, at : at + HD]


def softmax(s):
    e = jnp.exp(s - jnp.max(s, axis=-1, keepdims=True))
    return e * (ONE / jnp.sum(e, axis=-1, keepdims=True))


def attn_fwd_kernel(group, info, qkv, ctx, s_ref, p_ref):
    row, col = positions(info[ALL_SEQS])
    for first in range(0, SEQS, group):
        some = [(i, h) for i in range(first, first + group) for h in range(HEADS)]
        xs = {i: qkv[:, i].reshape(ROWS, QKV_N) for i, _ in some}
        for n, (i, h) in enumerate(some):
            mask = (col <= row) & (col < info[pl.program_id(0) * SEQS + i])
            score = dims(heads_of(xs[i], 0, h), heads_of(xs[i], 1, h), 1, 1) * HD**-HALF
            s_ref[n] = jnp.where(mask, score, NEG)
        p_ref[...] = softmax(s_ref[...]).astype(BF)
        out = {i: [] for i in xs}
        for n, (i, h) in enumerate(some):
            out[i].append(dims(p_ref[n], heads_of(xs[i], TWO, h), 1, 0).astype(BF))
        for i, parts in out.items():
            ctx[:, i] = jnp.concatenate(parts, axis=-1).reshape(PEERS, GROUP, INNER)


def attn_bwd_steps(group, info, qkv, dctx, out, s_ref, dp_ref, p_ref, ds_ref):
    row, col = positions(info[ALL_SEQS])
    for first in range(0, SEQS, group):
        some = [(i, h) for i in range(first, first + group) for h in range(HEADS)]
        xs = {i: (qkv[:, i].reshape(ROWS, QKV_N), dctx[:, i].reshape(ROWS, INNER)) for i, _ in some}
        for n, (i, h) in enumerate(some):
            x, d = xs[i]
            mask = (col <= row) & (col < info[pl.program_id(0) * SEQS + i])
            score = dims(heads_of(x, 0, h), heads_of(x, 1, h), 1, 1) * HD**-HALF
            s_ref[n] = jnp.where(mask, score, NEG)
            dp_ref[n] = dims(heads_of(d, 0, h), heads_of(x, TWO, h), 1, 1).astype(BF)
        p = softmax(s_ref[...])
        dp = dp_ref[...].astype(F32)
        p_ref[...] = p.astype(BF)
        ds = p * (dp - jnp.sum(dp * p, axis=-1, keepdims=True))
        ds_ref[...] = (ds * HD**-HALF).astype(BF)
        grads = {i: ([], [], []) for i in xs}
        for n, (i, h) in enumerate(some):
            x, d = xs[i]
            dq, dk, dv = grads[i]
            dq.append(dims(ds_ref[n], heads_of(x, 1, h), 1, 0).astype(BF))
            dk.append(dims(ds_ref[n], heads_of(x, 0, h), 0, 0).astype(BF))
            dv.append(dims(p_ref[n], heads_of(d, 0, h), 0, 0).astype(BF))
        for i, parts in grads.items():
            out[:, i] = jnp.concatenate(sum(parts, []), axis=-1).reshape(PEERS, GROUP, QKV_N)


def seq_spec(n):
    per_half = PEERS // SEQS
    return pl.BlockSpec((None, PEERS, SEQS, GROUP, n), lambda i, info: (lax.div(i, per_half), 0, lax.rem(i, per_half), 0, 0))


def by_seq(a):
    return a.reshape(TWO, PEERS, PEERS, GROUP, a.shape[-1])


def seq_shape(n):
    return jax.ShapeDtypeStruct((TWO, PEERS, PEERS, GROUP, n), BF)


def attn_tiles(group, *types):
    return [pltpu.VMEM((group * HEADS, ROWS, ROWS), t) for t in types]


def attn_fwd(info, qkv, group):
    grid_spec = pltpu.PrefetchScalarGridSpec(
        num_scalar_prefetch=1, grid=(ALL_SEQS // SEQS,), in_specs=[seq_spec(QKV_N)], out_specs=seq_spec(INNER), scratch_shapes=attn_tiles(group, F32, BF)
    )
    out = pl.pallas_call(partial(attn_fwd_kernel, group), name="attn_fwd", out_shape=seq_shape(INNER), grid_spec=grid_spec)(info, by_seq(qkv))
    return out.reshape(TWO, PEERS, ROWS, INNER)


def stacking(puts, stacks):
    used = sorted({p[1] for p in puts})
    first = [next(p for p in puts if p[1] == k) for k in used]
    shapes = [jax.ShapeDtypeStruct((p[3],) + p[0].shape, p[0].dtype) for p in first]
    given = [k for k in used if stacks[k] is not None]
    dma = pltpu.SemaphoreType.DMA
    scratch = [pltpu.VMEM(p[0].shape, p[0].dtype) for p in puts] + [dma((len(puts),)), dma((len(puts),))]
    return used, shapes, given, scratch


def attn_bwd(info, qkv, dctx, puts, stacks, group):
    used, shapes, given, scratch = stacking(puts, stacks)
    m = len(puts)

    def kernel(info, qkv, dctx, *refs):
        grads, refs = refs[:m], refs[m + len(given) :]
        out, outs, refs = refs[0], refs[1 : 1 + len(used)], refs[1 + len(used) :]
        bounce, load_sem, put_sem, tiles = refs[:m], refs[m], refs[m + 1], refs[m + TWO :]
        step = pl.program_id(0)

        def load(i):
            return Pieces(grads[i], bounce[i], load_sem.at[i], PEERS)

        def put(i):
            return Pieces(bounce[i], outs[used.index(puts[i][1])].at[puts[i][TWO]], put_sem.at[i], PEERS)

        @pl.when(step == 0)
        def _():
            for i in range(m):
                load(i).start()

        for at, some in ((1, range(m // TWO)), (TWO, range(m // TWO, m))):

            @pl.when(step == at)
            def _(some=some):
                for i in some:
                    load(i).wait()
                    put(i).start()

        attn_bwd_steps(group, info, qkv, dctx, out, *tiles)

        @pl.when(step == ALL_SEQS // SEQS - 1)
        def _():
            for i in range(m):
                put(i).wait()

    hbm = pl.BlockSpec(memory_space=ANY)
    grid_spec = pltpu.PrefetchScalarGridSpec(
        num_scalar_prefetch=1,
        grid=(ALL_SEQS // SEQS,),
        in_specs=[seq_spec(QKV_N), seq_spec(INNER)] + [hbm] * (m + len(given)),
        out_specs=[seq_spec(QKV_N)] + [hbm] * len(used),
        scratch_shapes=scratch + attn_tiles(group, F32, BF, BF, BF),
    )
    res = pl.pallas_call(
        kernel,
        name="attn_bwd",
        out_shape=[seq_shape(QKV_N)] + shapes,
        grid_spec=grid_spec,
        input_output_aliases={3 + m + j: 1 + used.index(k) for j, k in enumerate(given)},
        compiler_params=pltpu.CompilerParams(vmem_limit_bytes=VMEM_LIMIT),
    )(info, by_seq(qkv), by_seq(dctx), *[p[0] for p in puts], *[stacks[k] for k in given])
    for k, a in zip(used, res[1:]):
        stacks[k] = a
    return res[0].reshape(TWO, PEERS, ROWS, QKV_N)


def put_last(puts, stacks):
    used, shapes, given, scratch = stacking(puts, stacks)
    m = len(puts)

    def kernel(*refs):
        grads, refs = refs[:m], refs[m + len(given) :]
        outs, refs = refs[: len(used)], refs[len(used) :]
        bounce, load_sem, put_sem = refs[:m], refs[m], refs[m + 1]
        loads = [Pieces(grads[i], bounce[i], load_sem.at[i], PEERS).start() for i in range(m)]
        stores = []
        for i, p in enumerate(puts):
            loads[i].wait()
            stores.append(Pieces(bounce[i], outs[used.index(p[1])].at[p[TWO]], put_sem.at[i], PEERS).start())
        for c in stores:
            c.wait()

    hbm = pl.BlockSpec(memory_space=ANY)
    res = pl.pallas_call(
        kernel,
        name="put_last",
        out_shape=shapes,
        in_specs=[hbm] * (m + len(given)),
        out_specs=[hbm] * len(used),
        scratch_shapes=scratch,
        input_output_aliases={m + j: used.index(k) for j, k in enumerate(given)},
        compiler_params=pltpu.CompilerParams(vmem_limit_bytes=VMEM_LIMIT),
    )(*[p[0] for p in puts], *[stacks[k] for k in given])
    for k, a in zip(used, res):
        stacks[k] = a


def sum_rows(parts, cid):
    n, half = len(parts), D // TWO
    per = 6
    rows = -(-per * n // SUBL) * SUBL
    ins = SimpleNamespace()
    for l, (a, b) in enumerate(parts):
        setattr(ins, f"a{l}", a)
        setattr(ins, f"b{l}", b)

    def body(r):
        core, px, py = peers()
        say_here((core, px, py))
        odd = lax.rem(lax.axis_index(TP), TWO)
        mine = pl.ds(pl.multiple_of(odd * half, half), half)
        for l in range(n):
            at = per * l
            r.v[at : at + TWO, :] = getattr(r, f"a{l}")[:TWO, :]
            r.v[at + TWO : at + per, :] = getattr(r, f"b{l}")[: per - TWO, :]
        if rows > per * n:
            r.v[per * n :, :] = jnp.zeros((rows - per * n, D), F32)
        await_peers()

        def send(src, dst, i, dev):
            c = remote(src, dst, r.send.at[i], r.recv.at[i], dev)
            c.start()
            return c

        send(r.v, r.a, 0, core).wait()
        r.s[0] = r.v[:, mine] + r.a[:, mine]
        for i, dev in enumerate((px, py)):
            send(r.s.at[i], r.b.at[i], 1 + i, dev).wait()
            r.s[i + 1] = r.s[i] + r.b[i]
        c = send(r.s.at[TWO], r.t.at[:, mine], 3, core)
        r.u[:, mine] = r.s[TWO]
        c.wait()
        first = lax.broadcasted_iota(jnp.int32, (1, D), 1) < half
        keep = first == (odd == 0)
        for l in range(n):
            at = slice(per * l, per * (l + 1))
            r.o[l] = jnp.where(keep, r.u[at, :], r.t[at, :])

    dma = pltpu.SemaphoreType.DMA
    whole, part = pltpu.VMEM((rows, D), F32), (rows, half)
    scratch = SimpleNamespace(v=whole, a=whole, t=whole, u=whole, s=pltpu.VMEM((3,) + part, F32), b=pltpu.VMEM((TWO,) + part, F32), send=dma((4,)), recv=dma((4,)))
    outs = SimpleNamespace(o=jax.ShapeDtypeStruct((n, per, D), F32))
    return call("sum_rows", cid, body, ins, outs, scratch, list(vars(ins)) + ["o"]).o


def group_body(x_loc, dy_loc, len_loc, wqkv, wout, wup, bup, wdown, vec):
    n = wqkv.shape[0]
    ids = iter(range(ROWS))
    shape = x_loc.shape
    x = x_loc.reshape(TWO, ROWS, D)
    dy = dy_loc.reshape(TWO, ROWS, D)
    wq = jnp.transpose(wqkv, (0, 2, 3, 4, 1)).reshape(n, QKV_N, D)
    wo = wout.reshape(n, INNER, D)
    info = jnp.concatenate([len_loc, lax.axis_index(TP).reshape(1).astype(jnp.int32)])

    def flat(a):
        return a.reshape(TOK, a.shape[-1])

    def row(layer, i, bias=None):
        return SimpleNamespace(gain=(layer, i), shift=(layer, i + 1), bias=bias)

    ln2, bias1, bias2 = TWO, 4, 5
    saved = [SimpleNamespace() for _ in range(n)]
    (r,) = fused("first", next(ids), FIRST, config(N_FIRST, dict(in0=x, wb=wq, vec=vec), row(0, 0), ag=(QKV, 0)))
    s = saved[0]
    s.x, s.a, s.qkv = x, r.full, r.res
    for l in range(n):
        s = saved[l]
        s.ctx = attn_fwd(info, s.qkv, SEQS)
        arrays = dict(lhs1=s.ctx, wa=wo, wb=wup, in0=s.x, vec=vec, b_up=bup)
        stages = [config(N_LN, arrays, row(l, ln2, (l, bias1)), rs=(l, INNER, False), ag=(UP, l))]
        if l + 1 < n:
            taken = (("lhs1", "res"), ("in0", "out0"))
            arrays = dict(wa=wdown, wb=wq, vec=vec)
            stages.append(config(N_LN, arrays, row(l + 1, 0, (l, bias2)), rs=(l, FF, False), ag=(QKV, l + 1), taken=taken))
        r, *more = fused(f"fwd_{l}", next(ids), MID, *stages)
        s.hid, s.act, s.slope, s.m_t, s.act_t = r.out0, r.res, r.slope, r.full_t, r.res_t
        for r in more:
            s = saved[l + 1]
            s.x, s.a, s.qkv = r.out0, r.full, r.res
    s = saved[n - 1]
    arrays = dict(lhs1=s.act, wa=wdown, wb=wdown, in0=s.hid, vec=vec, src=dy, slope=s.slope)
    (r,) = fused("top", next(ids), TOP, config(N_RES, arrays, row(0, 0, (n - 1, bias2)), rs=(n - 1, FF, False), ag=(DACT, n - 1)))
    y, d_cur, d_full, d_pre = r.out0, r.out1, r.full, r.res
    g_bup, rows, puts, stacks = [r.bup], [], [(y.reshape(KT, D), 4, 0, 1)], [None] * 6
    mlp_plans = ((3, 1, 0, 4, 1, 0, 2, 0, 2, 2, 3, 0, 2), (3, 1, 0, 6, 1, 0, 2, 0, 2, 2, 3, 0, 2), (3, 1, 0, 5, 1, 0, 2, 0, 2, 2, 2, 0, 1))
    attn_plans = ((2, 2), (2, 1, 0, 4, 1, 0, 1, 1, 1, 1, 4, 1, 2), (4, 2, 0, 6, 2, 0, 1, 1, 1, 1, 2, 1, 1))
    for l in reversed(range(n)):
        s = saved[l]
        arrays = dict(lhs1=d_pre, wa=wup, wb=wo, in0=s.hid, in1=d_cur, vec=vec, f0l=s.act_t, f0r=flat(d_full), f1l=s.m_t, f1r=flat(d_pre))
        common = dict(fills=((FF, D, TWO), (D, FF, 1)), bm=BM + BM, flat_t=True, plan=mlp_plans[l])
        (r,) = fused(f"d_mlp_{l}", next(ids), MID, config(N_BWD2, arrays, row(l, ln2), rs=(l, FF, True), ag=(DCTX, l), **common))
        d_hid, d_attn, v3 = r.out0, r.full, r.vo
        puts += [(r.g0, 3, l, n), (r.g1, TWO, l, n)]
        d_qkv = attn_bwd(info, s.qkv, r.res, puts, stacks, TWO if l else 1)
        arrays = dict(lhs1=d_qkv, wa=wq, in0=s.x, in1=d_hid, vec=vec, f0l=flat(s.ctx), f0r=flat(d_attn), f1l=flat(d_qkv), f1r=flat(s.a))
        common = dict(rs=(l, QKV_N, False), fills=((INNER, D, 1), (QKV_N, D, 3)), plan=attn_plans[l])
        if l:
            arrays.update(wb=wdown, slope=saved[l - 1].slope)
            common.update(ag=(DACT, l - 1))
        (r,) = fused(f"d_attn_{l}", next(ids), MID if l else LAST, config(N_BWD1, arrays, row(l, 0), **common))
        if l:
            g_bup.append(r.bup)
            d_full, d_pre = r.full, r.res
        puts = [(r.g0, 1, l, n), (r.g1, 0, l, n)]
        rows.append((r.vo, v3))
        d_cur = r.out0
    put_last(puts + [(d_cur.reshape(KT, D), 5, 0, 1)], stacks)
    g_vec = sum_rows(rows[::-1], next(ids))
    g_qkv = jnp.transpose(stacks[0].reshape(n, 3, HEADS, HD, D), (0, 4, 1, 2, 3))
    g_out = stacks[1].reshape(n, HEADS, HD, D)
    return stacks[4].reshape(shape), stacks[5].reshape(shape), g_qkv, g_out, stacks[2], jnp.concatenate(g_bup[::-1]), stacks[3], g_vec


def solution(mesh):
    act_spec = P(DP, TP, None)
    in_specs = (act_spec, act_spec, P(DP), P(None, None, None, TP, None), P(None, TP, None, None), P(None, None, TP), P(None, TP), P(None, TP, None), P())
    out_specs = (act_spec, act_spec, P(DP, None, None, TP, None), P(DP, TP, None, None), P(DP, None, TP), P(DP, TP), P(DP, TP, None), P(DP, None, None))
    return jax.shard_map(group_body, mesh=mesh, in_specs=in_specs, out_specs=out_specs, check_vma=False)
```

time: 2570 us -> 1620 us (0.63)
  Pallas kernels: 0 us -> 1600 us
  waiting for transfers between devices: 1520 us -> 0 us
  matrix products: 848 us -> 0 us
  other arithmetic: 140 us -> 1.87 us
  local copies, waits for them, and re-layouts: 41.2 us -> 1.71 us
    pallas_call x0 -> x19, Pallas kernels: none -> 1600 us  [the longest x12 1500 us: call(): pl.pallas_call(kernel, name=name, out_shape=list(vars(outs).values()), in...]
    dot_general x54 -> x0, matrix products: 848 us -> none  [the longest x3 105 us: layer_bwd(): jnp.einsum('bsd,fd->bsf', d_mlp, w_down, preferred_element_type=jnp.float32)]
    reduce_scatter x12 -> x0, waiting for transfers between devices: 830 us -> none  [the longest x3 248 us: layer_fwd(): lax.psum_scatter(attn_part, TENSOR_AXIS, scatter_dimension=1, tiled=True)]
    all_gather x12 -> x0, waiting for transfers between devices: 650 us -> none  [the longest x3 202 us: layer_fwd(): a_full = lax.all_gather(a_shard, TENSOR_AXIS, axis=1, tiled=True)]
    reduce_sum x29 -> x0, other arithmetic: 57.8 us -> none  [the longest x12 29.7 us: layer_norm(): return centered * lax.rsqrt(row_var + 1e-05) * gain_vec + shift_vec]
    another operation x6 -> x0, other arithmetic: 52.6 us -> none  [group_body(): jnp.stack([grad_set[grad_pos] for grad_set in layer_grads])]
    psum x1 -> x0, waiting for transfers between devices: 37.6 us -> none  [group_body(): g_vec = lax.psum(stacked[5], TENSOR_AXIS)]
    unnamed x315 -> x7, local copies, waits for them, and re-layouts: 37 us -> 1.71 us
  transfers between devices with their start and end apart: 25 -> 0, of which waited for: 23 -> 0; matrix products, arithmetic and copies ran while one was open for 14% -> 0% of each run, Pallas kernels for 0% -> 0%
where the time goes in v4:
time: 1620 us; the launch traced here: 1610 us
  Pallas kernels  1600 us (99%)
    pallas_call x12, Pallas kernels, call(): pl.pallas_call(kernel, name=name, out_shape=list(vars(outs).values()), in...  1500 us
    pallas_call x3, Pallas kernels, attn_bwd(): pl.pallas_call(kernel, name='attn_bwd', out_shape=[seq_shape(QKV_N)] + sh...  66.4 us

profile of v4, /device:TPU:0, one launch (start us, length us, event | category | flops | bytes accessed | tf_op | source)
XLA Modules:
  0.0 1608.9 jit_solution(14839786395012585112)
XLA Ops:
  0.6 1.2 pad_add_fusion.info
  1.9 69.2 %first.1 = (bf16[2,8,128,3072]{3,2,1,0:T(8,128)(2,1)}, bf16[2,8,128,1152]{3,2,1,0:T(8,128)(2,1)}) custom-call(f32[2,128,3072]{2,1,0:T(8,128)} %bitcast.58, bf16[3,1152,3072]{2,1,0:T(8,128)(2,1)} %bitcast.45, f32[3,6,3072]{2,1,0:T(8,128)} %refs_4_.13), custom_call_target="tpu_custom_call" | custom-call | tf_op jit(solution)/shard_map/first/pallas_call | solution.py:96
  71.1 10.0 attn_fwd.3
  81.2 228.3 %fwd_0.1 = (f32[2,128,3072]{2,1,0:T(8,128)}, bf16[2,8,128,3072]{3,2,1,0:T(8,128)(2,1)}, bf16[2,8,128,1536]{3,2,1,0:T(8,128)(2,1)}, f32[2,8,128,1536]{3,2,1,0:T(8...) custom-call(bf16[2,8,128,384]{3,2,1,0:T(8,128)(2,1)} %bitcast.79, ...), custom_call_target="tpu_custom_call" | custom-call | tf_op jit(solution)/shard_map/fwd_0/pallas_call | solution.py:96
  309.5 10.1 attn_fwd.4
  319.5 228.3 %fwd_1.1 = (f32[2,128,3072]{2,1,0:T(8,128)}, bf16[2,8,128,3072]{3,2,1,0:T(8,128)(2,1)}, bf16[2,8,128,1536]{3,2,1,0:T(8,128)(2,1)}, f32[2,8,128,1536]{3,2,1,0:T(8...) custom-call(bf16[2,8,128,384]{3,2,1,0:T(8,128)(2,1)} %bitcast.81, ...), custom_call_target="tpu_custom_call" | custom-call | tf_op jit(solution)/shard_map/fwd_1/pallas_call | solution.py:96
  547.8 10.0 attn_fwd.5
  557.9 121.2 %fwd_2.1 = (f32[2,128,3072]{2,1,0:T(8,128)}, bf16[2,8,128,3072]{3,2,1,0:T(8,128)(2,1)}, bf16[2,8,128,1536]{3,2,1,0:T(8,128)(2,1)}, f32[2,8,128,1536]{3,2,1,0:T(8...) custom-call(bf16[2,8,128,384]{3,2,1,0:T(8,128)(2,1)} %bitcast.77, bf16[3,384,3072]{2,1,0:T(8,128)(2,1)} %bitcast.53, ...), custom_call_target="tpu_custom_call" | custom-call | tf_op jit(solution)/shard_map/fwd_2/pallas_call | solution.py:96
  679.1 116.4 %top.1 = (f32[2,128,3072]{2,1,0:T(8,128)}, f32[2,128,3072]{2,1,0:T(8,128)}, bf16[2,8,128,3072]{3,2,1,0:T(8,128)(2,1)}, bf16[2,8,128,1536]{3,2,1,0:T(8,128)(2,1)}, f32[1,1536]{1,0:T(1,128)}) custom-call(bf16[2,8,128,1536]{3,2,1,0:T(8,128)(2,1)} %get-tuple-element.92.refs_0_, bf16[3,1536,3072]{2,1,0:T(8,128)(2,1)} %refs_9_.3, bf16[3,1536,3072]{2,1,0:T(8,128)(2,1)} %refs_9_.3, ...), custom_call_target="tpu_custom_call" | custom-call | tf_op jit(solution)/shard_map/top/pallas_call | solution.py:96
  795.5 128.6 %d_mlp_2.1 = (f32[2,128,3072]{2,1,0:T(8,128)}, f32[8,3072]{1,0:T(8,128)}, bf16[2,8,128,3072]{3,2,1,0:T(8,128)(2,1)}, bf16[2,8,128,384]{3,2,1,0:T(8,128)(2,1)}, b...) custom-call(bf16[2,8,128,1536]{3,2,1,0:T(8,128)(2,1)} %get-tuple-element.95.refs_0_, ...), custom_call_target="tpu_custom_call" | custom-call | tf_op jit(solution)/shard_map/d_mlp_2/pallas_call | solution.py:96
  924.1 19.6 %attn_bwd.3 = (bf16[2,8,8,16,1152]{4,3,2,1,0:T(8,128)(2,1)}, bf16[3,3072,1536]{2,1,0:T(8,128)(2,1)}, bf16[3,1536,3072]{2,1,0:T(8,128)(2,1)}, f32[1,256,3072]{2,1,0:T(8,128)}) custom-call(s32[17]{0:T(128)} %pad_add_fusion.info, bf16[2,8,8,16,1152]{4,3,2,1,0:T(8,128)(2,1)} %bitcast.76, bf16[2,8,8,16,384]{4,3,2,1,0:T(8,128)(2,1)} %bitcast.97, ...), custom_call_target="tpu_custom_call" | custom-call | tf_op jit(solution)/shard_map/attn_bwd/pallas_call | solution.py:1059
  943.7 127.1 %d_attn_2.1 = (f32[2,128,3072]{2,1,0:T(8,128)}, f32[8,3072]{1,0:T(8,128)}, bf16[2,8,128,3072]{3,2,1,0:T(8,128)(2,1)}, bf16[2,8,128,1536]{3,2,1,0:T(8,128)(2,1)},...) custom-call(bf16[2,8,128,1152]{3,2,1,0:T(8,128)(2,1)} %bitcast.69, ...), custom_call_target="tpu_custom_call" | custom-call | tf_op jit(solution)/shard_map/d_attn_2/pallas_call | solution.py:96
  1070.8 126.2 %d_mlp_1.1 = (f32[2,128,3072]{2,1,0:T(8,128)}, f32[8,3072]{1,0:T(8,128)}, bf16[2,8,128,3072]{3,2,1,0:T(8,128)(2,1)}, bf16[2,8,128,384]{3,2,1,0:T(8,128)(2,1)}, b...) custom-call(bf16[2,8,128,1536]{3,2,1,0:T(8,128)(2,1)} %get-tuple-element.110.refs_0_, ...), custom_call_target="tpu_custom_call" | custom-call | tf_op jit(solution)/shard_map/d_mlp_1/pallas_call | solution.py:96
  1197.0 23.3 %attn_bwd.4 = (bf16[2,8,8,16,1152]{4,3,2,1,0:T(8,128)(2,1)}, bf16[3,1152,3072]{2,1,0:T(8,128)(2,1)}, bf16[3,384,3072]{2,1,0:T(8,128)(2,1)}, bf16[3,3072,1536]{2,1,0:T(8,128)(2,1)}, bf16[3,1536,3072]{2,1,0:T(8,128)(2,1)}) custom-call(s32[17]{0:T(128)} %pad_add_fusion.info, ...), custom_call_target="tpu_custom_call", output_to_operand_aliasing={{3}: (7, {}), {4}: (8, {})} | custom-call | tf_op jit(solution)/shard_map/attn_bwd/pallas_call | solution.py:1059
  1220.2 130.5 %d_attn_1.1 = (f32[2,128,3072]{2,1,0:T(8,128)}, f32[8,3072]{1,0:T(8,128)}, bf16[2,8,128,3072]{3,2,1,0:T(8,128)(2,1)}, bf16[2,8,128,1536]{3,2,1,0:T(8,128)(2,1)},...) custom-call(bf16[2,8,128,1152]{3,2,1,0:T(8,128)(2,1)} %bitcast.65, ...), custom_call_target="tpu_custom_call" | custom-call | tf_op jit(solution)/shard_map/d_attn_1/pallas_call | solution.py:96
  1350.8 127.7 %d_mlp_0.1 = (f32[2,128,3072]{2,1,0:T(8,128)}, f32[8,3072]{1,0:T(8,128)}, bf16[2,8,128,3072]{3,2,1,0:T(8,128)(2,1)}, bf16[2,8,128,384]{3,2,1,0:T(8,128)(2,1)}, b...) custom-call(bf16[2,8,128,1536]{3,2,1,0:T(8,128)(2,1)} %get-tuple-element.128.refs_0_, ...), custom_call_target="tpu_custom_call" | custom-call | tf_op jit(solution)/shard_map/d_mlp_0/pallas_call | solution.py:96
  1478.5 23.6 %attn_bwd.5 = (bf16[2,8,8,16,1152]{4,3,2,1,0:T(8,128)(2,1)}, bf16[3,1152,3072]{2,1,0:T(8,128)(2,1)}, bf16[3,384,3072]{2,1,0:T(8,128)(2,1)}, bf16[3,3072,1536]{2,1,0:T(8,128)(2,1)}, bf16[3,1536,3072]{2,1,0:T(8,128)(2,1)}) custom-call(s32[17]{0:T(128)} %pad_add_fusion.info, ...), custom_call_target="tpu_custom_call", output_to_operand_aliasing={{1}: (7, {}), {2}: (8, {}), {3}: (9, {}), {4}: (10, {})} | custom-call | tf_op jit(solution)/shard_map/attn_bwd/pallas_call | solution.py:1059
  1502.0 79.6 %d_attn_0.1 = (f32[2,128,3072]{2,1,0:T(8,128)}, f32[8,3072]{1,0:T(8,128)}, bf16[384,3072]{1,0:T(8,128)(2,1)}, bf16[1152,3072]{1,0:T(8,128)(2,1)}) custom-call(bf16[2,8,128,1152]{3,2,1,0:T(8,128)(2,1)} %bitcast.67, bf16[3,1152,3072]{2,1,0:T(8,128)(2,1)} %bitcast.50, f32[2,128,3072]{2,1,0:T(8,128)} %bitcast.60, f32[2,128,3072]{2,1,0:T(8,128)} %get-tuple-element.144.refs_3_, ...), custom_call_target="tpu_custom_call" | custom-call | tf_op jit(solution)/shard_map/d_attn_0/pallas_call | solution.py:96
  1581.7 16.0 sum_rows.1
  1597.7 0.0 copy-start
  1597.7 0.0 copy-start.1
  1597.7 8.4 put_last.1
  1606.2 0.6 pad_maximum_fusion
  1606.8 1.7 copy.34
  (4 shorter events, 0.0 us)
Async XLA Ops:
  1597.7 8.5 copy-start
  1597.7 8.5 copy-start.1
  1597.7 8.5 copy-start.2

commit v5 on v4

--- a/solution.py
+++ b/solution.py
@@ -34,6 +34,7 @@
 N_FIRST, N_LN, N_RES, N_BWD2, N_BWD1 = range(5)
 QKV, UP, DACT, DCTX = range(4)
 WIDTH = (QKV_N, FF, FF, INNER)
+PER = 6
 ALL = 1 << 20
 
 
@@ -105,8 +106,8 @@
     return SimpleNamespace(**dict(zip(names[1], res)))
 
 
-def config(norm, arrays, vec, rs=None, ag=None, fills=(), bm=BM, flat_t=False, plan=(), taken=()):
-    return SimpleNamespace(norm=norm, arrays=arrays, vec=vec, rs=rs, ag=ag, fills=fills, bm=bm, flat_t=flat_t, plan=plan, taken=dict(taken))
+def config(norm, arrays, vec, rs=None, ag=None, fills=(), bm=BM, flat_t=False, plan=(), taken=(), layers=0):
+    return SimpleNamespace(norm=norm, arrays=arrays, vec=vec, rs=rs, ag=ag, fills=fills, bm=bm, flat_t=flat_t, plan=plan, taken=dict(taken), layers=layers)
 
 
 def declare(c):
@@ -180,15 +181,25 @@
     if c.fills:
         slots = TWO if c.flat_t else max(f[2] for f in c.fills)
         sc.f_at = pltpu.VMEM((slots, c.bm, TOK), BF)
-        sc.f_rhs = pltpu.VMEM((TWO, TOK, BN), BF)
+        ahead = 3 if c.flat_t or not c.ag else TWO
+        sc.f_rhs = pltpu.VMEM((ahead, TOK, BN), BF)
         sc.f_out = pltpu.VMEM((TWO, c.bm, BN), BF)
         if not c.flat_t:
             sc.f_lhs = pltpu.VMEM((TOK, c.bm), BF)
         sc.fl_sem = dma((slots,))
-        sc.fr_sem = dma((TWO,))
+        sc.fr_sem = dma((ahead,))
         sc.fo_sem = dma((TWO,))
         outs.g0 = jax.ShapeDtypeStruct(c.fills[0][:2], BF)
         outs.g1 = jax.ShapeDtypeStruct(c.fills[1][:2], BF)
+    if c.layers:
+        outs.row_o = jax.ShapeDtypeStruct((c.layers, PER, D), F32)
+        rows = -(-PER * c.layers // SUBL) * SUBL
+        for k, n in (("e", rows), ("l", SUBL)):
+            half = (n, D // TWO)
+            parts = dict(v=pltpu.VMEM((n, D), F32), a=pltpu.VMEM((n, D), F32), t=pltpu.VMEM((n, D), F32), s=pltpu.VMEM((3,) + half, F32), b=pltpu.VMEM((TWO,) + half, F32))
+            parts.update(send=dma((4,)), recv=dma((4,)))
+            for p, x in parts.items():
+                setattr(sc, k + p, x)
     return outs, sc
 
 
@@ -529,6 +540,9 @@
     if fills:
         refs = ((r.f0l, r.f0r, r.g0), (r.f1l, r.f1r, r.g1))
         jobs = [SimpleNamespace(lhs=f[0], rhs=f[1], out=f[2], blocks=c[0] // bm // c[2], tiles=c[1] // BN, sub=c[2], done=0) for f, c in zip(refs, fills)]
+        slots = r.f_rhs.shape[0]
+        for j in jobs:
+            j.fetches = j.tiles if j.tiles <= slots else j.blocks * j.tiles
 
     def lhs_copy(j, k):
         at = pl.ds(pl.multiple_of(k * bm, bm), bm)
@@ -538,7 +552,7 @@
         return Pieces(j.lhs.at[:, at], r.f_lhs, r.fl_sem.at[0], PEERS)
 
     def rhs_copy(j, v):
-        s = lax.rem(v, TWO)
+        s = lax.rem(v, slots)
         return Pieces(j.rhs.at[:, pl.ds(pl.multiple_of(lax.rem(v, j.tiles) * BN, BN), BN)], r.f_rhs.at[s], r.fr_sem.at[s], PEERS)
 
     def put_copy(j, u):
@@ -551,7 +565,8 @@
         lhs_copy(j, jnp.int32(0)).start()
         if flat_t:
             lhs_copy(j, jnp.int32(1)).start()
-        rhs_copy(j, jnp.int32(0)).start()
+        for v in range(slots - 1):
+            rhs_copy(j, jnp.int32(v)).start()
 
     def fill(n):
         while n > 0 and jobs:
@@ -561,7 +576,7 @@
 
             def unit(u, carry):
                 v, b, s = lax.div(u, j.sub), lax.rem(u, j.sub), lax.rem(u, TWO)
-                vs, t = lax.rem(v, TWO), lax.rem(v, j.tiles)
+                vs, t = lax.rem(v, slots), lax.rem(v, j.tiles)
                 k = lax.div(v, j.tiles) * j.sub + b
 
                 @pl.when(t == 0)
@@ -576,13 +591,13 @@
                     def _():
                         lhs_copy(j, k + 1).start()
 
-                @pl.when(b == 0)
+                @pl.when((b == 0) & (v < j.fetches))
                 def _():
                     rhs_copy(j, v).wait()
 
-                    @pl.when(v + 1 < rhs_all)
+                    @pl.when(v + (slots - 1) < j.fetches)
                     def _():
-                        rhs_copy(j, v + 1).start()
+                        rhs_copy(j, v + (slots - 1)).start()
 
                 @pl.when(u >= TWO)
                 def _():
@@ -670,31 +685,35 @@
     return SimpleNamespace(**locals())
 
 
-SHARED = ("own", "snd", "drx", "hx", "hy", "rx", "ry", "nin", "nout", "g", "agin", "last")
+SHARED = ("own", "snd", "drx", "hx", "hy", "rx", "ry", "nin", "nout", "agin")
 
 
 def fused(name, cid, kind, *stages):
     ins, outs, scratch, small, views = SimpleNamespace(), SimpleNamespace(), SimpleNamespace(), [], []
+    shared = SHARED + (("res_st", "slope_st") if kind == TOP else ("g", "last"))
     for i, c in enumerate(stages):
         c.first = i == 0
         c_outs, c_sc = declare(c)
         view = {}
         for group, names in ((ins, c.arrays), (outs, vars(c_outs)), (scratch, vars(c_sc))):
             for n, x in names.items():
-                view[n] = f"{n}{0 if group is scratch and n in SHARED else i}"
+                view[n] = f"{n}{0 if group is scratch and n in shared else i}"
                 setattr(group, view[n], x)
-                if group is not scratch and n in ("vec", "b_up", "vo", "bup"):
+                if group is not scratch and (n in ("vec", "b_up", "vo", "bup") or n.startswith("row_")):
                     small.append(view[n])
         view.update({n: f"{prev}{i - 1}" for n, prev in c.taken.items()})
         views.append(view)
-    if len(stages) > 1:
+    if kind == TOP:
+        del scratch.w21
+        views[1]["w2"] = views[1]["w1"]
+    elif len(stages) > 1:
         del scratch.w10
         views[0]["w1"] = views[1]["w2"]
 
     def body(refs):
         refs = vars(refs)
         st = [stage(c, SimpleNamespace(**{n: refs[x] for n, x in v.items()})) for c, v in zip(stages, views)]
-        if len(st) > 1:
+        if kind == MID and len(st) > 1:
             st[0].r.w1 = st[0].r.w1.at[pl.ds(0, stages[0].rs[1])]
         say_here(peers())
         PROGRAMS[kind](*st)
@@ -756,17 +775,77 @@
     s.end()
 
 
+def sum_steps(v, a, t, s, b, send, recv):
+    core, px, py = peers()
+    half = D // TWO
+    mine = pl.ds(pl.multiple_of(lax.rem(lax.axis_index(TP), TWO) * half, half), half)
+    copies = []
+
+    def go(src, dst, i, dev):
+        x = remote(src, dst, send.at[i], recv.at[i], dev)
+        x.start()
+        copies.append(x)
+
+    def one():
+        go(v, a, 0, core)
+
+    def two():
+        copies.pop().wait()
+        s[0] = v[:, mine] + a[:, mine]
+        go(s.at[0], b.at[0], 1, px)
+
+    def three():
+        copies.pop().wait()
+        s[1] = s[0] + b[0]
+        go(s.at[1], b.at[1], TWO, py)
+
+    def four():
+        copies.pop().wait()
+        s[TWO] = s[1] + b[1]
+        t[:, mine] = s[TWO]
+        go(s.at[TWO], t.at[:, mine], 3, core)
+
+    def five():
+        copies.pop().wait()
+
+    return one, two, three, four, five
+
+
 def last_program(s):
+    r = s.r
     s.prologue()
     loads = s.norm_load(A)
     s.clear()
-    both_halves(s, loads)
+    layers = range(s.c.layers)
+    r.ev[...] = jnp.zeros(r.ev.shape, F32)
+    for l in layers:
+        at = PER * l
+        if l:
+            r.ev[at : at + TWO, :] = getattr(r, f"row_a{l}")[:TWO, :]
+        r.ev[at + TWO : at + PER, :] = getattr(r, f"row_b{l}")[: PER - TWO, :]
+    early = sum_steps(r.ev, r.ea, r.et, r.es, r.eb, r.esend, r.erecv)
+    late = sum_steps(r.lv, r.la, r.lt, r.ls, r.lb, r.lsend, r.lrecv)
+    for i in range(len(PAIRS)):
+        s.step(i)
+        early[i]()
+    s.merge(A, OWN)
+    s.third_sends(A)
+    second_half(s, loads)
+    early[-1]()
     loads = s.norm_load(B)
     s.fill_next()
     s.third_sends(B)
     s.fill(ALL)
     s.rs_done(B)
     s.norm_half(B, loads)
+    r.lv[...] = jnp.zeros(r.lv.shape, F32)
+    for j in range(TWO):
+        r.lv[pl.ds(j, 1), :] = jnp.sum(r.acc[j], axis=0, keepdims=True)
+    for x in late:
+        x()
+    for l in layers:
+        r.row_o[l] = r.et[PER * l : PER * (l + 1), :]
+    r.row_o[0, :TWO, :] = r.lt[:TWO, :]
     s.end()
 
 
@@ -855,61 +934,85 @@
     to_end(z)
 
 
-def top_program(s):
+def top_program(s, z):
     s.prologue()
     loads = s.norm_load(A)
-    srcs = [s.begin(s.r.src.at[h], s.r.g.at[h], s.r.g_sem.at[h]) for h in HALVES]
-    s.clear()
+    z.clear()
+    both_halves(s, loads)
+    srcs = []
+
+    def next_loads():
+        z.w1_load()
+        srcs.extend(z.begin(z.r.src.at[h], z.r.g.at[h], z.r.g_sem.at[h]) for h in HALVES)
+
+    to_forward(s, next_loads)
     for x in srcs:
         x.wait()
-    s.await_once()
-    s.own_sends(A)
-    for i in range(len(PAIRS)):
-        s.step(i, False)
-        if i == TWO:
-            s.forward(A)
-            s.own_sends(B)
-    s.merge(A, OWN)
-    s.product(A, OWN)
-    s.ready(B, OWN)
-    s.cross(A)
-    s.product(B, OWN)
-    s.ready(A, XN)
-    s.ready(A, YN)
-    s.product(A, XN)
-    s.product(A, YN)
-    s.forward(B)
-    s.cross_far(A)
-    for n in range(s.tiles1):
-        s.far_sends(n)
-    s.first_sends(A, XN)
-    s.first_sends(A, YN)
-    s.product_in(4)
-    s.product(A, FAR)
+    z.own_sends(A)
+    s.res_done()
+    s.rows_out()
+    s.rs_sent()
+    z.lhs_load(0)
+    z.lhs_load(1)
+    loads = z.norm_load(A)
+    z.step(0, False)
+    z.step(1, False)
     s.cross(B)
-    s.step(5, False)
+    z.step(TWO, False)
+    z.step(3, False)
     s.ready(B, XN)
     s.ready(B, YN)
+    z.merge(A, OWN)
+    s.cross_far(B)
     s.product(B, XN)
-    s.cross_far(B)
     s.product(B, YN)
-    s.third_sends(A)
-    s.first_sends(B, FAR)
-    s.merge(B, XN)
-    s.first_sends(B, XN)
-    s.product_in(6)
-    s.merge(B, YN)
-    s.first_sends(B, YN)
-    s.product_in(7)
-    s.merge(B, OWN)
-    s.rs_done(A)
-    s.norm_half(A, loads)
-    loads = s.norm_load(B)
+    s.flip_all()
+    z.forward(A)
     s.product(B, FAR)
-    s.third_sends(B)
-    s.rs_done(B)
-    s.norm_half(B, loads)
+    s.flip_all()
     s.end()
+    z.own_sends(B)
+    z.lhs_late()
+    z.product(A, OWN)
+    z.ready(B, OWN)
+    z.cross(A)
+    z.product(B, OWN)
+    z.ready(A, XN)
+    z.ready(A, YN)
+    z.product(A, XN)
+    z.product(A, YN)
+    z.forward(B)
+    z.cross_far(A)
+    for n in range(z.tiles1):
+        z.far_sends(n)
+    z.first_sends(A, XN)
+    z.first_sends(A, YN)
+    z.product_in(4)
+    z.product(A, FAR)
+    z.cross(B)
+    z.step(5, False)
+    z.ready(B, XN)
+    z.ready(B, YN)
+    z.product(B, XN)
+    z.cross_far(B)
+    z.product(B, YN)
+    z.third_sends(A)
+    z.first_sends(B, FAR)
+    z.merge(B, XN)
+    z.first_sends(B, XN)
+    z.product_in(6)
+    z.merge(B, YN)
+    z.first_sends(B, YN)
+    z.product_in(7)
+    z.merge(B, OWN)
+    z.rs_done(A)
+    z.norm_half(A, loads)
+    loads = z.norm_load(B)
+    z.product(B, FAR)
+    z.third_sends(B)
+    z.rs_done(B)
+    z.norm_half(B, loads)
+    z.end()
 
 
 PROGRAMS = (first_program, mid_program, top_program, last_program)
@@ -1100,54 +1203,6 @@
         stacks[k] = a
 
 
-def sum_rows(parts, cid):
-    n, half = len(parts), D // TWO
-    per = 6
-    rows = -(-per * n // SUBL) * SUBL
-    ins = SimpleNamespace()
-    for l, (a, b) in enumerate(parts):
-        setattr(ins, f"a{l}", a)
-        setattr(ins, f"b{l}", b)
-
-    def body(r):
-        core, px, py = peers()
-        say_here((core, px, py))
-        odd = lax.rem(lax.axis_index(TP), TWO)
-        mine = pl.ds(pl.multiple_of(odd * half, half), half)
-        for l in range(n):
-            at = per * l
-            r.v[at : at + TWO, :] = getattr(r, f"a{l}")[:TWO, :]
-            r.v[at + TWO : at + per, :] = getattr(r, f"b{l}")[: per - TWO, :]
-        if rows > per * n:
-            r.v[per * n :, :] = jnp.zeros((rows - per * n, D), F32)
-        await_peers()
-
-        def send(src, dst, i, dev):
-            c = remote(src, dst, r.send.at[i], r.recv.at[i], dev)
-            c.start()
-            return c
-
-        send(r.v, r.a, 0, core).wait()
-        r.s[0] = r.v[:, mine] + r.a[:, mine]
-        for i, dev in enumerate((px, py)):
-            send(r.s.at[i], r.b.at[i], 1 + i, dev).wait()
-            r.s[i + 1] = r.s[i] + r.b[i]
-        c = send(r.s.at[TWO], r.t.at[:, mine], 3, core)
-        r.u[:, mine] = r.s[TWO]
-        c.wait()
-        first = lax.broadcasted_iota(jnp.int32, (1, D), 1) < half
-        keep = first == (odd == 0)
-        for l in range(n):
-            at = slice(per * l, per * (l + 1))
-            r.o[l] = jnp.where(keep, r.u[at, :], r.t[at, :])
-
-    dma = pltpu.SemaphoreType.DMA
-    whole, part = pltpu.VMEM((rows, D), F32), (rows, half)
-    scratch = SimpleNamespace(v=whole, a=whole, t=whole, u=whole, s=pltpu.VMEM((3,) + part, F32), b=pltpu.VMEM((TWO,) + part, F32), send=dma((4,)), recv=dma((4,)))
-    outs = SimpleNamespace(o=jax.ShapeDtypeStruct((n, per, D), F32))
-    return call("sum_rows", cid, body, ins, outs, scratch, list(vars(ins)) + ["o"]).o
-
-
 def group_body(x_loc, dy_loc, len_loc, wqkv, wout, wup, bup, wdown, vec):
     n = wqkv.shape[0]
     ids = iter(range(ROWS))
@@ -1174,22 +1229,24 @@
         s.ctx = attn_fwd(info, s.qkv, SEQS)
         arrays = dict(lhs1=s.ctx, wa=wo, wb=wup, in0=s.x, vec=vec, b_up=bup)
         stages = [config(N_LN, arrays, row(l, ln2, (l, bias1)), rs=(l, INNER, False), ag=(UP, l))]
+        kind, taken = MID, (("lhs1", "res"), ("in0", "out0"))
+        arrays = dict(wa=wdown, vec=vec)
         if l + 1 < n:
-            taken = (("lhs1", "res"), ("in0", "out0"))
-            arrays = dict(wa=wdown, wb=wq, vec=vec)
+            arrays.update(wb=wq)
             stages.append(config(N_LN, arrays, row(l + 1, 0, (l, bias2)), rs=(l, FF, False), ag=(QKV, l + 1), taken=taken))
-        r, *more = fused(f"fwd_{l}", next(ids), MID, *stages)
+        else:
+            kind = TOP
+            arrays.update(src=dy)
+            stages.append(config(N_RES, arrays, row(0, 0, (l, bias2)), rs=(l, FF, False), ag=(DACT, l), taken=taken + (("slope", "slope"),)))
+        r, z = fused(f"fwd_{l}", next(ids), kind, *stages)
         s.hid, s.act, s.slope, s.m_t, s.act_t = r.out0, r.res, r.slope, r.full_t, r.res_t
-        for r in more:
+        if l + 1 < n:
             s = saved[l + 1]
-            s.x, s.a, s.qkv = r.out0, r.full, r.res
-    s = saved[n - 1]
-    arrays = dict(lhs1=s.act, wa=wdown, wb=wdown, in0=s.hid, vec=vec, src=dy, slope=s.slope)
-    (r,) = fused("top", next(ids), TOP, config(N_RES, arrays, row(0, 0, (n - 1, bias2)), rs=(n - 1, FF, False), ag=(DACT, n - 1)))
-    y, d_cur, d_full, d_pre = r.out0, r.out1, r.full, r.res
-    g_bup, rows, puts, stacks = [r.bup], [], [(y.reshape(KT, D), 4, 0, 1)], [None] * 6
-    mlp_plans = ((3, 1, 0, 4, 1, 0, 2, 0, 2, 2, 3, 0, 2), (3, 1, 0, 6, 1, 0, 2, 0, 2, 2, 3, 0, 2), (3, 1, 0, 5, 1, 0, 2, 0, 2, 2, 2, 0, 1))
-    attn_plans = ((2, 2), (2, 1, 0, 4, 1, 0, 1, 1, 1, 1, 4, 1, 2), (4, 2, 0, 6, 2, 0, 1, 1, 1, 1, 2, 1, 1))
+            s.x, s.a, s.qkv = z.out0, z.full, z.res
+    y, d_cur, d_full, d_pre = z.out0, z.out1, z.full, z.res
+    g_bup, rows, puts, stacks = [z.bup], [], [(y.reshape(KT, D), 4, 0, 1)], [None] * 6
+    mlp_plans = ((3, 1, 0, 6, 1, 0, 2, 0, 2, 2, 3, 0, 2), (3, 1, 0, 5, 1, 0, 2, 0, 2, 2, 3, 0, 2), (3, 1, 0, 5, 1, 0, 2, 0, 2, 2, 3, 0, 2))
+    attn_plans = ((8, 5), (4, 2, 0, 6, 2, 0, 1, 1, 1, 1, 2, 1, 1), (3, 2, 0, 7, 2, 0, 1, 1, 1, 1, 3, 1, 1))
     for l in reversed(range(n)):
         s = saved[l]
         arrays = dict(lhs1=d_pre, wa=wup, wb=wo, in0=s.hid, in1=d_cur, vec=vec, f0l=s.act_t, f0r=flat(d_full), f1l=s.m_t, f1r=flat(d_pre))
@@ -1203,6 +1260,9 @@
         if l:
             arrays.update(wb=wdown, slope=saved[l - 1].slope)
             common.update(ag=(DACT, l - 1))
+        else:
+            arrays.update({f"row_a{i}": rows[n - 1 - i][0] for i in range(1, n)}, row_b0=v3, **{f"row_b{i}": rows[n - 1 - i][1] for i in range(1, n)})
+            common.update(layers=n)
         (r,) = fused(f"d_attn_{l}", next(ids), MID if l else LAST, config(N_BWD1, arrays, row(l, 0), **common))
         if l:
             g_bup.append(r.bup)
@@ -1211,10 +1271,9 @@
         rows.append((r.vo, v3))
         d_cur = r.out0
     put_last(puts + [(d_cur.reshape(KT, D), 5, 0, 1)], stacks)
-    g_vec = sum_rows(rows[::-1], next(ids))
     g_qkv = jnp.transpose(stacks[0].reshape(n, 3, HEADS, HD, D), (0, 4, 1, 2, 3))
     g_out = stacks[1].reshape(n, HEADS, HD, D)
-    return stacks[4].reshape(shape), stacks[5].reshape(shape), g_qkv, g_out, stacks[2], jnp.concatenate(g_bup[::-1]), stacks[3], g_vec
+    return stacks[4].reshape(shape), stacks[5].reshape(shape), g_qkv, g_out, stacks[2], jnp.concatenate(g_bup[::-1]), stacks[3], r.row_o
 
 
 def solution(mesh):

time: 1620 us -> 1590 us (0.981)
  Pallas kernels: 1600 us -> 1570 us
    pallas_call x12 -> x10, Pallas kernels: 1500 us -> 1460 us  [call(): pl.pallas_call(kernel, name=name, out_shape=list(vars(outs).values()), in...]
where the time goes in v5:
time: 1590 us; the launch traced here: 1570 us
  Pallas kernels  1570 us (99%)
    pallas_call x10, Pallas kernels, call(): pl.pallas_call(kernel, name=name, out_shape=list(vars(outs).values()), in...  1460 us
    pallas_call x3, Pallas kernels, attn_bwd(): pl.pallas_call(kernel, name='attn_bwd', out_shape=[seq_shape(QKV_N)] + sh...  66.2 us

profile of v5, /device:TPU:0, one launch (start us, length us, event | category | flops | bytes accessed | tf_op | source)
XLA Modules:
  0.0 1574.6 jit_solution(17452784382640593935)
XLA Ops:
  0.6 1.2 pad_add_fusion.info
  1.9 69.2 %first.1 = (bf16[2,8,128,3072]{3,2,1,0:T(8,128)(2,1)}, bf16[2,8,128,1152]{3,2,1,0:T(8,128)(2,1)}) custom-call(f32[2,128,3072]{2,1,0:T(8,128)} %bitcast.58, bf16[3,1152,3072]{2,1,0:T(8,128)(2,1)} %bitcast.45, f32[3,6,3072]{2,1,0:T(8,128)} %refs_4_.11), custom_call_target="tpu_custom_call" | custom-call | tf_op jit(solution)/shard_map/first/pallas_call | solution.py:97
  71.1 10.0 attn_fwd.3
  81.1 228.5 %fwd_0.1 = (f32[2,128,3072]{2,1,0:T(8,128)}, bf16[2,8,128,3072]{3,2,1,0:T(8,128)(2,1)}, bf16[2,8,128,1536]{3,2,1,0:T(8,128)(2,1)}, f32[2,8,128,1536]{3,2,1,0:T(8...) custom-call(bf16[2,8,128,384]{3,2,1,0:T(8,128)(2,1)} %bitcast.77, ...), custom_call_target="tpu_custom_call" | custom-call | tf_op jit(solution)/shard_map/fwd_0/pallas_call | solution.py:97
  309.6 10.1 attn_fwd.4
  319.7 228.0 %fwd_1.1 = (f32[2,128,3072]{2,1,0:T(8,128)}, bf16[2,8,128,3072]{3,2,1,0:T(8,128)(2,1)}, bf16[2,8,128,1536]{3,2,1,0:T(8,128)(2,1)}, f32[2,8,128,1536]{3,2,1,0:T(8...) custom-call(bf16[2,8,128,384]{3,2,1,0:T(8,128)(2,1)} %bitcast.79, ...), custom_call_target="tpu_custom_call" | custom-call | tf_op jit(solution)/shard_map/fwd_1/pallas_call | solution.py:97
  547.8 10.1 attn_fwd.5
  557.8 221.5 %fwd_2.1 = (f32[2,128,3072]{2,1,0:T(8,128)}, bf16[2,8,128,3072]{3,2,1,0:T(8,128)(2,1)}, bf16[2,8,128,1536]{3,2,1,0:T(8,128)(2,1)}, f32[2,8,128,1536]{3,2,1,0:T(8...) custom-call(bf16[2,8,128,384]{3,2,1,0:T(8,128)(2,1)} %bitcast.81, ...), custom_call_target="tpu_custom_call" | custom-call | tf_op jit(solution)/shard_map/fwd_2/pallas_call | solution.py:97
  779.3 125.4 %d_mlp_2.1 = (f32[2,128,3072]{2,1,0:T(8,128)}, f32[8,3072]{1,0:T(8,128)}, bf16[2,8,128,3072]{3,2,1,0:T(8,128)(2,1)}, bf16[2,8,128,384]{3,2,1,0:T(8,128)(2,1)}, b...) custom-call(bf16[2,8,128,1536]{3,2,1,0:T(8,128)(2,1)} %get-tuple-element.90.refs_0_, ...), custom_call_target="tpu_custom_call" | custom-call | tf_op jit(solution)/shard_map/d_mlp_2/pallas_call | solution.py:97
  904.8 19.6 %attn_bwd.3 = (bf16[2,8,8,16,1152]{4,3,2,1,0:T(8,128)(2,1)}, bf16[3,3072,1536]{2,1,0:T(8,128)(2,1)}, bf16[3,1536,3072]{2,1,0:T(8,128)(2,1)}, f32[1,256,3072]{2,1,0:T(8,128)}) custom-call(s32[17]{0:T(128)} %pad_add_fusion.info, bf16[2,8,8,16,1152]{4,3,2,1,0:T(8,128)(2,1)} %bitcast.74, bf16[2,8,8,16,384]{4,3,2,1,0:T(8,128)(2,1)} %bitcast.97, ...), custom_call_target="tpu_custom_call" | custom-call | tf_op jit(solution)/shard_map/attn_bwd/pallas_call | solution.py:1162
  924.4 125.3 %d_attn_2.1 = (f32[2,128,3072]{2,1,0:T(8,128)}, f32[8,3072]{1,0:T(8,128)}, bf16[2,8,128,3072]{3,2,1,0:T(8,128)(2,1)}, bf16[2,8,128,1536]{3,2,1,0:T(8,128)(2,1)},...) custom-call(bf16[2,8,128,1152]{3,2,1,0:T(8,128)(2,1)} %bitcast.67, ...), custom_call_target="tpu_custom_call" | custom-call | tf_op jit(solution)/shard_map/d_attn_2/pallas_call | solution.py:97
  1049.7 125.5 %d_mlp_1.1 = (f32[2,128,3072]{2,1,0:T(8,128)}, f32[8,3072]{1,0:T(8,128)}, bf16[2,8,128,3072]{3,2,1,0:T(8,128)(2,1)}, bf16[2,8,128,384]{3,2,1,0:T(8,128)(2,1)}, b...) custom-call(bf16[2,8,128,1536]{3,2,1,0:T(8,128)(2,1)} %get-tuple-element.106.refs_0_, ...), custom_call_target="tpu_custom_call" | custom-call | tf_op jit(solution)/shard_map/d_mlp_1/pallas_call | solution.py:97
  1175.1 23.3 %attn_bwd.4 = (bf16[2,8,8,16,1152]{4,3,2,1,0:T(8,128)(2,1)}, bf16[3,1152,3072]{2,1,0:T(8,128)(2,1)}, bf16[3,384,3072]{2,1,0:T(8,128)(2,1)}, bf16[3,3072,1536]{2,1,0:T(8,128)(2,1)}, bf16[3,1536,3072]{2,1,0:T(8,128)(2,1)}) custom-call(s32[17]{0:T(128)} %pad_add_fusion.info, ...), custom_call_target="tpu_custom_call", output_to_operand_aliasing={{3}: (7, {}), {4}: (8, {})} | custom-call | tf_op jit(solution)/shard_map/attn_bwd/pallas_call | solution.py:1162
  1198.5 127.4 %d_attn_1.1 = (f32[2,128,3072]{2,1,0:T(8,128)}, f32[8,3072]{1,0:T(8,128)}, bf16[2,8,128,3072]{3,2,1,0:T(8,128)(2,1)}, bf16[2,8,128,1536]{3,2,1,0:T(8,128)(2,1)},...) custom-call(bf16[2,8,128,1152]{3,2,1,0:T(8,128)(2,1)} %bitcast.65, ...), custom_call_target="tpu_custom_call" | custom-call | tf_op jit(solution)/shard_map/d_attn_1/pallas_call | solution.py:97
  1325.9 124.0 %d_mlp_0.1 = (f32[2,128,3072]{2,1,0:T(8,128)}, f32[8,3072]{1,0:T(8,128)}, bf16[2,8,128,3072]{3,2,1,0:T(8,128)(2,1)}, bf16[2,8,128,384]{3,2,1,0:T(8,128)(2,1)}, b...) custom-call(bf16[2,8,128,1536]{3,2,1,0:T(8,128)(2,1)} %get-tuple-element.124.refs_0_, ...), custom_call_target="tpu_custom_call" | custom-call | tf_op jit(solution)/shard_map/d_mlp_0/pallas_call | solution.py:97
  1449.9 23.3 %attn_bwd.5 = (bf16[2,8,8,16,1152]{4,3,2,1,0:T(8,128)(2,1)}, bf16[3,1152,3072]{2,1,0:T(8,128)(2,1)}, bf16[3,384,3072]{2,1,0:T(8,128)(2,1)}, bf16[3,3072,1536]{2,1,0:T(8,128)(2,1)}, bf16[3,1536,3072]{2,1,0:T(8,128)(2,1)}) custom-call(s32[17]{0:T(128)} %pad_add_fusion.info, ...), custom_call_target="tpu_custom_call", output_to_operand_aliasing={{1}: (7, {}), {2}: (8, {}), {3}: (9, {}), {4}: (10, {})} | custom-call | tf_op jit(solution)/shard_map/attn_bwd/pallas_call | solution.py:1162
  1473.2 90.1 %d_attn_0.1 = (f32[2,128,3072]{2,1,0:T(8,128)}, f32[8,3072]{1,0:T(8,128)}, bf16[384,3072]{1,0:T(8,128)(2,1)}, bf16[1152,3072]{1,0:T(8,128)(2,1)}, f32[3,6,3072]{2,1,0:T(8,128)}) custom-call(bf16[2,8,128,1152]{3,2,1,0:T(8,128)(2,1)} %bitcast.75, bf16[3,1152,3072]{2,1,0:T(8,128)(2,1)} %bitcast.50, f32[2,128,3072]{2,1,0:T(8,128)} %bitcast.60, ...), custom_call_target="tpu_custom_call" | custom-call | tf_op jit(solution)/shard_map/d_attn_0/pallas_call | solution.py:97
  1563.3 0.0 copy-start
  1563.4 0.0 copy-start.1
  1563.4 0.0 copy-start.2
  1563.4 8.4 put_last.1
  1571.8 0.0 copy-done
  1571.9 0.6 pad_maximum_fusion
  1572.5 1.7 copy.34
  (2 shorter events, 0.0 us)
Async XLA Ops:
  1563.3 8.5 copy-start
  1563.4 8.5 copy-start.1
  1563.4 8.5 copy-start.2

commit v6 on v5

--- a/solution.py
+++ b/solution.py
@@ -189,8 +189,8 @@
         sc.fl_sem = dma((slots,))
         sc.fr_sem = dma((ahead,))
         sc.fo_sem = dma((TWO,))
-        outs.g0 = jax.ShapeDtypeStruct(c.fills[0][:2], BF)
-        outs.g1 = jax.ShapeDtypeStruct(c.fills[1][:2], BF)
+        for i, f in enumerate(c.fills):
+            setattr(outs, f"g{i}", jax.ShapeDtypeStruct(f[:TWO], BF))
     if c.layers:
         outs.row_o = jax.ShapeDtypeStruct((c.layers, PER, D), F32)
         rows = -(-PER * c.layers // SUBL) * SUBL
@@ -538,7 +538,7 @@
 
     jobs = []
     if fills:
-        refs = ((r.f0l, r.f0r, r.g0), (r.f1l, r.f1r, r.g1))
+        refs = [[getattr(r, k) for k in (f"f{i}l", f"f{i}r", f"g{i}")] for i in range(len(fills))]
         jobs = [SimpleNamespace(lhs=f[0], rhs=f[1], out=f[2], blocks=c[0] // bm // c[2], tiles=c[1] // BN, sub=c[2], done=0) for f, c in zip(refs, fills)]
         slots = r.f_rhs.shape[0]
         for j in jobs:
@@ -1172,35 +1172,66 @@
     return res[0].reshape(TWO, PEERS, ROWS, QKV_N)
 
 
-def put_last(puts, stacks):
+def put_last(puts, stacks, lhs, rhs, k, layer):
     used, shapes, given, scratch = stacking(puts, stacks)
-    m = len(puts)
+    m, n, wide = len(puts), lhs.shape[-1], rhs.shape[-1]
+    skip = m + TWO + len(given)
+    tiles, ahead = wide // BN, 3
 
     def kernel(*refs):
-        grads, refs = refs[:m], refs[m + len(given) :]
-        outs, refs = refs[: len(used)], refs[len(used) :]
-        bounce, load_sem, put_sem = refs[:m], refs[m], refs[m + 1]
+        grads, lhs_ref, rhs_ref, refs = refs[:m], refs[m], refs[m + 1], refs[skip + 1 :]
+        outs, goal, refs = refs[: len(used)], refs[len(used)], refs[len(used) + 1 :]
+        bounce, load_sem, put_sem, refs = refs[:m], refs[m], refs[m + 1], refs[m + TWO :]
+        f_lhs, f_at, f_rhs, f_out, l_sem, r_sem, o_sem = refs
+
+        def right(t):
+            return Pieces(rhs_ref.at[:, pl.ds(t * BN, BN)], f_rhs.at[t % ahead], r_sem.at[t % ahead], PEERS)
+
+        def store(t):
+            return Pieces(f_out.at[t % TWO], goal.at[layer, :, pl.ds(t * BN, BN)], o_sem.at[t % TWO], ahead)
+
+        left = Pieces(lhs_ref, f_lhs, l_sem, PEERS).start()
+        for t in range(ahead - 1):
+            right(t).start()
         loads = [Pieces(grads[i], bounce[i], load_sem.at[i], PEERS).start() for i in range(m)]
         stores = []
-        for i, p in enumerate(puts):
-            loads[i].wait()
-            stores.append(Pieces(bounce[i], outs[used.index(p[1])].at[p[TWO]], put_sem.at[i], PEERS).start())
+        left.wait()
+        for i in range(TOK // KT):
+            f_at[:, i * KT : (i + 1) * KT] = f_lhs[i * KT : (i + 1) * KT, :].T
+        for t in range(tiles):
+            right(t).wait()
+            if t + ahead - 1 < tiles:
+                right(t + ahead - 1).start()
+            if t >= TWO:
+                store(t - TWO).wait()
+            f_out[t % TWO] = dims(f_at[...], f_rhs[t % ahead], 1, 0).astype(BF)
+            store(t).start()
+            if t < m:
+                loads[t].wait()
+                stores.append(Pieces(bounce[t], outs[used.index(puts[t][1])].at[puts[t][TWO]], put_sem.at[t], PEERS).start())
+        for t in range(tiles - TWO, tiles):
+            store(t).wait()
         for c in stores:
             c.wait()
 
     hbm = pl.BlockSpec(memory_space=ANY)
-    res = pl.pallas_call(
+    dma = pltpu.SemaphoreType.DMA
+    old = stacks[k]
+    aliases = {m + TWO + j: used.index(g) for j, g in enumerate(given)}
+    *res, stacks[k] = pl.pallas_call(
         kernel,
         name="put_last",
-        out_shape=shapes,
-        in_specs=[hbm] * (m + len(given)),
-        out_specs=[hbm] * len(used),
-        scratch_shapes=scratch,
-        input_output_aliases={m + j: used.index(k) for j, k in enumerate(given)},
+        out_shape=shapes + [jax.ShapeDtypeStruct(old.shape, old.dtype)],
+        in_specs=[hbm] * (skip + 1),
+        out_specs=[hbm] * (len(used) + 1),
+        scratch_shapes=scratch
+        + [pltpu.VMEM(x, BF) for x in ((TOK, n), (n, TOK), (ahead, TOK, BN), (TWO, n, BN))]
+        + [dma, dma((ahead,)), dma((TWO,))],
+        input_output_aliases={**aliases, skip: len(used)},
         compiler_params=pltpu.CompilerParams(vmem_limit_bytes=VMEM_LIMIT),
-    )(*[p[0] for p in puts], *[stacks[k] for k in given])
-    for k, a in zip(used, res):
-        stacks[k] = a
+    )(*[p[0] for p in puts], lhs, rhs, *[stacks[g] for g in given], old)
+    for g, a in zip(used, res):
+        stacks[g] = a
 
 
 def group_body(x_loc, dy_loc, len_loc, wqkv, wout, wup, bup, wdown, vec):
@@ -1245,19 +1276,21 @@
             s.x, s.a, s.qkv = z.out0, z.full, z.res
     y, d_cur, d_full, d_pre = z.out0, z.out1, z.full, z.res
     g_bup, rows, puts, stacks = [z.bup], [], [(y.reshape(KT, D), 4, 0, 1)], [None] * 6
-    mlp_plans = ((3, 1, 0, 6, 1, 0, 2, 0, 2, 2, 3, 0, 2), (3, 1, 0, 5, 1, 0, 2, 0, 2, 2, 3, 0, 2), (3, 1, 0, 5, 1, 0, 2, 0, 2, 2, 3, 0, 2))
-    attn_plans = ((8, 5), (4, 2, 0, 6, 2, 0, 1, 1, 1, 1, 2, 1, 1), (3, 2, 0, 7, 2, 0, 1, 1, 1, 1, 3, 1, 1))
+    mlp_plan = (3, 1, 0, 7, 1, 0, TWO, 0, TWO, TWO, 3, 0, TWO)
+    attn_plan = (3, TWO, 0, 7, TWO, 0, 1, 1, 1, 1, 3, 1, 1)
     for l in reversed(range(n)):
         s = saved[l]
         arrays = dict(lhs1=d_pre, wa=wup, wb=wo, in0=s.hid, in1=d_cur, vec=vec, f0l=s.act_t, f0r=flat(d_full), f1l=s.m_t, f1r=flat(d_pre))
-        common = dict(fills=((FF, D, TWO), (D, FF, 1)), bm=BM + BM, flat_t=True, plan=mlp_plans[l])
+        common = dict(fills=((FF, D, TWO), (D, FF, 1)), bm=BM + BM, flat_t=True, plan=mlp_plan)
         (r,) = fused(f"d_mlp_{l}", next(ids), MID, config(N_BWD2, arrays, row(l, ln2), rs=(l, FF, True), ag=(DCTX, l), **common))
         d_hid, d_attn, v3 = r.out0, r.full, r.vo
         puts += [(r.g0, 3, l, n), (r.g1, TWO, l, n)]
         d_qkv = attn_bwd(info, s.qkv, r.res, puts, stacks, TWO if l else 1)
-        arrays = dict(lhs1=d_qkv, wa=wq, in0=s.x, in1=d_hid, vec=vec, f0l=flat(s.ctx), f0r=flat(d_attn), f1l=flat(d_qkv), f1r=flat(s.a))
-        common = dict(rs=(l, QKV_N, False), fills=((INNER, D, 1), (QKV_N, D, 3)), plan=attn_plans[l])
+        arrays = dict(lhs1=d_qkv, wa=wq, in0=s.x, in1=d_hid, vec=vec, f0l=flat(d_qkv), f0r=flat(s.a))
+        fills = ((QKV_N, D, 3), (INNER, D, 1))
+        common = dict(rs=(l, QKV_N, False), fills=fills if l else fills[:1], plan=attn_plan if l else (6, 4))
         if l:
+            arrays.update(f1l=flat(s.ctx), f1r=flat(d_attn))
             arrays.update(wb=wdown, slope=saved[l - 1].slope)
             common.update(ag=(DACT, l - 1))
         else:
@@ -1267,10 +1300,10 @@
         if l:
             g_bup.append(r.bup)
             d_full, d_pre = r.full, r.res
-        puts = [(r.g0, 1, l, n), (r.g1, 0, l, n)]
+        puts = [(r.g0, 0, l, n)] + ([(r.g1, 1, l, n)] if l else [])
         rows.append((r.vo, v3))
         d_cur = r.out0
-    put_last(puts + [(d_cur.reshape(KT, D), 5, 0, 1)], stacks)
+    put_last(puts + [(d_cur.reshape(KT, D), 5, 0, 1)], stacks, flat(s.ctx), flat(d_attn), 1, 0)
     g_qkv = jnp.transpose(stacks[0].reshape(n, 3, HEADS, HD, D), (0, 4, 1, 2, 3))
     g_out = stacks[1].reshape(n, HEADS, HD, D)
     return stacks[4].reshape(shape), stacks[5].reshape(shape), g_qkv, g_out, stacks[2], jnp.concatenate(g_bup[::-1]), stacks[3], r.row_o

time: 1590 us -> 1580 us (level)
  no operation moved by 1% of the time
where the time goes in v6:
time: 1580 us; the launch traced here: 1570 us
  Pallas kernels  1560 us (99%)
    pallas_call x10, Pallas kernels, call(): pl.pallas_call(kernel, name=name, out_shape=list(vars(outs).values()), in...  1450 us
    pallas_call x3, Pallas kernels, attn_bwd(): pl.pallas_call(kernel, name='attn_bwd', out_shape=[seq_shape(QKV_N)] + sh...  66.2 us

profile of v6, /device:TPU:0, one launch (start us, length us, event | category | flops | bytes accessed | tf_op | source)
XLA Modules:
  0.0 1568.1 jit_solution(3960560479264658661)
XLA Ops:
  0.6 1.2 pad_add_fusion.info
  1.9 69.2 %first.1 = (bf16[2,8,128,3072]{3,2,1,0:T(8,128)(2,1)}, bf16[2,8,128,1152]{3,2,1,0:T(8,128)(2,1)}) custom-call(f32[2,128,3072]{2,1,0:T(8,128)} %bitcast.58, bf16[3,1152,3072]{2,1,0:T(8,128)(2,1)} %bitcast.45, f32[3,6,3072]{2,1,0:T(8,128)} %refs_4_.11), custom_call_target="tpu_custom_call" | custom-call | tf_op jit(solution)/shard_map/first/pallas_call | solution.py:97
  71.1 10.1 attn_fwd.3
  81.2 228.5 %fwd_0.1 = (f32[2,128,3072]{2,1,0:T(8,128)}, bf16[2,8,128,3072]{3,2,1,0:T(8,128)(2,1)}, bf16[2,8,128,1536]{3,2,1,0:T(8,128)(2,1)}, f32[2,8,128,1536]{3,2,1,0:T(8...) custom-call(bf16[2,8,128,384]{3,2,1,0:T(8,128)(2,1)} %bitcast.77, ...), custom_call_target="tpu_custom_call" | custom-call | tf_op jit(solution)/shard_map/fwd_0/pallas_call | solution.py:97
  309.7 10.0 attn_fwd.4
  319.7 228.0 %fwd_1.1 = (f32[2,128,3072]{2,1,0:T(8,128)}, bf16[2,8,128,3072]{3,2,1,0:T(8,128)(2,1)}, bf16[2,8,128,1536]{3,2,1,0:T(8,128)(2,1)}, f32[2,8,128,1536]{3,2,1,0:T(8...) custom-call(bf16[2,8,128,384]{3,2,1,0:T(8,128)(2,1)} %bitcast.79, ...), custom_call_target="tpu_custom_call" | custom-call | tf_op jit(solution)/shard_map/fwd_1/pallas_call | solution.py:97
  547.8 10.1 attn_fwd.5
  557.8 221.5 %fwd_2.1 = (f32[2,128,3072]{2,1,0:T(8,128)}, bf16[2,8,128,3072]{3,2,1,0:T(8,128)(2,1)}, bf16[2,8,128,1536]{3,2,1,0:T(8,128)(2,1)}, f32[2,8,128,1536]{3,2,1,0:T(8...) custom-call(bf16[2,8,128,384]{3,2,1,0:T(8,128)(2,1)} %bitcast.81, ...), custom_call_target="tpu_custom_call" | custom-call | tf_op jit(solution)/shard_map/fwd_2/pallas_call | solution.py:97
  779.3 123.3 %d_mlp_2.1 = (f32[2,128,3072]{2,1,0:T(8,128)}, f32[8,3072]{1,0:T(8,128)}, bf16[2,8,128,3072]{3,2,1,0:T(8,128)(2,1)}, bf16[2,8,128,384]{3,2,1,0:T(8,128)(2,1)}, b...) custom-call(bf16[2,8,128,1536]{3,2,1,0:T(8,128)(2,1)} %get-tuple-element.89.refs_0_, ...), custom_call_target="tpu_custom_call" | custom-call | tf_op jit(solution)/shard_map/d_mlp_2/pallas_call | solution.py:97
  902.6 19.6 %attn_bwd.3 = (bf16[2,8,8,16,1152]{4,3,2,1,0:T(8,128)(2,1)}, bf16[3,3072,1536]{2,1,0:T(8,128)(2,1)}, bf16[3,1536,3072]{2,1,0:T(8,128)(2,1)}, f32[1,256,3072]{2,1,0:T(8,128)}) custom-call(s32[17]{0:T(128)} %pad_add_fusion.info, bf16[2,8,8,16,1152]{4,3,2,1,0:T(8,128)(2,1)} %bitcast.76, bf16[2,8,8,16,384]{4,3,2,1,0:T(8,128)(2,1)} %bitcast.97, ...), custom_call_target="tpu_custom_call" | custom-call | tf_op jit(solution)/shard_map/attn_bwd/pallas_call | solution.py:1162
  922.2 126.6 %d_attn_2.1 = (f32[2,128,3072]{2,1,0:T(8,128)}, f32[8,3072]{1,0:T(8,128)}, bf16[2,8,128,3072]{3,2,1,0:T(8,128)(2,1)}, bf16[2,8,128,1536]{3,2,1,0:T(8,128)(2,1)},...) custom-call(bf16[2,8,128,1152]{3,2,1,0:T(8,128)(2,1)} %bitcast.69, ...), custom_call_target="tpu_custom_call" | custom-call | tf_op jit(solution)/shard_map/d_attn_2/pallas_call | solution.py:97
  1048.8 123.4 %d_mlp_1.1 = (f32[2,128,3072]{2,1,0:T(8,128)}, f32[8,3072]{1,0:T(8,128)}, bf16[2,8,128,3072]{3,2,1,0:T(8,128)(2,1)}, bf16[2,8,128,384]{3,2,1,0:T(8,128)(2,1)}, b...) custom-call(bf16[2,8,128,1536]{3,2,1,0:T(8,128)(2,1)} %get-tuple-element.105.refs_0_, ...), custom_call_target="tpu_custom_call" | custom-call | tf_op jit(solution)/shard_map/d_mlp_1/pallas_call | solution.py:97
  1172.2 23.3 %attn_bwd.4 = (bf16[2,8,8,16,1152]{4,3,2,1,0:T(8,128)(2,1)}, bf16[3,1152,3072]{2,1,0:T(8,128)(2,1)}, bf16[3,384,3072]{2,1,0:T(8,128)(2,1)}, bf16[3,3072,1536]{2,1,0:T(8,128)(2,1)}, bf16[3,1536,3072]{2,1,0:T(8,128)(2,1)}) custom-call(s32[17]{0:T(128)} %pad_add_fusion.info, ...), custom_call_target="tpu_custom_call", output_to_operand_aliasing={{3}: (7, {}), {4}: (8, {})} | custom-call | tf_op jit(solution)/shard_map/attn_bwd/pallas_call | solution.py:1162
  1195.5 125.6 %d_attn_1.1 = (f32[2,128,3072]{2,1,0:T(8,128)}, f32[8,3072]{1,0:T(8,128)}, bf16[2,8,128,3072]{3,2,1,0:T(8,128)(2,1)}, bf16[2,8,128,1536]{3,2,1,0:T(8,128)(2,1)},...) custom-call(bf16[2,8,128,1152]{3,2,1,0:T(8,128)(2,1)} %bitcast.67, ...), custom_call_target="tpu_custom_call" | custom-call | tf_op jit(solution)/shard_map/d_attn_1/pallas_call | solution.py:97
  1321.1 123.7 %d_mlp_0.1 = (f32[2,128,3072]{2,1,0:T(8,128)}, f32[8,3072]{1,0:T(8,128)}, bf16[2,8,128,3072]{3,2,1,0:T(8,128)(2,1)}, bf16[2,8,128,384]{3,2,1,0:T(8,128)(2,1)}, b...) custom-call(bf16[2,8,128,1536]{3,2,1,0:T(8,128)(2,1)} %get-tuple-element.123.refs_0_, ...), custom_call_target="tpu_custom_call" | custom-call | tf_op jit(solution)/shard_map/d_mlp_0/pallas_call | solution.py:97
  1444.8 23.3 %attn_bwd.5 = (bf16[2,8,8,16,1152]{4,3,2,1,0:T(8,128)(2,1)}, bf16[3,1152,3072]{2,1,0:T(8,128)(2,1)}, bf16[3,384,3072]{2,1,0:T(8,128)(2,1)}, bf16[3,3072,1536]{2,1,0:T(8,128)(2,1)}, bf16[3,1536,3072]{2,1,0:T(8,128)(2,1)}) custom-call(s32[17]{0:T(128)} %pad_add_fusion.info, ...), custom_call_target="tpu_custom_call", output_to_operand_aliasing={{1}: (7, {}), {2}: (8, {}), {3}: (9, {}), {4}: (10, {})} | custom-call | tf_op jit(solution)/shard_map/attn_bwd/pallas_call | solution.py:1162
  1468.2 81.4 %d_attn_0.1 = (f32[2,128,3072]{2,1,0:T(8,128)}, f32[8,3072]{1,0:T(8,128)}, bf16[1152,3072]{1,0:T(8,128)(2,1)}, f32[3,6,3072]{2,1,0:T(8,128)}) custom-call(bf16[2,8,128,1152]{3,2,1,0:T(8,128)(2,1)} %bitcast.65, bf16[3,1152,3072]{2,1,0:T(8,128)(2,1)} %bitcast.50, f32[2,128,3072]{2,1,0:T(8,128)} %bitcast.60, f32[2,128,3072]{2,1,0:T(8,128)} %get-tuple-element.139.refs_3_, ...), custom_call_target="tpu_custom_call" | custom-call | tf_op jit(solution)/shard_map/d_attn_0/pallas_call | solution.py:97
  1549.6 0.0 copy-start
  1549.6 0.0 copy-start.1
  1549.6 0.0 copy-start.2
  1549.6 15.6 put_last.1
  1565.3 0.0 copy-done
  1565.3 0.6 pad_maximum_fusion
  1565.9 1.7 copy.34
  (2 shorter events, 0.0 us)
Async XLA Ops:
  1549.6 15.7 copy-start
  1549.6 15.7 copy-start.1
  1549.6 15.7 copy-start.2
